TPU v7x, 32 devices: a whole 2x2x4 slice. The times are simulated.
32 devices in a mesh: section: 2 (over core), dp: 16 (over z, y, x).
Axes of the slice: x: 2, y: 2, z: 4, core: 2. Of those that a mesh axis runs over, the one named last changes fastest.
Arguments:
- tokens: bfloat16 [2, 2048, 1536], P(None, 'dp'), may hold values from -6 to 6
- cotangent: bfloat16 [2, 2048, 1536], P(None, 'dp'), may hold values from -6 to 6
- lengths: int32 [2, 16, 4], P(None, 'dp'), may hold values from 1 to 64, 128 in all within a row
- routes: int32 [2, 2, 2048, 8], P('section', None, 'dp'), may hold values from 0 to 15, all different within a row; in each aligned block of 128 rows (0 to 127, 128 to 255, ..., all dimensions but the last counted through in order) at most 80 rows name the same one
- combined_weight: bfloat16 [2, 1536, 2560], P('section', 'dp'), may hold values from -0.15625 to 0.15625
- output_weight: bfloat16 [2, 1536, 1536], P('section', 'dp'), may hold values from -0.625 to 0.625
- router_weight: bfloat16 [2, 1536, 16], P('section', 'dp'), may hold values from -0.078125 to 0.078125
- attention_gain: bfloat16 [2, 1536], P('section', 'dp'), may hold values from 0.5 to 1.5
- mixture_gain: bfloat16 [2, 1536], P('section', 'dp'), may hold values from 0.5 to 1.5
- expert_gate_up: bfloat16 [2, 16, 1536, 1024], P('section', 'dp'), may hold values from -0.3125 to 0.3125
- expert_down: bfloat16 [2, 16, 512, 1536], P('section', 'dp'), may hold values from -0.5 to 0.5
Outputs:
- boundary: bfloat16 [2, 2, 2048, 1536], P('section', None, 'dp')
- joint_grad: float32 [2, 1536, 2560], P('section', 'dp')
- output_grad: float32 [2, 1536, 1536], P('section', 'dp')
- router_grad: float32 [2, 1536, 16], P('section', 'dp')
- attention_gain_grad: float32 [2, 1536], P('section', 'dp')
- mixture_gain_grad: float32 [2, 1536], P('section', 'dp')
- expert_gate_up_grad: float32 [2, 16, 1536, 1024], P('section', 'dp')
- expert_down_grad: float32 [2, 16, 512, 1536], P('section', 'dp')
Inputs may be any that keep to these rules, and one draw needn't show every extreme that they name: Each row of 4 lengths fills the 128 rows of one device's micro-batch, and its longest sequence has 64 rows. `routes`: each token names 8 different experts; among the rows of one device in one micro-batch and layer no expert is named more than 80 times, a bound that some block reaches.
All inputs are finite; a program needn't handle non-finite values.
Results may differ from a plain program's by a relative error of at most 0.023.
Values may be sent and summed in bfloat16 or wider, within the bound.
A program may use at most 256 MiB of HBM per device.

v0:
```python
import jax
import jax.numpy as jnp
from jax import lax
from jax.sharding import PartitionSpec as P

MODEL_WIDTH = 1536
QUERY_HEADS = 24
KEY_VALUE_HEADS = 8
HEAD_SIZE = 64
FFE = 512
TOPK = 8
DEVICE_ROWS = 128
MB = 2
NSEQ = 4


norm_epsilon = 1e-06


def passed_along(value, axis, steps):
    count = lax.axis_size(axis)
    leading, last = (max(0, -steps), min(count, count - steps))
    return lax.ppermute(value, axis, [(source, source + steps) for source in range(leading, last)])


def cut_along(x, dim, peers):
    shape = x.shape
    pieces = x.reshape(*shape[:dim], peers, shape[dim] // peers, *shape[dim + 1 :])
    return jnp.moveaxis(pieces, dim, 0)


def sum_at_owner(x, axis, dim):
    pieces = cut_along(x, dim, lax.axis_size(axis))
    arrived = lax.all_to_all(pieces, axis, split_axis=0, concat_axis=0, tiled=True)
    return arrived.astype(jnp.float32).sum(axis=0)


def in_one_piece(arrays, axis, dim, along):
    columns = [a.reshape(*a.shape[:along], -1) for a in arrays]
    both = jnp.concatenate(columns, axis=along)
    out, at, outs = (sum_at_owner(both, axis, dim), 0, [])
    for a, column in zip(arrays, columns):
        share = out[..., at : at + column.shape[along]]
        outs.append(share.reshape(*share.shape[:along], *a.shape[along:]))
        at += column.shape[along]
    return tuple(outs)


def layout(length_rows):
    seq_ends = jnp.cumsum(length_rows, axis=-1)
    seq_starts = seq_ends - length_rows
    row_ids = jnp.arange(DEVICE_ROWS, dtype=jnp.int32)
    segment = jnp.sum((row_ids[None, :, None] >= seq_ends[:, None, :]).astype(jnp.int32), axis=-1)
    member = (segment[:, :, None] == jnp.arange(NSEQ, dtype=jnp.int32)[None, None, :]).astype(
        jnp.int32
    )
    token_position = row_ids[None, :] - jnp.sum(member * seq_starts[:, None, :], axis=-1)
    return (segment[0], token_position[0])


def rotary_embedding(values, token_position, direction):
    half_width = HEAD_SIZE // 2
    frequency = 10000.0 ** (-2.0 * jnp.arange(half_width, dtype=jnp.float32) / HEAD_SIZE)
    angles = direction * token_position.astype(jnp.float32)[..., None] * frequency
    cosine = jnp.cos(angles)[..., None, :]
    sine_part = jnp.sin(angles)[..., None, :]
    former = values[..., :half_width]
    latter = values[..., half_width:]
    return jnp.concatenate(
        [former * cosine - latter * sine_part, latter * cosine + former * sine_part], axis=-1
    )


def contract_rows(left_side, right_side):
    return lax.dot_general(
        left_side, right_side, (((0,), (0,)), ((), ())), preferred_element_type=jnp.float32
    )


def contracted_columns(left_side, right_side):
    return lax.dot_general(
        left_side, right_side, (((1,), (1,)), ((), ())), preferred_element_type=jnp.float32
    )


def slot_tables(route, experts, capacity):
    chosen = route.reshape(-1)
    pick_count = chosen.shape[0]
    member = chosen[:, None] == jnp.arange(experts, dtype=jnp.int32)[None, :]
    earlier = (jnp.arange(pick_count)[:, None] > jnp.arange(pick_count)[None, :]).astype(
        jnp.bfloat16
    )
    before = jnp.dot(earlier, member.astype(jnp.bfloat16), preferred_element_type=jnp.float32)
    ranking = jnp.sum(jnp.where(member, before, 0.0), axis=-1).astype(jnp.int32)
    target = chosen * capacity + ranking
    anchor = (
        jnp.full((experts * capacity,), pick_count, jnp.int32)
        .at[target]
        .set(jnp.arange(pick_count, dtype=jnp.int32))
    )
    return (member.reshape(DEVICE_ROWS, TOPK, experts), target, anchor)


def front(hidden, length_rows, weights):
    joint, result_output, router, gain_attention, gain_mixture = weights
    query_total_width = QUERY_HEADS * HEAD_SIZE
    rotary_pair_width = KEY_VALUE_HEADS * HEAD_SIZE
    count_of_rows = hidden.shape[0]
    segment, token_position = layout(length_rows)
    inverse_one = lax.rsqrt(jnp.mean(hidden * hidden, axis=-1, keepdims=True) + norm_epsilon)
    scaled_one = hidden * inverse_one
    normed = (scaled_one * gain_attention).astype(jnp.bfloat16)
    projected_rows = jnp.dot(normed, joint, preferred_element_type=jnp.float32)
    query_matrix = rotary_embedding(
        projected_rows[:, :query_total_width].reshape(count_of_rows, QUERY_HEADS, HEAD_SIZE),
        token_position,
        1.0,
    ).astype(jnp.bfloat16)
    key_matrix = rotary_embedding(
        projected_rows[:, query_total_width : query_total_width + rotary_pair_width].reshape(
            count_of_rows, KEY_VALUE_HEADS, HEAD_SIZE
        ),
        token_position,
        1.0,
    ).astype(jnp.bfloat16)
    value_matrix = (
        projected_rows[:, query_total_width + rotary_pair_width :]
        .reshape(count_of_rows, KEY_VALUE_HEADS, HEAD_SIZE)
        .astype(jnp.bfloat16)
    )
    grouped_heads = query_matrix.reshape(
        count_of_rows, KEY_VALUE_HEADS, QUERY_HEADS // KEY_VALUE_HEADS, HEAD_SIZE
    )
    scores = jnp.einsum(
        "qhgd,khd->hgqk", grouped_heads, key_matrix, preferred_element_type=jnp.float32
    ) * HEAD_SIZE ** (-0.5)
    row_ids = jnp.arange(count_of_rows, dtype=jnp.int32)
    allowed = (row_ids[:, None] >= row_ids[None, :]) & (segment[:, None] == segment[None, :])
    exponent = jnp.where(allowed, jnp.exp(scores), 0.0)
    attention = exponent / jnp.sum(exponent, axis=-1, keepdims=True)
    attention_low = attention.astype(jnp.bfloat16)
    context = jnp.einsum(
        "hgqk,khd->qhgd", attention_low, value_matrix, preferred_element_type=jnp.float32
    )
    context = context.reshape(count_of_rows, query_total_width).astype(jnp.bfloat16)
    middle = hidden + jnp.dot(context, result_output, preferred_element_type=jnp.float32)
    inverse_two = lax.rsqrt(jnp.mean(middle * middle, axis=-1, keepdims=True) + norm_epsilon)
    scaled_two = middle * inverse_two
    normed_two = (scaled_two * gain_mixture).astype(jnp.bfloat16)
    logits = jnp.dot(normed_two, router, preferred_element_type=jnp.float32)
    router_exp = jnp.exp(logits)
    probability = router_exp / jnp.sum(router_exp, axis=-1, keepdims=True)
    return (
        token_position,
        inverse_one,
        scaled_one,
        normed,
        grouped_heads,
        key_matrix,
        value_matrix,
        attention,
        attention_low,
        context,
        middle,
        inverse_two,
        scaled_two,
        normed_two,
        probability,
    )


def layer_forward(layer_in, length_rows, route, weights, expert_weights, experts, capacity):
    hidden = layer_in.astype(jnp.float32)
    front_parts = front(hidden, length_rows, weights)
    middle = front_parts[10]
    normed_two = front_parts[13]
    probability = front_parts[14]
    member, target, anchor = slot_tables(route, experts, capacity)
    padded = jnp.concatenate([normed_two, jnp.zeros((1, MODEL_WIDTH), jnp.bfloat16)], axis=0)
    outgoing = padded[anchor // TOPK].reshape(experts, capacity, MODEL_WIDTH)
    up_weight, down_weight = expert_weights
    arrived = lax.all_to_all(outgoing, "dp", split_axis=0, concat_axis=0, tiled=True)
    flat_rows = arrived.reshape(-1, MODEL_WIDTH)
    gate_values = jnp.dot(flat_rows, up_weight, preferred_element_type=jnp.float32)
    activated = (jax.nn.silu(gate_values[:, :FFE]) * gate_values[:, FFE:]).astype(jnp.bfloat16)
    produced = jnp.dot(activated, down_weight, preferred_element_type=jnp.float32).astype(
        jnp.bfloat16
    )
    produced, gate_values, arrived = (
        produced.reshape(arrived.shape),
        gate_values.reshape(arrived.shape[0], arrived.shape[1], 2 * FFE),
        arrived,
    )
    returned = lax.all_to_all(produced, "dp", split_axis=0, concat_axis=0, tiled=True)
    picked = returned.reshape(-1, MODEL_WIDTH)[target].reshape(DEVICE_ROWS, TOPK, MODEL_WIDTH)
    weight = jnp.sum(jnp.where(member, probability[:, None, :], 0.0), axis=-1)
    mixed_out = middle + jnp.sum(weight[..., None] * picked.astype(jnp.float32), axis=1)
    return (mixed_out, (front_parts, arrived, gate_values, returned))


def layer_backward(stored, grad_in, route, weights, expert_weights, experts, capacity):
    front_parts, arrived_kept, gate_values, returned = stored
    joint, result_output, router, gain_attention, gain_mixture = weights
    up_weight, down_weight = expert_weights
    (
        token_position,
        inverse_one,
        scaled_one,
        normed,
        grouped_heads,
        key_matrix,
        value_matrix,
        attention,
        attention_low,
        context,
        middle,
        inverse_two,
        scaled_two,
        normed_two,
        probability,
    ) = front_parts
    member, target, anchor = slot_tables(route, experts, capacity)
    grad_out = grad_in.astype(jnp.float32)
    picked = (
        returned.reshape(-1, MODEL_WIDTH)[target]
        .reshape(DEVICE_ROWS, TOPK, MODEL_WIDTH)
        .astype(jnp.float32)
    )
    weight = jnp.sum(jnp.where(member, probability[:, None, :], 0.0), axis=-1)
    grad_weight = jnp.sum(grad_out[:, None, :] * picked, axis=-1)
    grad_picked = (
        (weight[..., None] * grad_out[:, None, :]).astype(jnp.bfloat16).reshape(-1, MODEL_WIDTH)
    )
    grad_padded = jnp.concatenate([grad_picked, jnp.zeros((1, MODEL_WIDTH), jnp.bfloat16)], axis=0)
    outgoing_grad = grad_padded[anchor].reshape(experts, capacity, MODEL_WIDTH)
    arrived_grad = lax.all_to_all(outgoing_grad, "dp", split_axis=0, concat_axis=0, tiled=True)
    flat_rows = arrived_kept.reshape(-1, MODEL_WIDTH)
    flat_grad = arrived_grad.reshape(-1, MODEL_WIDTH)
    gate_flat = gate_values.reshape(-1, 2 * FFE)
    gate_part = gate_flat[:, :FFE]
    up_part = gate_flat[:, FFE:]
    sigmoid = jax.nn.sigmoid(gate_part)
    silu_part = gate_part * sigmoid
    activated = (jax.nn.silu(gate_part) * up_part).astype(jnp.bfloat16)
    grad_down = contract_rows(activated, flat_grad)
    grad_act = contracted_columns(flat_grad, down_weight)
    grad_gate = grad_act * up_part * sigmoid * (1.0 + gate_part * (1.0 - sigmoid))
    grad_up = grad_act * silu_part
    grad_gate_up = jnp.concatenate([grad_gate, grad_up], axis=-1).astype(jnp.bfloat16)
    grad_expert_in = contract_rows(flat_rows, grad_gate_up)
    grad_rows = (
        contracted_columns(grad_gate_up, up_weight).astype(jnp.bfloat16).reshape(arrived_kept.shape)
    )
    grad_back = lax.all_to_all(grad_rows, "dp", split_axis=0, concat_axis=0, tiled=True)
    grad_normed_two = jnp.sum(
        grad_back.reshape(-1, MODEL_WIDTH)[target]
        .reshape(DEVICE_ROWS, TOPK, MODEL_WIDTH)
        .astype(jnp.float32),
        axis=1,
    )
    grad_prob = jnp.sum(jnp.where(member, grad_weight[..., None], 0.0), axis=1)
    grad_logit = (
        probability * (grad_prob - jnp.sum(grad_prob * probability, axis=-1, keepdims=True))
    ).astype(jnp.bfloat16)
    grad_router = contract_rows(normed_two, grad_logit)
    grad_normed_two = grad_normed_two + contracted_columns(grad_logit, router)
    grad_gain_two = jnp.sum(grad_normed_two * scaled_two, axis=0)
    scaled_grad_two = grad_normed_two * gain_mixture
    grad_middle = grad_out + inverse_two * (
        scaled_grad_two
        - scaled_two * jnp.mean(scaled_grad_two * scaled_two, axis=-1, keepdims=True)
    )
    branch_gradient = grad_middle.astype(jnp.bfloat16)
    grad_output = contract_rows(context, branch_gradient)
    grad_context = (
        contracted_columns(branch_gradient, result_output)
        .astype(jnp.bfloat16)
        .reshape(DEVICE_ROWS, KEY_VALUE_HEADS, QUERY_HEADS // KEY_VALUE_HEADS, HEAD_SIZE)
    )
    grad_attention = jnp.einsum(
        "qhgd,khd->hgqk", grad_context, value_matrix, preferred_element_type=jnp.float32
    )
    grad_value = jnp.einsum(
        "hgqk,qhgd->khd", attention_low, grad_context, preferred_element_type=jnp.float32
    )
    grad_scores = (
        attention * (grad_attention - jnp.sum(grad_attention * attention, axis=-1, keepdims=True))
    ).astype(jnp.bfloat16)
    score_scale = HEAD_SIZE ** (-0.5)
    grad_query = (
        jnp.einsum(
            "hgqk,khd->qhgd", grad_scores, key_matrix, preferred_element_type=jnp.float32
        ).reshape(DEVICE_ROWS, QUERY_HEADS, HEAD_SIZE)
        * score_scale
    )
    grad_key = (
        jnp.einsum("hgqk,qhgd->khd", grad_scores, grouped_heads, preferred_element_type=jnp.float32)
        * score_scale
    )
    grad_query = rotary_embedding(grad_query, token_position, -1.0)
    grad_key = rotary_embedding(grad_key, token_position, -1.0)
    grad_projected = jnp.concatenate(
        [
            grad_query.reshape(DEVICE_ROWS, -1),
            grad_key.reshape(DEVICE_ROWS, -1),
            grad_value.reshape(DEVICE_ROWS, -1),
        ],
        axis=-1,
    ).astype(jnp.bfloat16)
    grad_joint = contract_rows(normed, grad_projected)
    grad_normed = contracted_columns(grad_projected, joint)
    grad_gain_one = jnp.sum(grad_normed * scaled_one, axis=0)
    scaled_grad_one = grad_normed * gain_attention
    grad_hidden = grad_middle + inverse_one * (
        scaled_grad_one
        - scaled_one * jnp.mean(scaled_grad_one * scaled_one, axis=-1, keepdims=True)
    )
    return (
        grad_hidden,
        (
            grad_joint,
            grad_output,
            grad_router,
            grad_gain_one,
            grad_gain_two,
            grad_expert_in,
            grad_down,
        ),
    )


def body(
    tokens,
    cotangent,
    lengths,
    routes,
    combined_weight,
    output_weight,
    router_weight,
    attention_gain,
    mixture_gain,
    expert_gate_up,
    expert_down,
):
    experts = lax.axis_size("dp")
    capacity = 5 * DEVICE_ROWS * TOPK // (4 * experts)
    gathered = (
        lax.all_gather(combined_weight, "dp", axis=1, tiled=True),
        lax.all_gather(output_weight, "dp", axis=1, tiled=True),
        lax.all_gather(router_weight, "dp", axis=1, tiled=True),
        lax.all_gather(attention_gain, "dp", axis=1, tiled=True),
        lax.all_gather(mixture_gain, "dp", axis=1, tiled=True),
    )
    weights = (
        gathered[0][0],
        gathered[1][0],
        gathered[2][0],
        gathered[3][0].astype(jnp.float32),
        gathered[4][0].astype(jnp.float32),
    )
    expert_weights = (expert_gate_up[0, 0], expert_down[0, 0])
    section_id = lax.axis_index("section")
    leading = section_id == 0
    incoming = jnp.zeros((DEVICE_ROWS, MODEL_WIDTH), jnp.bfloat16)
    kept_list = []
    finals = []
    for tick_index in range(MB + 1):
        micro_id = jnp.clip(tick_index - section_id, 0, MB - 1)
        layer_in = jnp.where(leading, tokens[min(tick_index, MB - 1)], incoming)
        mixed_out, stored = layer_forward(
            layer_in,
            lengths[micro_id],
            routes[0, micro_id],
            weights,
            expert_weights,
            experts,
            capacity,
        )
        kept_list.append(stored)
        produced = mixed_out.astype(jnp.bfloat16)
        finals.append(produced)
        if tick_index < MB:
            incoming = passed_along(produced, "section", 1)
    totals = (
        jnp.zeros(weights[0].shape, jnp.float32),
        jnp.zeros(weights[1].shape, jnp.float32),
        jnp.zeros(weights[2].shape, jnp.float32),
        jnp.zeros((MODEL_WIDTH,), jnp.float32),
        jnp.zeros((MODEL_WIDTH,), jnp.float32),
    )
    expert_totals = (
        jnp.zeros(expert_weights[0].shape, jnp.float32),
        jnp.zeros(expert_weights[1].shape, jnp.float32),
    )
    returning = jnp.zeros((DEVICE_ROWS, MODEL_WIDTH), jnp.bfloat16)
    starts = []
    for tick_index in range(MB + 1):
        micro_raw = tick_index - 1 + section_id
        active = (micro_raw >= 0) & (micro_raw < MB)
        micro_id = jnp.clip(micro_raw, 0, MB - 1)
        grad_in = jnp.where(leading, returning, cotangent[min(tick_index, MB - 1)])
        grad_in = jnp.where(active, grad_in, jnp.zeros_like(grad_in))
        stored = jax.tree.map(
            lambda earlier, later: jnp.where(leading, earlier, later),
            kept_list[max(tick_index - 1, 0)],
            kept_list[min(tick_index + 1, MB)],
        )
        grad_hidden, layer_grads = layer_backward(
            stored, grad_in, routes[0, micro_id], weights, expert_weights, experts, capacity
        )
        sent_back = grad_hidden.astype(jnp.bfloat16)
        starts.append(sent_back)
        if tick_index < MB:
            returning = passed_along(sent_back, "section", -1)
        expert_totals = (expert_totals[0] + layer_grads[5], expert_totals[1] + layer_grads[6])
        totals = tuple((held + added for held, added in zip(totals, layer_grads[:5])))
    shards = in_one_piece(
        (
            totals[0][None].astype(jnp.bfloat16),
            totals[1][None].astype(jnp.bfloat16),
            totals[2][None].astype(jnp.bfloat16),
            totals[3][None].astype(jnp.bfloat16),
            totals[4][None].astype(jnp.bfloat16),
        ),
        "dp",
        1,
        2,
    )
    boundary = jnp.where(leading, jnp.stack(starts[1:]), jnp.stack(finals[1:]))[None]
    return (
        boundary,
        shards[0],
        shards[1],
        shards[2],
        shards[3],
        shards[4],
        expert_totals[0][None, None],
        expert_totals[1][None, None],
    )


def solution(mesh):
    return jax.shard_map(
        body,
        mesh=mesh,
        in_specs=(
            P(None, "dp", None),
            P(None, "dp", None),
            P(None, "dp", None),
            P("section", None, "dp", None),
            P("section", "dp", None),
            P("section", "dp", None),
            P("section", "dp", None),
            P("section", "dp"),
            P("section", "dp"),
            P("section", "dp", None, None),
            P("section", "dp", None, None),
        ),
        out_specs=(
            P("section", None, "dp", None),
            P("section", "dp", None),
            P("section", "dp", None),
            P("section", "dp", None),
            P("section", "dp"),
            P("section", "dp"),
            P("section", "dp", None, None),
            P("section", "dp", None, None),
        ),
        check_vma=False,
    )
```

profile of v0, /device:TPU:28, one launch (start us, length us, event | category | flops | bytes accessed | tf_op | source)
XLA Modules:
  0.0 2189.1 jit_solution(3393950756745232911)
XLA Ops:
  13.6 37.1 %all-reduce.8 = (bf16[1536]{0:T(1024)(128)(2,1)S(1)}, bf16[1536]{0:T(1024)(128)(2,1)S(1)}) all-reduce(bf16[1536]{0:T(1024)(128)(2,1)S(1)} %dynamic-update-slice, bf16[1536]{0:T(1024)(128)(2,1)S(1)} %dynamic-update-slice.1), channel_id=1, replica_groups=mesh['section'=2,'dp'=16] {'dp'}, use_global_device_ids=true, to_apply=%add.6 | all-reduce | flops 3072 | bytes 12288
  63.5 54.6 %all-gather.3.cloned.1.call-done = bf16[1,1536,2560]{2,1,0:T(8,128)(2,1)} async-done(((bf16[1,96,2560]{2,1,0:T(8,128)(2,1)}), bf16[1,1536,2560]{2,1,0:T(8,128)(2,1)}) %all-gather.3.cloned.1.call-update) | async-done | bytes 7864336 | tf_op jit(solution)/shard_map/all_gather | solution.py:348
  135.3 64.0 %all-gather.5.cloned.1.call-done = bf16[1,1536,1536]{2,1,0:T(8,128)(2,1)} async-done(((bf16[1,96,1536]{2,1,0:T(8,128)(2,1)}), bf16[1,1536,1536]{2,1,0:T(8,128)(2,1)}) %all-gather.5.cloned.1.call-update) | async-done | bytes 4718608 | tf_op jit(solution)/shard_map/all_gather | solution.py:349
  204.5 10.1 gather_fusion
  214.6 92.0 %all_to_all.65 = bf16[16,80,1536]{2,1,0:T(8,128)(2,1)S(1)} all-to-all(bf16[16,80,1536]{2,1,0:T(8,128)(2,1)} %bitcast.595), channel_id=1, replica_groups=mesh['section'=2,'dp'=16] {'dp'}, dimensions={0} | all-to-all | bytes 7864320 | tf_op jit(solution)/shard_map/all_to_all | solution.py:182
  324.1 111.5 %all_gather.19 = bf16[1,1536,16]{2,0,1:T(2,128)(2,1)} all-gather(bf16[1,96,16]{2,0,1:T(2,128)(2,1)} %copy.284), channel_id=1, replica_groups=mesh['section'=2,'dp'=16] {'dp'}, dimensions={1}, use_global_device_ids=true | all-gather | bytes 52224 | tf_op jit(solution)/shard_map/all_gather | solution.py:350
  464.8 10.0 gather_fusion.1
  509.0 10.1 gather_fusion.3
  519.1 96.8 %all_to_all.66 = bf16[16,80,1536]{2,1,0:T(8,128)(2,1)S(1)} all-to-all(bf16[16,80,1536]{2,1,0:T(8,128)(2,1)} %bitcast.596), channel_id=1, replica_groups=mesh['section'=2,'dp'=16] {'dp'}, dimensions={0} | all-to-all | bytes 7864320 | tf_op jit(solution)/shard_map/all_to_all | solution.py:182
  659.7 58.3 %all-to-all-done.5 = bf16[16,80,1536]{2,1,0:T(8,128)(2,1)} async-done(((bf16[16,80,1536]{2,1,0:T(8,128)(2,1)}), bf16[16,80,1536]{2,1,0:T(8,128)(2,1)}, u32[]{:S(2)}, u32[]{:S(2)}) %all-to-all-start.5) | async-done | bytes 3932192 | tf_op jit(solution)/shard_map/all_to_all | solution.py:194
  718.1 10.0 gather_fusion.6
  764.0 10.1 gather_fusion.8
  774.1 93.5 %all_to_all.67 = bf16[16,80,1536]{2,1,0:T(8,128)(2,1)} all-to-all(bf16[16,80,1536]{2,1,0:T(8,128)(2,1)} %bitcast.597), channel_id=1, replica_groups=mesh['section'=2,'dp'=16] {'dp'}, dimensions={0} | all-to-all | bytes 7864320 | tf_op jit(solution)/shard_map/all_to_all | solution.py:182
  867.6 13.5 broadcast_select_fusion.6
  905.5 74.8 %all-to-all-done.9 = bf16[16,80,1536]{2,1,0:T(8,128)(2,1)} async-done(((bf16[16,80,1536]{2,1,0:T(8,128)(2,1)}), bf16[16,80,1536]{2,1,0:T(8,128)(2,1)}, u32[]{:S(2)}, u32[]{:S(2)}) %all-to-all-start.9) | async-done | bytes 3932192 | tf_op jit(solution)/shard_map/all_to_all | solution.py:194
  1011.4 11.3 gather_fusion.2
  1022.7 92.3 %all_to_all.68 = bf16[16,80,1536]{2,1,0:T(8,128)(2,1)S(1)} all-to-all(bf16[16,80,1536]{2,1,0:T(8,128)(2,1)} %bitcast.598), channel_id=1, replica_groups=mesh['section'=2,'dp'=16] {'dp'}, dimensions={0} | all-to-all | bytes 7864320 | tf_op jit(solution)/shard_map/all_to_all | solution.py:236
  1146.5 73.0 %all-to-all-done.4 = bf16[16,80,1536]{2,1,0:T(8,128)(2,1)} async-done(((bf16[16,80,1536]{2,1,0:T(8,128)(2,1)}), bf16[16,80,1536]{2,1,0:T(8,128)(2,1)}, u32[]{:S(2)}, u32[]{:S(2)}) %all-to-all-start.4) | async-done | bytes 3932192 | tf_op jit(solution)/shard_map/all_to_all | solution.py:254
  1219.5 10.0 gather_fusion.4
  1280.9 11.3 gather_fusion.7
  1292.2 93.4 %all_to_all.69 = bf16[16,80,1536]{2,1,0:T(8,128)(2,1)S(1)} all-to-all(bf16[16,80,1536]{2,1,0:T(8,128)(2,1)} %bitcast.599), channel_id=1, replica_groups=mesh['section'=2,'dp'=16] {'dp'}, dimensions={0} | all-to-all | bytes 7864320 | tf_op jit(solution)/shard_map/all_to_all | solution.py:236
  1430.8 65.5 %all-to-all-done.8 = bf16[16,80,1536]{2,1,0:T(8,128)(2,1)} async-done(((bf16[16,80,1536]{2,1,0:T(8,128)(2,1)}), bf16[16,80,1536]{2,1,0:T(8,128)(2,1)}, u32[]{:S(2)}, u32[]{:S(2)}) %all-to-all-start.8) | async-done | bytes 3932192 | tf_op jit(solution)/shard_map/all_to_all | solution.py:254
  1496.4 10.0 gather_fusion.9
  1536.5 10.2 gather_fusion.13
  1561.3 11.3 gather_fusion.11
  1572.7 93.1 %all_to_all.70 = bf16[16,80,1536]{2,1,0:T(8,128)(2,1)S(1)} all-to-all(bf16[16,80,1536]{2,1,0:T(8,128)(2,1)} %bitcast.600), channel_id=1, replica_groups=mesh['section'=2,'dp'=16] {'dp'}, dimensions={0} | all-to-all | bytes 7864320 | tf_op jit(solution)/shard_map/all_to_all | solution.py:236
  1713.7 63.1 %all-to-all-done.11 = bf16[16,80,1536]{2,1,0:T(8,128)(2,1)} async-done(((bf16[16,80,1536]{2,1,0:T(8,128)(2,1)}), bf16[16,80,1536]{2,1,0:T(8,128)(2,1)}, u32[]{:S(2)}, u32[]{:S(2)}) %all-to-all-start.11) | async-done | bytes 3932192 | tf_op jit(solution)/shard_map/all_to_all | solution.py:254
  1776.9 10.1 gather_fusion.12
  1829.9 16.0 add_convert_fusion
  1845.9 19.5 concatenate.162
  1907.6 10.1 add_bitcast_fusion
  1920.2 246.4 %all-to-all-done.12 = bf16[16,1,96,4114]{3,2,1,0:T(8,128)(2,1)} async-done(((bf16[16,1,96,4114]{3,2,1,0:T(8,128)(2,1)}), bf16[16,1,96,4114]{3,2,1,0:T(8,128)(2,1)}, u32[]{:S(2)}, u32[]{:S(2)}) %all-to-all-start.12) | async-done | bytes 12638240 | tf_op jit(solution)/shard_map/all_to_all | solution.py:34
  (735 shorter events, 578.0 us)
Async XLA Ops:
  7.2 299.4 %copy-start = (bf16[1,1,1536,1024]{3,2,1,0:T(8,128)(2,1)S(1)}, bf16[1,1,1536,1024]{3,2,1,0:T(8,128)(2,1)}, u32[]{:S(2)}) copy-start(bf16[1,1,1536,1024]{3,2,1,0:T(8,128)(2,1)} %param.20) | copy-start | bytes 9437188
  7.2 52.6 %copy-start.152 = (s32[2,1,4]{2,1,0:T(1,128)S(1)}, s32[2,1,4]{2,1,0:T(1,128)}, u32[]{:S(2)}) copy-start(s32[2,1,4]{2,1,0:T(1,128)} %param.13) | copy-start | bytes 100
  7.2 110.9 %all-gather.3.cloned.1.call-start = ((), (), s32[]{:S(2)}) async-start(), calls=%async_computation.13 | async-start | bytes 8355840 | tf_op jit(solution)/shard_map/all_gather | solution.py:348
  7.9 191.3 %all-gather.5.cloned.1.call-start = ((), (), s32[]{:S(2)}) async-start(), calls=%async_computation.14 | async-start | bytes 5013504 | tf_op jit(solution)/shard_map/all_gather | solution.py:349
  52.1 66.0 %copy-start.127 = (s32[1,1,128,8]{2,3,1,0:T(8,128)}, s32[1,1,128,8]{2,3,1,0:T(8,128)S(1)}, u32[]{:S(2)}) copy-start(s32[1,1,128,8]{2,3,1,0:T(8,128)S(1)} %get-tuple-element.149) | copy-start | bytes 12292
  52.1 66.0 %copy-start.128 = (s32[1,1,128,8]{2,3,1,0:T(8,128)}, s32[1,1,128,8]{2,3,1,0:T(8,128)S(1)}, u32[]{:S(2)}) copy-start(s32[1,1,128,8]{2,3,1,0:T(8,128)S(1)} %get-tuple-element.151) | copy-start | bytes 12292
  59.6 58.5 %copy-start.163 = (s32[128]{0:T(128)}, s32[128]{0:T(128)S(1)}, u32[]{:S(2)}) copy-start(s32[128]{0:T(128)S(1)} %convert_reduce_fusion.4) | copy-start | bytes 1540
  59.7 58.4 %copy-start.165 = (s32[128]{0:T(128)}, s32[128]{0:T(128)S(1)}, u32[]{:S(2)}) copy-start(s32[128]{0:T(128)S(1)} %convert_reduce_fusion.5) | copy-start | bytes 1540
  61.7 56.4 %copy-start.132 = (f32[128]{0:T(128)}, f32[128]{0:T(128)S(1)}, u32[]{:S(2)}) copy-start(f32[128]{0:T(128)S(1)} %add_rsqrt_fusion.5) | copy-start | bytes 1540
  135.2 67.3 %copy-start.60 = (bf16[8,64,3,128]{3,1,2,0:T(8,128)(2,1)}, bf16[8,64,3,128]{3,1,2,0:T(8,128)(2,1)S(1)}, u32[]{:S(2)}) copy-start(bf16[8,64,3,128]{3,1,2,0:T(8,128)(2,1)S(1)} %convolution_convert_fusion.8) | copy-start | bytes 1179652
  203.6 258.7 %copy-start.42 = (bf16[128,1536]{1,0:T(8,128)(2,1)}, bf16[128,1536]{1,0:T(8,128)(2,1)S(1)}, u32[]{:S(2)}) copy-start(bf16[128,1536]{1,0:T(8,128)(2,1)S(1)} %multiply_convert_fusion.14) | copy-start | bytes 1179652
  315.6 149.2 %all-to-all-start.1 = ((bf16[16,80,1536]{2,1,0:T(8,128)(2,1)}), bf16[16,80,1536]{2,1,0:T(8,128)(2,1)}, u32[]{:S(2)}, u32[]{:S(2)}) async-start(bf16[16,80,1536]{2,1,0:T(8,128)(2,1)} %bitcast.618), calls=%async_computation.1 | async-start | bytes 7864320 | tf_op jit(solution)/shard_map/all_to_all | solution.py:194
  479.7 2.6 collective-permute-start
  482.6 21.1 copy-start.7
  508.2 147.8 %copy-start.44 = (bf16[128,1536]{1,0:T(8,128)(2,1)}, bf16[128,1536]{1,0:T(8,128)(2,1)S(1)}, u32[]{:S(2)}) copy-start(bf16[128,1536]{1,0:T(8,128)(2,1)S(1)} %multiply_convert_fusion.13) | copy-start | bytes 1179652
  625.0 93.1 %all-to-all-start.5 = ((bf16[16,80,1536]{2,1,0:T(8,128)(2,1)}), bf16[16,80,1536]{2,1,0:T(8,128)(2,1)}, u32[]{:S(2)}, u32[]{:S(2)}) async-start(bf16[16,80,1536]{2,1,0:T(8,128)(2,1)} %bitcast.619), calls=%async_computation.5 | async-start | bytes 7864320 | tf_op jit(solution)/shard_map/all_to_all | solution.py:194
  733.1 2.7 collective-permute-start.2
  735.9 22.7 %copy-start.9 = (bf16[128,1536]{1,0:T(8,128)(2,1)}, bf16[128,1536]{1,0:T(8,128)(2,1)S(1)}, u32[]{:S(2)}) copy-start(bf16[128,1536]{1,0:T(8,128)(2,1)S(1)} %get-tuple-element.89) | copy-start | bytes 1179652
  763.2 379.7 %copy-start.46 = (bf16[128,1536]{1,0:T(8,128)(2,1)}, bf16[128,1536]{1,0:T(8,128)(2,1)S(1)}, u32[]{:S(2)}) copy-start(bf16[128,1536]{1,0:T(8,128)(2,1)S(1)} %multiply_convert_fusion.12) | copy-start | bytes 1179652
  888.2 92.1 %all-to-all-start.9 = ((bf16[16,80,1536]{2,1,0:T(8,128)(2,1)}), bf16[16,80,1536]{2,1,0:T(8,128)(2,1)}, u32[]{:S(2)}, u32[]{:S(2)}) async-start(bf16[16,80,1536]{2,1,0:T(8,128)(2,1)} %bitcast.623), calls=%async_computation.9 | async-start | bytes 7864320 | tf_op jit(solution)/shard_map/all_to_all | solution.py:194
  1022.7 92.3 %copy-start.187 = (bf16[1,1,512,1536]{3,2,1,0:T(8,128)(2,1)S(1)}, bf16[1,1,512,1536]{3,2,1,0:T(8,128)(2,1)}, u32[]{:S(2)}) copy-start(bf16[1,1,512,1536]{3,2,1,0:T(8,128)(2,1)} %param.21) | copy-start | bytes 4718596
  1127.7 91.8 %all-to-all-start.4 = ((bf16[16,80,1536]{2,1,0:T(8,128)(2,1)}), bf16[16,80,1536]{2,1,0:T(8,128)(2,1)}, u32[]{:S(2)}, u32[]{:S(2)}) async-start(bf16[16,80,1536]{2,1,0:T(8,128)(2,1)} %bitcast.621), calls=%async_computation.4 | async-start | bytes 7864320 | tf_op jit(solution)/shard_map/all_to_all | solution.py:254
  1146.5 87.2 %copy-start.129 = (bf16[128,16]{0,1:T(8,128)(2,1)}, bf16[128,16]{0,1:T(8,128)(2,1)S(1)}, u32[]{:S(2)}) copy-start(bf16[128,16]{0,1:T(8,128)(2,1)S(1)} %multiply_convert_fusion.17) | copy-start | bytes 12292
  1253.3 12.9 collective-permute-start.1
  1292.2 93.4 %copy-start.188 = (bf16[1,1,512,1536]{3,2,1,0:T(8,128)(2,1)S(1)}, bf16[1,1,512,1536]{3,2,1,0:T(8,128)(2,1)}, u32[]{:S(2)}) copy-start(bf16[1,1,512,1536]{3,2,1,0:T(8,128)(2,1)} %param.21) | copy-start | bytes 4718596
  1398.3 98.1 %all-to-all-start.8 = ((bf16[16,80,1536]{2,1,0:T(8,128)(2,1)}), bf16[16,80,1536]{2,1,0:T(8,128)(2,1)}, u32[]{:S(2)}, u32[]{:S(2)}) async-start(bf16[16,80,1536]{2,1,0:T(8,128)(2,1)} %bitcast.622), calls=%async_computation.8 | async-start | bytes 7864320 | tf_op jit(solution)/shard_map/all_to_all | solution.py:254
  1532.0 14.7 collective-permute-start.3
  1572.7 93.1 %copy-start.189 = (bf16[1,1,512,1536]{3,2,1,0:T(8,128)(2,1)S(1)}, bf16[1,1,512,1536]{3,2,1,0:T(8,128)(2,1)}, u32[]{:S(2)}) copy-start(bf16[1,1,512,1536]{3,2,1,0:T(8,128)(2,1)} %param.21) | copy-start | bytes 4718596
  1678.4 98.5 %all-to-all-start.11 = ((bf16[16,80,1536]{2,1,0:T(8,128)(2,1)}), bf16[16,80,1536]{2,1,0:T(8,128)(2,1)}, u32[]{:S(2)}, u32[]{:S(2)}) async-start(bf16[16,80,1536]{2,1,0:T(8,128)(2,1)} %bitcast.620), calls=%async_computation.11 | async-start | bytes 7864320 | tf_op jit(solution)/shard_map/all_to_all | solution.py:254
  1865.5 301.1 %all-to-all-start.12 = ((bf16[16,1,96,4114]{3,2,1,0:T(8,128)(2,1)}), bf16[16,1,96,4114]{3,2,1,0:T(8,128)(2,1)}, u32[]{:S(2)}, u32[]{:S(2)}) async-start(bf16[16,1,96,4114]{3,2,1,0:T(8,128)(2,1)} %concatenate.162), calls=%async_computation.12 | async-start | bytes 25952256 | tf_op jit(solution)/shard_map/all_to_all | solution.py:34
  1883.6 13.9 slice-start.6
  1883.6 17.8 slice-start.4
  (190 other events, 789.6 us)
Sparse Core Ops, SparseCore 0:
  10.8 107.2 all-gather.2
  120.9 78.3 all-gather.4
where the time goes:
time: 2200 us; the launch traced here: 2190 us
  blocking collectives  710 us (32%)
  waiting for transfers between devices  701 us (32%)
  local copies, waits for them, and re-layouts  316 us (14%)
  matrix products  260 us (12%)
  other arithmetic  131 us (6%)
  starting transfers between devices  53.7 us (2%)
    all_to_all x3, blocking collectives, layer_forward(): lax.all_to_all(outgoing, 'dp', split_axis=0, concat_axis=0, tiled=True)  282 us
    all_to_all x3, blocking collectives, layer_backward(): lax.all_to_all(outgoing_grad, 'dp', split_axis=0, concat_axis=0, tiled=True)  279 us
    all_to_all x1, waiting for transfers between devices, sum_at_owner(): lax.all_to_all(pieces, axis, split_axis=0, concat_axis=0, tiled=True)  246 us
    all_to_all x3, waiting for transfers between devices, layer_backward(): lax.all_to_all(grad_rows, 'dp', split_axis=0, concat_axis=0, tiled=True)  202 us
    all_to_all x3, waiting for transfers between devices, layer_forward(): lax.all_to_all(produced, 'dp', split_axis=0, concat_axis=0, tiled=True)  133 us
    all_gather x1, blocking collectives, body(): lax.all_gather(router_weight, 'dp', axis=1, tiled=True)  111 us
    dot_general x15, matrix products, contract_rows(): lax.dot_general(left_side, right_side, (((0,), (0,)), ((), ())), preferre...  89.6 us
    dot_general x15, matrix products, contracted_columns(): lax.dot_general(left_side, right_side, (((1,), (1,)), ((), ())), preferre...  68.7 us
  transfers between devices with their start and end apart: 13, of which 8 were waited for; matrix products, arithmetic and copies ran while one was open for 11% of the time, Pallas kernels for 0%

commit v1 on v0

v1 whole, which is shorter than its diff:
```python
import functools
import jax
import jax.numpy as jnp
from jax import lax
from jax.experimental import pallas as pl
from jax.experimental.pallas import tpu as pltpu
from jax.sharding import PartitionSpec as P

MODEL_WIDTH = 1536
QUERY_HEADS = 24
KEY_VALUE_HEADS = 8
GROUP = QUERY_HEADS // KEY_VALUE_HEADS
HEAD_SIZE = 64
FFE = 512
TOPK = 8
DEVICE_ROWS = 128
NSEQ = 4
QUERY_WIDTH = QUERY_HEADS * HEAD_SIZE
KEY_WIDTH = KEY_VALUE_HEADS * HEAD_SIZE
SCORE_SCALE = HEAD_SIZE ** (-0.5)
norm_epsilon = 1e-06
CHUNK_ROWS = 2048

VMEM_BYTES = 66_000_000


def torus_axes(count):
    side = 1
    while (side + 1) ** 3 <= count:
        side += 1
    assert count % (side * side) == 0
    return [(side * side, count // (side * side)), (1, side), (side, side)]


def offsets(sizes):
    return [(k, j, i) for k in range(sizes[0]) for j in range(sizes[1]) for i in range(sizes[2])]


class Place:
    def __init__(self, axes, order):
        self.me = lax.axis_index("dp")
        self.sec = lax.axis_index("section")
        long, first, second = axes
        if order is None:
            flip = self.sec
            stride_one = first[0] + (second[0] - first[0]) * flip
            stride_two = second[0] + (first[0] - second[0]) * flip
            assert first[1] == second[1]
            self.axes = [long, (stride_one, first[1]), (stride_two, second[1])]
        elif order == 0:
            self.axes = [long, first, second]
        else:
            self.axes = [long, second, first]
        self.sizes = [size for _, size in self.axes]

    def moved(self, steps):
        out = self.me
        for (stride, size), step in zip(self.axes, steps):
            if step % size:
                digit = lax.rem(lax.div(self.me, stride), size)
                out = out + (lax.rem(digit + (step % size), size) - digit) * stride
        return out

    def source(self, offs):
        return self.moved([-o for o in offs])

    def target(self, offs):
        return self.moved(list(offs))

    def flat(self, offs):
        return (offs[0] * self.sizes[1] + offs[1]) * self.sizes[2] + offs[2]


def last_hop(offs):
    for axis in (2, 1, 0):
        if offs[axis]:
            hop = [0, 0, 0]
            hop[axis] = offs[axis]
            base = list(offs)
            base[axis] = 0
            return tuple(hop), tuple(base)
    return None


def greet(axes, pair):
    place = Place(axes, 0)
    barrier = pltpu.get_barrier_semaphore()
    count = 0
    for axis in range(3):
        for step in range(1, place.sizes[axis]):
            hop = [0, 0, 0]
            hop[axis] = step
            pl.semaphore_signal(barrier, inc=1, device_id={"dp": place.target(hop)}, device_id_type=pl.DeviceIdType.MESH)
            count += 1
    if pair:
        pl.semaphore_signal(barrier, inc=1, device_id={"section": 1 - place.sec}, device_id_type=pl.DeviceIdType.MESH)
        count += 1
    pl.semaphore_wait(barrier, count)


def gather_kernel(axes, pair, count, *refs):
    ins, outs = refs[:count], refs[count : 2 * count]
    send, recv, local = refs[2 * count : 2 * count + 3]
    psend, precv = refs[2 * count + 3 :] if pair else (None, None)
    streams = []
    for a in range(count):
        if pair:
            place = Place(axes, None)
            half = ins[a].shape[1]
            cols = pl.ds(pl.multiple_of(place.sec * half, 128), half)
            streams.append((place, ins[a], lambda b, o=outs[a], c=cols: o.at[b, :, c]))
        else:
            half = ins[a].shape[0] // 2
            for h in range(2):
                rows = pl.ds(h * half, half)
                streams.append((Place(axes, h), ins[a].at[rows], lambda b, o=outs[a], r=rows: o.at[b, r]))

    def copy(s, offs):
        place, own, out = streams[s]
        hop, base = last_hop(offs)
        block = place.source(base)
        src = out(block) if any(base) else own
        f = place.flat(offs)
        return pltpu.make_async_remote_copy(
            src_ref=src, dst_ref=out(block), send_sem=send.at[s, f], recv_sem=recv.at[s, f],
            device_id={"dp": place.target(hop)}, device_id_type=pl.DeviceIdType.MESH)

    def share(s, offs):
        place, own, out = streams[s]
        block = place.source(offs)
        src = out(block) if any(offs) else own
        f = place.flat(offs)
        return pltpu.make_async_remote_copy(
            src_ref=src, dst_ref=out(block), send_sem=psend.at[s, f], recv_sem=precv.at[s, f],
            device_id={"section": 1 - place.sec}, device_id_type=pl.DeviceIdType.MESH)

    greet(axes, pair)
    ids = range(len(streams))
    n0, n1, n2 = streams[0][0].sizes
    keep = []
    for s in ids:
        place, own, out = streams[s]
        c = pltpu.make_async_copy(own, out(place.me), local.at[s])
        c.start()
        keep.append(c)
    for k in range(1, n0):
        for s in ids:
            copy(s, (k, 0, 0)).start()

    def first(k):
        for s in ids:
            if k:
                copy(s, (k, 0, 0)).wait_recv()
            for j in range(1, n1):
                copy(s, (k, j, 0)).start()
            for i in range(1, n2):
                copy(s, (k, 0, i)).start()
            if pair:
                share(s, (k, 0, 0)).start()

    def second(k):
        for j in range(1, n1):
            for s in ids:
                copy(s, (k, j, 0)).wait_recv()
                for i in range(1, n2):
                    copy(s, (k, j, i)).start()
                if pair:
                    share(s, (k, j, 0)).start()

    def third(k):
        for j in range(n1):
            for i in range(1, n2):
                for s in ids:
                    copy(s, (k, j, i)).wait_recv()
                    if pair:
                        share(s, (k, j, i)).start()

    for k in range(n0 + 2):
        if k < n0:
            first(k)
        if 0 <= k - 1 < n0:
            second(k - 1)
        if 0 <= k - 2 < n0:
            third(k - 2)
    for s in ids:
        for offs in offsets((n0, n1, n2)):
            if any(offs):
                copy(s, offs).wait_send()
            if pair:
                share(s, offs).wait()
    for c in keep:
        c.wait()


def gather_all(arrays, count, cid, pair=False):
    axes = torus_axes(count)
    streams = len(arrays) * (1 if pair else 2)
    sem = pltpu.SemaphoreType.DMA((streams, count))
    out_shape = [jax.ShapeDtypeStruct((count, a.shape[0], a.shape[1] * (2 if pair else 1)), a.dtype) for a in arrays]
    scratch = [sem, sem, pltpu.SemaphoreType.DMA((streams,))]
    if pair:
        scratch += [sem, sem]
    sent = sum(a.size * a.dtype.itemsize for a in arrays) * (count - 1)
    return pl.pallas_call(
        functools.partial(gather_kernel, axes, pair, len(arrays)),
        out_shape=out_shape,
        in_specs=[pl.BlockSpec(memory_space=pltpu.VMEM)] * len(arrays),
        out_specs=[pl.BlockSpec(memory_space=pl.ANY)] * len(arrays),
        scratch_shapes=scratch,
        compiler_params=pltpu.CompilerParams(collective_id=cid, has_side_effects=True),
        cost_estimate=pl.CostEstimate(flops=0, bytes_accessed=2 * sent, transcendentals=0),
        name="spread" if not pair else "spread_pair",
    )(*arrays)


def reduce_kernel(axes, pair, count, *refs):
    ins, outs = refs[:count], refs[count : 2 * count]
    rest = list(refs[2 * count :])
    send, recv = rest[:2]
    rest = rest[2:]
    if pair:
        psend, precv = rest[:2]
        rest = rest[2:]
    streams = []
    for a in range(count):
        if pair:
            got, held, pgot, psum = rest[:4]
            rest = rest[4:]
            place = Place(axes, None)
            half = outs[a].shape[1]
            mine = pl.ds(pl.multiple_of(place.sec * half, 128), half)
            other = pl.ds(pl.multiple_of((1 - place.sec) * half, 128), half)
            streams.append(dict(place=place, got=got, held=held, pgot=pgot, psum=psum, raw=ins[a], mine=mine, other=other,
                                out=outs[a], rows=outs[a].shape[0]))
        else:
            got, held = rest[:2]
            rest = rest[2:]
            half = outs[a].shape[0] // 2
            for h in range(2):
                rows = pl.ds(h * half, half)
                streams.append(dict(place=Place(axes, h), got=got.at[h], held=held.at[h], raw=ins[a], span=rows,
                                    out=outs[a].at[rows], rows=half))
    step = 8 if streams[0]["rows"] % 16 else 16

    def own_ref(t, offs):
        if pair:
            return t["psum"].at[t["place"].flat(offs)]
        return t["raw"].at[t["place"].target(offs), t["span"]]

    def summed(t, sources, dest):
        def one(r, _):
            rows = pl.ds(pl.multiple_of(r * step, step), step)
            total = sources[0][rows].astype(jnp.float32)
            for source in sources[1:]:
                total = total + source[rows].astype(jnp.float32)
            dest[rows] = total.astype(dest.dtype)
            return 0

        lax.fori_loop(0, t["rows"] // step, one, 0)

    def copy(s, offs):
        t = streams[s]
        place = t["place"]
        hop, base = last_hop(offs)
        f = place.flat(offs)
        src = own_ref(t, offs) if hop[2] else t["held"].at[f // place.sizes[2]]
        return pltpu.make_async_remote_copy(
            src_ref=src, dst_ref=t["got"].at[f], send_sem=send.at[s, f], recv_sem=recv.at[s, f],
            device_id={"dp": place.target(hop)}, device_id_type=pl.DeviceIdType.MESH)

    def share(s, offs):
        t = streams[s]
        place = t["place"]
        f = place.flat(offs)
        return pltpu.make_async_remote_copy(
            src_ref=t["raw"].at[place.target((offs[0], offs[2], offs[1])), :, t["other"]], dst_ref=t["pgot"].at[f],
            send_sem=psend.at[s, f], recv_sem=precv.at[s, f],
            device_id={"section": 1 - place.sec}, device_id_type=pl.DeviceIdType.MESH)

    ids = range(len(streams))
    n0, n1, n2 = streams[0]["place"].sizes
    greet(axes, pair)

    def phase_pair(k):
        for j in reversed(range(n1)):
            for i in reversed(range(n2)):
                for s in ids:
                    share(s, (k, j, i)).start()

    def phase_first(k):
        for j in reversed(range(n1)):
            for i in reversed(range(n2)):
                for s in ids:
                    t = streams[s]
                    if pair:
                        share(s, (k, j, i)).wait_recv()
                        f = t["place"].flat((k, j, i))
                        summed(t, [t["raw"].at[t["place"].target((k, j, i)), :, t["mine"]], t["pgot"].at[f]], t["psum"].at[f])
                    if i:
                        copy(s, (k, j, i)).start()

    def phase_second(k):
        for j in range(1, n1):
            for s in ids:
                t = streams[s]
                for i in range(1, n2):
                    copy(s, (k, j, i)).wait_recv()
                parts = [own_ref(t, (k, j, 0))] + [t["got"].at[t["place"].flat((k, j, i))] for i in range(1, n2)]
                summed(t, parts, t["held"].at[t["place"].flat((k, j, 0)) // n2])
                copy(s, (k, j, 0)).start()

    def gathered_parts(s, k):
        t = streams[s]
        offs = [(k, 0, i) for i in range(1, n2)] + [(k, j, 0) for j in range(1, n1)]
        for o in offs:
            copy(s, o).wait_recv()
        return [own_ref(t, (k, 0, 0))] + [t["got"].at[t["place"].flat(o)] for o in offs]

    def phase_third(k):
        for s in ids:
            t = streams[s]
            parts = gathered_parts(s, k)
            if k:
                summed(t, parts, t["held"].at[t["place"].flat((k, 0, 0)) // n2])
                copy(s, (k, 0, 0)).start()
            else:
                for q in range(1, n0):
                    copy(s, (q, 0, 0)).wait_recv()
                    parts.append(t["got"].at[t["place"].flat((q, 0, 0))])
                summed(t, parts, t["out"])

    chunks = list(range(1, n0)) + [0]
    if pair:
        phase_pair(chunks[0])
    for c in range(n0 + 3):
        if pair and c + 1 < n0:
            phase_pair(chunks[c + 1])
        if c < n0:
            phase_first(chunks[c])
        if 0 <= c - 1 < n0:
            phase_second(chunks[c - 1])
        if 0 <= c - 2 < n0:
            phase_third(chunks[c - 2])
    for s in ids:
        for offs in offsets((n0, n1, n2)):
            if any(offs):
                copy(s, offs).wait_send()
            if pair:
                share(s, offs).wait_send()


def reduce_all(arrays, count, cid, pair=False):
    axes = torus_axes(count)
    streams = len(arrays) * (1 if pair else 2)
    sem = pltpu.SemaphoreType.DMA((streams, count))
    scratch = [sem, sem]
    if pair:
        scratch += [sem, sem]
    groups = count // axes[2][1]
    out_shape = []
    for a in arrays:
        rows, cols = a.shape[1:]
        if pair:
            cols = cols // 2
            scratch += [pltpu.VMEM((count, rows, cols), a.dtype), pltpu.VMEM((groups, rows, cols), a.dtype),
                        pltpu.VMEM((count, rows, cols), a.dtype), pltpu.VMEM((count, rows, cols), a.dtype)]
        else:
            scratch += [pltpu.VMEM((2, count, rows // 2, cols), a.dtype), pltpu.VMEM((2, groups, rows // 2, cols), a.dtype)]
        out_shape.append(jax.ShapeDtypeStruct((rows, cols), jnp.float32))
    sent = sum(a.size * a.dtype.itemsize for a in arrays)
    return pl.pallas_call(
        functools.partial(reduce_kernel, axes, pair, len(arrays)),
        out_shape=out_shape,
        in_specs=[pl.BlockSpec(memory_space=pltpu.VMEM)] * len(arrays),
        out_specs=[pl.BlockSpec(memory_space=pltpu.VMEM)] * len(arrays),
        scratch_shapes=scratch,
        compiler_params=pltpu.CompilerParams(collective_id=cid, has_side_effects=True, vmem_limit_bytes=VMEM_BYTES),
        cost_estimate=pl.CostEstimate(flops=0, bytes_accessed=2 * sent, transcendentals=0),
        name="fold" if not pair else "fold_pair",
    )(*arrays)

def swapped(value):
    return lax.ppermute(value, "section", [(0, 1), (1, 0)])


def layout(length_row):
    seq_ends = jnp.cumsum(length_row)
    seq_starts = seq_ends - length_row
    row_ids = jnp.arange(DEVICE_ROWS, dtype=jnp.int32)
    segment = jnp.sum((row_ids[:, None] >= seq_ends[None, :]).astype(jnp.int32), axis=-1)
    member = (segment[:, None] == jnp.arange(NSEQ, dtype=jnp.int32)[None, :]).astype(jnp.int32)
    token_position = row_ids - jnp.sum(member * seq_starts[None, :], axis=-1)
    return segment, token_position


def rotation(token_position):
    half_width = HEAD_SIZE // 2
    frequency = 10000.0 ** (-2.0 * jnp.arange(half_width, dtype=jnp.float32) / HEAD_SIZE)
    angles = token_position.astype(jnp.float32)[:, None] * frequency
    return jnp.cos(angles)[:, None, :], jnp.sin(angles)[:, None, :]


def rotary_embedding(values, cosine, sine):
    half_width = HEAD_SIZE // 2
    former, latter = values[..., :half_width], values[..., half_width:]
    return jnp.concatenate([former * cosine - latter * sine, latter * cosine + former * sine], axis=-1)


def dot(left, right):
    return jnp.dot(left, right, preferred_element_type=jnp.float32)


def dot_rows(left, right):
    return lax.dot_general(left, right, (((0,), (0,)), ((), ())), preferred_element_type=jnp.float32)


def dot_columns(left, right):
    return lax.dot_general(left, right, (((1,), (1,)), ((), ())), preferred_element_type=jnp.float32)


def router_chances(normed_two, router):
    chance = jnp.exp(dot(normed_two, router))
    return chance / jnp.sum(chance, axis=-1, keepdims=True)


def front(hidden, place, weights):
    joint, result_output, router, gain_attention, gain_mixture = weights
    allowed, cosine, sine = place
    rows = hidden.shape[0]
    inverse_one = lax.rsqrt(jnp.mean(hidden * hidden, axis=-1, keepdims=True) + norm_epsilon)
    scaled_one = hidden * inverse_one
    normed = (scaled_one * gain_attention).astype(jnp.bfloat16)
    projected = dot(normed, joint)
    query = rotary_embedding(projected[:, :QUERY_WIDTH].reshape(rows, QUERY_HEADS, HEAD_SIZE), cosine, sine)
    query = query.astype(jnp.bfloat16).reshape(rows, KEY_VALUE_HEADS, GROUP, HEAD_SIZE)
    key = rotary_embedding(projected[:, QUERY_WIDTH : QUERY_WIDTH + KEY_WIDTH].reshape(rows, KEY_VALUE_HEADS, HEAD_SIZE), cosine, sine)
    key = key.astype(jnp.bfloat16)
    value = projected[:, QUERY_WIDTH + KEY_WIDTH :].reshape(rows, KEY_VALUE_HEADS, HEAD_SIZE).astype(jnp.bfloat16)
    scores = jnp.einsum("qhgd,khd->hgqk", query, key, preferred_element_type=jnp.float32) * SCORE_SCALE
    exponent = jnp.where(allowed, jnp.exp(scores), 0.0)
    attention = exponent / jnp.sum(exponent, axis=-1, keepdims=True)
    context = jnp.einsum("hgqk,khd->qhgd", attention.astype(jnp.bfloat16), value, preferred_element_type=jnp.float32)
    context = context.reshape(rows, QUERY_WIDTH).astype(jnp.bfloat16)
    middle = hidden + dot(context, result_output)
    inverse_two = lax.rsqrt(jnp.mean(middle * middle, axis=-1, keepdims=True) + norm_epsilon)
    scaled_two = middle * inverse_two
    normed_two = (scaled_two * gain_mixture).astype(jnp.bfloat16)
    kept = (inverse_one, scaled_one, normed, query, key, value, attention, context, inverse_two, scaled_two, normed_two)
    return middle, normed_two, kept


def gates(everyone, up_weight):
    both = dot(everyone, up_weight)
    return both[:, :FFE], both[:, FFE:]


def expert_forward(everyone, mask, router, expert, count, me):
    up_weight, down_weight = expert
    chance = router_chances(everyone, router)
    own = jnp.arange(count, dtype=jnp.int32) == me
    weight = jnp.sum(jnp.where(own[None, :] & mask, chance, 0.0), axis=-1)
    gate, up = gates(everyone, up_weight)
    activated = (jax.nn.silu(gate) * up).astype(jnp.bfloat16)
    share = (dot(activated, down_weight) * weight[:, None]).astype(jnp.bfloat16)
    return share, weight, (gate, up)


def expert_backward(grads, everyone, weight, mask, held, expert):
    up_weight, down_weight = expert
    gate, up = held if held is not None else gates(everyone, up_weight)
    sigmoid = jax.nn.sigmoid(gate)
    silu = gate * sigmoid
    activated = silu * up
    grad_plain = dot_columns(grads, down_weight)
    grad_weight = jnp.where(mask[:, 0], jnp.sum(activated * grad_plain, axis=-1), 0.0)
    grad_act = grad_plain * weight[:, None]
    grad_gate = grad_act * up * sigmoid * (1.0 + gate * (1.0 - sigmoid))
    grad_gate_up = jnp.concatenate([grad_gate, grad_act * silu], axis=-1).astype(jnp.bfloat16)
    grad_down = dot_rows((activated * weight[:, None]).astype(jnp.bfloat16), grads)
    grad_up_weight = dot_rows(everyone, grad_gate_up)
    share = dot_columns(grad_gate_up, up_weight).astype(jnp.bfloat16)
    return share, grad_weight, grad_up_weight, grad_down


def pieces(value):
    return value.reshape(-1, CHUNK_ROWS, *value.shape[1:])


def mixture_forward(normed_two, router, mask, expert, count, me):
    (spread,) = gather_all([normed_two], count, 0)
    everyone = spread.reshape(-1, MODEL_WIDTH)
    if everyone.shape[0] <= CHUNK_ROWS:
        share, weight, held = expert_forward(everyone, mask, router, expert, count, me)
    else:
        share, weight = lax.map(
            lambda part: expert_forward(part[0], part[1], router, expert, count, me)[:2], (pieces(everyone), pieces(mask)))
        held = None
    (mixed,) = reduce_all([share.reshape(spread.shape)], count, 1)
    return mixed, (everyone, weight.reshape(-1), held)


def mixture_backward(grad_out, mask, kept, expert, count):
    everyone, weight, held = kept
    (spread,) = gather_all([grad_out], count, 0)
    grads = spread.reshape(-1, MODEL_WIDTH)
    if grads.shape[0] <= CHUNK_ROWS:
        share, grad_weight, grad_up, grad_down = expert_backward(grads, everyone, weight, mask, held, expert)
    else:
        def step(sums, part):
            share, grad_weight, grad_up, grad_down = expert_backward(*part, None, expert)
            return (sums[0] + grad_up, sums[1] + grad_down), (share, grad_weight)

        zero = tuple(jnp.zeros(w.shape, jnp.float32) for w in expert)
        (grad_up, grad_down), (share, grad_weight) = lax.scan(
            step, zero, (pieces(grads), pieces(everyone), pieces(weight), pieces(mask)))
    grad_chance = lax.all_to_all(grad_weight.reshape(count, DEVICE_ROWS), "dp", split_axis=0, concat_axis=0, tiled=True)
    (mixed,) = reduce_all([share.reshape(spread.shape)], count, 1)
    return mixed, grad_chance.T, grad_up, grad_down


def front_backward(grad_out, grad_mixed, grad_chance, kept, place, weights):
    joint, result_output, router, gain_attention, gain_mixture = weights
    allowed, cosine, sine = place
    inverse_one, scaled_one, normed, query, key, value, attention, context, inverse_two, scaled_two, normed_two = kept
    rows = normed.shape[0]
    chance = router_chances(normed_two, router)
    grad_logit = (chance * (grad_chance - jnp.sum(grad_chance * chance, axis=-1, keepdims=True))).astype(jnp.bfloat16)
    grad_router = dot_rows(normed_two, grad_logit)
    grad_normed_two = grad_mixed + dot_columns(grad_logit, router)
    grad_gain_two = jnp.sum(grad_normed_two * scaled_two, axis=0)
    scaled_grad_two = grad_normed_two * gain_mixture
    grad_middle = grad_out + inverse_two * (scaled_grad_two - scaled_two * jnp.mean(scaled_grad_two * scaled_two, axis=-1, keepdims=True))
    branch = grad_middle.astype(jnp.bfloat16)
    grad_output = dot_rows(context, branch)
    grad_context = dot_columns(branch, result_output).astype(jnp.bfloat16).reshape(rows, KEY_VALUE_HEADS, GROUP, HEAD_SIZE)
    grad_attention = jnp.einsum("qhgd,khd->hgqk", grad_context, value, preferred_element_type=jnp.float32)
    grad_value = jnp.einsum("hgqk,qhgd->khd", attention.astype(jnp.bfloat16), grad_context, preferred_element_type=jnp.float32)
    grad_scores = (attention * (grad_attention - jnp.sum(grad_attention * attention, axis=-1, keepdims=True))).astype(jnp.bfloat16)
    grad_query = jnp.einsum("hgqk,khd->qhgd", grad_scores, key, preferred_element_type=jnp.float32).reshape(rows, QUERY_HEADS, HEAD_SIZE)
    grad_key = jnp.einsum("hgqk,qhgd->khd", grad_scores, query, preferred_element_type=jnp.float32)
    grad_query = rotary_embedding(grad_query * SCORE_SCALE, cosine, -sine)
    grad_key = rotary_embedding(grad_key * SCORE_SCALE, cosine, -sine)
    grad_projected = jnp.concatenate(
        [grad_query.reshape(rows, -1), grad_key.reshape(rows, -1), grad_value.reshape(rows, -1)], axis=-1).astype(jnp.bfloat16)
    grad_joint = dot_rows(normed, grad_projected)
    grad_normed = dot_columns(grad_projected, joint)
    grad_gain_one = jnp.sum(grad_normed * scaled_one, axis=0)
    scaled_grad_one = grad_normed * gain_attention
    grad_hidden = grad_middle + inverse_one * (scaled_grad_one - scaled_one * jnp.mean(scaled_grad_one * scaled_one, axis=-1, keepdims=True))
    return grad_hidden, (grad_joint, grad_output, grad_router, grad_gain_one, grad_gain_two)


def small_halves(rows, router, gains, codes):
    second = jnp.concatenate([gains, codes], axis=1)
    width = -(-max(router.shape[1], second.shape[1]) // 128) * 128
    pad = lambda v: jnp.pad(v, ((0, 0), (0, width - v.shape[1])))
    return pad(router), pad(second)


def body(tokens, cotangent, lengths, routes, combined_weight, output_weight, router_weight, attention_gain, mixture_gain,
         expert_gate_up, expert_down):
    count = lax.axis_size("dp")
    me, sec = lax.axis_index("dp"), lax.axis_index("section")
    layers = lax.axis_size("section")
    leading = sec == 0
    shard = combined_weight.shape[1]
    micro = lambda a, axis: lax.dynamic_index_in_dim(a, sec, axis, keepdims=False)

    gains = jnp.stack([attention_gain[0], mixture_gain[0]], axis=1)
    codes = routes[0].astype(jnp.bfloat16).reshape(-1)
    code_count = codes.shape[0]
    codes = jnp.pad(codes, (0, -code_count % shard)).reshape(shard, -1)
    small = small_halves(shard, router_weight[0], gains, codes)
    small_width = small[0].shape[1]
    halves = [
        (combined_weight[0, :, : combined_weight.shape[2] // 2], combined_weight[0, :, combined_weight.shape[2] // 2 :]),
        (output_weight[0, :, : output_weight.shape[2] // 2], output_weight[0, :, output_weight.shape[2] // 2 :]),
        small,
    ]
    widths = [h[0].shape[1] for h in halves]
    mine = jnp.concatenate([jnp.where(leading, a, b) for a, b in halves], axis=1)
    given = swapped(jnp.concatenate([jnp.where(leading, b, a) for a, b in halves], axis=1))
    packs = [jnp.where(leading, mine, given), jnp.where(leading, given, mine)]
    partner_expert = tuple(swapped(w[0, 0]) for w in (expert_gate_up, expert_down))
    experts = []
    for layer in range(layers):
        keep = sec == layer
        experts.append((jnp.where(keep, expert_gate_up[0, 0], partner_expert[0]), jnp.where(keep, expert_down[0, 0], partner_expert[1])))

    def layer_weights(layer):
        at, parts = 0, []
        for w in widths:
            parts.append(packs[layer][:, at : at + w])
            at += w
        joint, output, tail = gather_all(parts, count, 2, pair=True)
        joint = joint.reshape(MODEL_WIDTH, -1)
        output = output.reshape(MODEL_WIDTH, -1)
        tail = tail.reshape(MODEL_WIDTH, -1)
        second = tail[:, small_width:]
        weights = (joint, output, tail[:, : router_weight.shape[2]], second[:, 0].astype(jnp.float32), second[:, 1].astype(jnp.float32))
        code = second[:, 2 : 2 + codes.shape[1]].reshape(count, -1)[:, :code_count].reshape(count, -1, DEVICE_ROWS, TOPK)
        named = lax.dynamic_index_in_dim(code, sec, 1, keepdims=False).reshape(count * DEVICE_ROWS, TOPK)
        mask = jnp.any(named == me.astype(jnp.bfloat16), axis=-1, keepdims=True)
        return weights, mask

    segment, token_position = layout(micro(lengths[:, 0], 0))
    row_ids = jnp.arange(DEVICE_ROWS, dtype=jnp.int32)
    allowed = (row_ids[:, None] >= row_ids[None, :]) & (segment[:, None] == segment[None, :])
    place = (allowed,) + rotation(token_position)

    weights, masks, stores = [], [], []
    hidden = micro(tokens, 0)
    for layer in range(layers):
        got, mask = layer_weights(layer)
        weights.append(got)
        masks.append(mask)
        middle, normed_two, kept = front(hidden.astype(jnp.float32), place, got)
        mixed, kept_mixture = mixture_forward(normed_two, got[2], mask, experts[layer], count, me)
        hidden = (middle + mixed).astype(jnp.bfloat16)
        stores.append((kept, kept_mixture))
    last = hidden
    grad = micro(cotangent, 0)
    shares, expert_grads = [None] * layers, [None] * layers
    for layer in reversed(range(layers)):
        kept, kept_mixture = stores[layer]
        mixed, grad_chance, grad_up, grad_down = mixture_backward(grad, masks[layer], kept_mixture, experts[layer], count)
        expert_grads[layer] = (grad_up, grad_down)
        grad_hidden, parts = front_backward(grad.astype(jnp.float32), mixed, grad_chance, kept, place, weights[layer])
        grad = grad_hidden.astype(jnp.bfloat16)
        tail = small_halves(MODEL_WIDTH, parts[2], jnp.stack([parts[3], parts[4]], axis=1), parts[2][:, :0])
        packed = [parts[0], parts[1], jnp.concatenate(tail, axis=1)]
        packed = [a.astype(jnp.bfloat16).reshape(count, shard, -1) for a in packed]
        shares[layer] = reduce_all(packed, count, 3, pair=True)
    outs = []
    for a in range(3):
        kept_half = jnp.where(leading, shares[0][a], shares[1][a])
        got_half = swapped(jnp.where(leading, shares[1][a], shares[0][a]))
        outs.append(jnp.concatenate([jnp.where(leading, kept_half, got_half), jnp.where(leading, got_half, kept_half)], axis=1))
    expert_outs = []
    for a in range(2):
        kept_sum = jnp.where(leading, expert_grads[0][a], expert_grads[1][a])
        got_sum = swapped(jnp.where(leading, expert_grads[1][a], expert_grads[0][a]))
        expert_outs.append((kept_sum + got_sum)[None, None])
    partner = swapped(jnp.where(leading, last, grad))
    boundary = jnp.where(leading, jnp.stack([grad, partner]), jnp.stack([partner, last]))[None]
    half = outs[2].shape[1] // 2
    return (
        boundary,
        outs[0][None],
        outs[1][None],
        outs[2][None, :, : router_weight.shape[2]],
        outs[2][None, :, half],
        outs[2][None, :, half + 1],
        expert_outs[0],
        expert_outs[1],
    )


def solution(mesh):
    return jax.shard_map(
        body,
        mesh=mesh,
        in_specs=(
            P(None, "dp", None),
            P(None, "dp", None),
            P(None, "dp", None),
            P("section", None, "dp", None),
            P("section", "dp", None),
            P("section", "dp", None),
            P("section", "dp", None),
            P("section", "dp"),
            P("section", "dp"),
            P("section", "dp", None, None),
            P("section", "dp", None, None),
        ),
        out_specs=(
            P("section", None, "dp", None),
            P("section", "dp", None),
            P("section", "dp", None),
            P("section", "dp", None),
            P("section", "dp"),
            P("section", "dp"),
            P("section", "dp", None, None),
            P("section", "dp", None, None),
        ),
        check_vma=False,
    )
```

time: 2200 us -> 1130 us (0.51)
  Pallas kernels: 0 us -> 811 us
  blocking collectives: 710 us -> 0 us
  waiting for transfers between devices: 701 us -> 0.03 us
  local copies, waits for them, and re-layouts: 316 us -> 30.5 us
  other arithmetic: 131 us -> 53.1 us
  matrix products: 260 us -> 200 us
  starting transfers between devices: 53.7 us -> 17.1 us
    pallas_call x0 -> x12, Pallas kernels: none -> 811 us  [the longest x6 406 us: reduce_all(): pl.pallas_call(functools.partial(reduce_kernel, axes, pair, len(arrays)),...]
    all_to_all x7 -> x2, waiting for transfers between devices: 581 us -> 0.01 us  [mixture_backward(): lax.all_to_all(grad_weight.reshape(count, DEVICE_ROWS), 'dp', split_axis=...]
    all_to_all x6 -> x0, blocking collectives: 561 us -> none  [the longest x3 282 us: layer_forward(): lax.all_to_all(outgoing, 'dp', split_axis=0, concat_axis=0, tiled=True)]
    gather x15 -> x0, local copies, waits for them, and re-layouts: 155 us -> none  [the longest x3 34 us: layer_backward(): outgoing_grad = grad_padded[anchor].reshape(experts, capacity, MODEL_WIDTH)]
    all_gather x2 -> x0, waiting for transfers between devices: 119 us -> none  [the longest x1 64 us: body(): lax.all_gather(output_weight, 'dp', axis=1, tiled=True)]
    all_gather x1 -> x0, blocking collectives: 111 us -> none  [body(): lax.all_gather(router_weight, 'dp', axis=1, tiled=True)]
    reduce_sum x25 -> x6, other arithmetic: 55.5 us -> 1.12 us  [the longest x2 0.74 us: front_backward(): jnp.sum(grad_chance * chance, axis=-1, keepdims=True)]
    dot_general x66 -> x44, matrix products: 251 us -> 200 us  [the longest x10 70.4 us: dot_columns(): lax.dot_general(left, right, (((1,), (1,)), ((), ())), preferred_element_...]
  transfers between devices with their start and end apart: 13 -> 11, of which waited for: 8 -> 0; matrix products, arithmetic and copies ran while one was open for 11% -> 16% of each run, Pallas kernels for 0% -> 55%
where the time goes in v1:
time: 1130 us; the launch traced here: 1120 us
  Pallas kernels  811 us (72%)
  matrix products  200 us (18%)
  other arithmetic  53.1 us (5%)
  local copies, waits for them, and re-layouts  30.5 us (3%)
  starting transfers between devices  17.1 us (2%)
    pallas_call x6, Pallas kernels, reduce_all(): pl.pallas_call(functools.partial(reduce_kernel, axes, pair, len(arrays)),...  406 us
    pallas_call x6, Pallas kernels, gather_all(): pl.pallas_call(functools.partial(gather_kernel, axes, pair, len(arrays)),...  405 us
    dot_general x10, matrix products, dot_columns(): lax.dot_general(left, right, (((1,), (1,)), ((), ())), preferred_element_...  70.4 us
    dot_general x12, matrix products, dot(): return jnp.dot(left, right, preferred_element_type=jnp.float32)  61.3 us
    dot_general x10, matrix products, dot_rows(): lax.dot_general(left, right, (((0,), (0,)), ((), ())), preferred_element_...  53.7 us
  transfers between devices with their start and end apart: 11, of which 0 were waited for; matrix products, arithmetic and copies ran while one was open for 16% of the time, Pallas kernels for 55%

profile of v1, /device:TPU:28, one launch (start us, length us, event | category | flops | bytes accessed | tf_op | source)
XLA Modules:
  0.0 1115.5 jit_solution(645365994431486045)
XLA Ops:
  11.8 67.0 %spread.5 = bf16[16,128,1536]{2,1,0:T(8,128)(2,1)} custom-call(bf16[128,1536]{1,0:T(8,128)(2,1)} %dynamic-slice_bitcast_fusion.refs_0_), custom_call_target="tpu_custom_call" | custom-call | bytes 11796480 | tf_op jit(solution)/shard_map/spread/pallas_call | solution.py:204
  81.1 70.4 %spread_pair.2 = (bf16[16,96,2560]{2,1,0:T(8,128)(2,1)}, bf16[16,96,1536]{2,1,0:T(8,128)(2,1)}, bf16[16,96,256]{2,1,0:T(8,128)(2,1)}) custom-call(bf16[96,1280]{1,0:T(8,128)(2,1)} %slice.206.refs_0_, bf16[96,768]{1,0:T(8,128)(2,1)} %slice.207.refs_1_, bf16[96,128]{1,0:T(8,128)(2,1)} %slice.208.refs_2_), custom_call_target="tpu_custom_call" | custom-call | bytes 12533760 | tf_op jit(solution)/shard_map/spread_pair/pallas_call | solution.py:204
  160.7 73.5 %spread_pair.3 = (bf16[16,96,2560]{2,1,0:T(8,128)(2,1)}, bf16[16,96,1536]{2,1,0:T(8,128)(2,1)}, bf16[16,96,256]{2,1,0:T(8,128)(2,1)}) custom-call(bf16[96,1280]{1,0:T(8,128)(2,1)} %slice.223.refs_0_, bf16[96,768]{1,0:T(8,128)(2,1)} %slice.224.refs_1_, bf16[96,128]{1,0:T(8,128)(2,1)} %slice.225.refs_2_), custom_call_target="tpu_custom_call" | custom-call | bytes 12533760 | tf_op jit(solution)/shard_map/spread_pair/pallas_call | solution.py:204
  247.0 65.9 %spread.4 = bf16[16,128,1536]{2,1,0:T(8,128)(2,1)} custom-call(bf16[128,1536]{1,0:T(8,128)(2,1)} %multiply_convert_fusion.11.refs_0_), custom_call_target="tpu_custom_call" | custom-call | bytes 11796480 | tf_op jit(solution)/shard_map/spread/pallas_call | solution.py:204
  316.5 4.9 fusion.127
  323.2 7.4 fusion.16
  334.1 5.9 multiply_convert_fusion.1
  339.9 67.7 %fold.4 = f32[128,1536]{1,0:T(8,128)} custom-call(bf16[16,128,1536]{2,1,0:T(8,128)(2,1)} %bitcast.349), custom_call_target="tpu_custom_call" | custom-call | bytes 12582912 | tf_op jit(solution)/shard_map/fold/pallas_call | solution.py:371
  420.6 66.7 %spread.6 = bf16[16,128,1536]{2,1,0:T(8,128)(2,1)} custom-call(bf16[128,1536]{1,0:T(8,128)(2,1)} %multiply_convert_fusion.10.refs_0_), custom_call_target="tpu_custom_call" | custom-call | bytes 11796480 | tf_op jit(solution)/shard_map/spread/pallas_call | solution.py:204
  492.2 11.4 %fusion.17 = f32[2048,1024]{0,1:T(8,128)} fusion(bf16[2048,1536]{1,0:T(8,128)(2,1)S(1)} %bitcast.312, bf16[1536,1024]{1,0:T(8,128)(2,1)} %collective-permute-done.1, pred[]{:T(512)S(6)} %eq.68, bf16[1,1,1536,1024]{3,2,1,0:T(8,128)(2,1)} %param.20), kind=kOutput, calls=%fused_computation.65 | convolution fusion | flops 6444023808 | bytes 20971520 | tf_op jit(solution)/shard_map/dot_general | solution.py:410
  503.6 10.4 multiply_reduce_fusion.1
  514.8 7.0 all-to-all-start
  521.8 9.0 multiply_convert_fusion
  530.9 10.6 convolution_convert_fusion.3
  542.3 62.6 %fold.5 = f32[128,1536]{1,0:T(8,128)} custom-call(bf16[16,128,1536]{2,1,0:T(8,128)(2,1)} %bitcast.348), custom_call_target="tpu_custom_call" | custom-call | bytes 12582912 | tf_op jit(solution)/shard_map/fold/pallas_call | solution.py:371
  604.9 61.9 %fold.7 = f32[128,1536]{1,0:T(8,128)} custom-call(bf16[16,128,1536]{2,1,0:T(8,128)(2,1)} %bitcast.346), custom_call_target="tpu_custom_call" | custom-call | bytes 12582912 | tf_op jit(solution)/shard_map/fold/pallas_call | solution.py:371
  687.8 6.0 fusion.50
  693.8 5.5 convolution_convert_fusion
  700.4 61.7 %spread.7 = bf16[16,128,1536]{2,1,0:T(8,128)(2,1)} custom-call(bf16[128,1536]{1,0:T(8,128)(2,1)} %fusion.49.refs_0_), custom_call_target="tpu_custom_call" | custom-call | bytes 11796480 | tf_op jit(solution)/shard_map/spread/pallas_call | solution.py:204
  762.1 6.9 fusion.4
  770.7 5.8 broadcast_select_fusion.4
  776.6 12.9 %multiply_convert_fusion.5 = (bf16[2048,512]{0,1:T(8,128)(2,1)}, bf16[2048,512]{0,1:T(8,128)(2,1)}, f32[2048]{0:T(1024)S(1)}) fusion(f32[2048,1024]{0,1:T(8,128)} %copy-done.5, f32[2048]{0:T(1024)S(1)} %copy-done.77, f32[2048,512]{0,1:T(8,128)S(1)} %copy-done.17, bf16[2048,1536]{1,0:T(8,128)(2,1)} %bitcast.345, ...), kind=kOutput, calls=%fused_computation.15 | convolution fusion | flops 3238787072 | bytes 26230784 | tf_op jit(solution)/shard_map/dot_general | solution.py:418
  789.4 11.1 fusion.2
  800.6 11.5 %broadcast_select_fusion.1 = (f32[1536,1024]{1,0:T(8,128)}, f32[1536,1024]{1,0:T(8,128)}) fusion(f32[1536,1024]{1,0:T(8,128)} %fusion.2, pred[]{:T(512)S(6)} %eq.57, bf16[2048,1536]{1,0:T(8,128)(2,1)S(1)} %bitcast.315, bf16[2048,512]{0,1:T(8,128)(2,1)S(1)} %copy-done.93, bf16[2048,512]{0,1:T(8,128)(2,1)} %get-tuple-element.98), kind=kOutput, calls=%fused_computation.27 | convolution fusion | flops 6452412416 | bytes 29360128 | tf_op jit(solution)/shard_map/dot_general | solution.py:414
  814.7 6.5 all-to-all-start.1
  821.9 11.6 %convolution_convert_fusion.2 = bf16[2048,1536]{1,0:T(8,128)(2,1)} fusion(bf16[2048,512]{0,1:T(8,128)(2,1)} %get-tuple-element.94, bf16[2048,512]{0,1:T(8,128)(2,1)} %get-tuple-element.93, bf16[1536,1024]{1,0:T(8,128)(2,1)} %collective-permute-done.1, pred[]{:T(512)S(6)} %eq.57, bf16[1,1,1536,1024]{3,2,1,0:T(8,128)(2,1)} %param.20), kind=kOutput, calls=%fused_computation.4 | convolution fusion | flops 6455558144 | bytes 16777216 | tf_op jit(solution)/shard_map/dot_general | solution.py:418
  834.5 68.3 %fold.6 = f32[128,1536]{1,0:T(8,128)} custom-call(bf16[16,128,1536]{2,1,0:T(8,128)(2,1)} %bitcast.347), custom_call_target="tpu_custom_call" | custom-call | bytes 12582912 | tf_op jit(solution)/shard_map/fold/pallas_call | solution.py:371
  902.8 72.3 %fold_pair.3 = (f32[96,1280]{1,0:T(8,128)}, f32[96,768]{1,0:T(8,128)}, f32[96,128]{1,0:T(8,128)}) custom-call(bf16[16,96,2560]{2,1,0:T(8,128)(2,1)} %bitcast.303, bf16[16,96,1536]{2,1,0:T(8,128)(2,1)} %bitcast.317, bf16[16,96,256]{2,1,0:T(8,128)(2,1)} %pad_maximum_fusion.7.refs_2_), custom_call_target="tpu_custom_call" | custom-call | bytes 26738688 | tf_op jit(solution)/shard_map/fold_pair/pallas_call | solution.py:371
  993.5 6.9 fusion.40
  1009.3 5.4 convolution_convert_fusion.1
  1014.7 73.4 %fold_pair.2 = (f32[96,1280]{1,0:T(8,128)}, f32[96,768]{1,0:T(8,128)}, f32[96,128]{1,0:T(8,128)}) custom-call(bf16[16,96,2560]{2,1,0:T(8,128)(2,1)} %bitcast.316, bf16[16,96,1536]{2,1,0:T(8,128)(2,1)} %bitcast.318, bf16[16,96,256]{2,1,0:T(8,128)(2,1)} %pad_maximum_fusion.6.refs_2_), custom_call_target="tpu_custom_call" | custom-call | bytes 26738688 | tf_op jit(solution)/shard_map/fold_pair/pallas_call | solution.py:371
  1107.2 7.8 add_bitcast_fusion
  (401 shorter events, 136.5 us)
Async XLA Ops:
  6.4 72.6 %collective-permute-start = (bf16[96,2176]{1,0:T(8,128)(2,1)S(1)}, bf16[96,2176]{1,0:T(8,128)(2,1)S(1)}, u32[]{:S(2)}, u32[]{:S(2)}) collective-permute-start(bf16[96,2176]{1,0:T(8,128)(2,1)S(1)} %pad_maximum_fusion.11), channel_id=1, source_target_pairs={{0,16},{16,0},{1,17},{17,1},{2,18},{18,2},{3,19},{19,3},{4,20},{20... | collective-permute-start | bytes 1253384 | tf_op jit(solution)/shard_map/ppermute | solution.py:383
  6.4 316.7 %collective-permute-start.1 = (bf16[1536,1024]{1,0:T(8,128)(2,1)}, bf16[1536,1024]{1,0:T(8,128)(2,1)}, u32[]{:S(2)}, u32[]{:S(2)}) collective-permute-start(bf16[1536,1024]{1,0:T(8,128)(2,1)} %bitcast.411), channel_id=1, source_target_pairs={{0,16},{16,0},{1,17},{17,1},{2,18},{18,2},{3,19},{19,3},{4,20},{20... | collective-permute-start | bytes 9437192 | tf_op jit(solution)/shard_map/ppermute | solution.py:383
  6.9 327.1 %collective-permute-start.2 = (bf16[512,1536]{1,0:T(8,128)(2,1)}, bf16[512,1536]{1,0:T(8,128)(2,1)}, u32[]{:S(2)}, u32[]{:S(2)}) collective-permute-start(bf16[512,1536]{1,0:T(8,128)(2,1)} %bitcast.412), channel_id=1, source_target_pairs={{0,16},{16,0},{1,17},{17,1},{2,18},{18,2},{3,19},{19,3},{4,20},{20... | collective-permute-start | bytes 4718600 | tf_op jit(solution)/shard_map/ppermute | solution.py:383
  7.0 314.4 %copy-start.84 = (pred[16]{0:T(512)(128)(4,1)}, pred[16]{0:T(512)(128)(4,1)S(1)}, u32[]{:S(2)}) copy-start(pred[16]{0:T(512)(128)(4,1)S(1)} %iota_compare_fusion.4) | copy-start | bytes 52
  8.2 144.9 %copy-start.71 = (f32[128]{0:T(128)}, f32[128]{0:T(128)S(1)}, u32[]{:S(2)}) copy-start(f32[128]{0:T(128)S(1)} %add_rsqrt_fusion.3) | copy-start | bytes 1540
  9.9 228.9 %copy-start.69 = (pred[128,128]{0,1:T(8,128)(4,1)}, pred[128,128]{0,1:T(8,128)(4,1)S(1)}, u32[]{:S(2)}) copy-start(pred[128,128]{0,1:T(8,128)(4,1)S(1)} %fusion.89) | copy-start | bytes 49156
  11.8 141.3 %copy-start.14 = (bf16[2,128,1536]{2,1,0:T(8,128)(2,1)S(1)}, bf16[2,128,1536]{2,1,0:T(8,128)(2,1)}, u32[]{:S(2)}) copy-start(bf16[2,128,1536]{2,1,0:T(8,128)(2,1)} %param.11) | copy-start | bytes 2359300
  153.1 93.0 %copy-start.64 = (f32[1536]{0:T(1024)}, f32[1536]{0:T(1024)S(1)}, u32[]{:S(2)}) copy-start(f32[1536]{0:T(1024)S(1)} %get-tuple-element.80) | copy-start | bytes 18436
  242.7 70.2 %copy-start.24 = (bf16[8,64,3,128]{3,1,2,0:T(8,128)(2,1)}, bf16[8,64,3,128]{3,1,2,0:T(8,128)(2,1)S(1)}, u32[]{:S(2)}) copy-start(bf16[8,64,3,128]{3,1,2,0:T(8,128)(2,1)S(1)} %convolution_convert_fusion.11) | copy-start | bytes 1179652
  246.1 161.6 %copy-start.1 = (f32[128,1536]{1,0:T(8,128)}, f32[128,1536]{1,0:T(8,128)S(1)}, u32[]{:S(2)}) copy-start(f32[128,1536]{1,0:T(8,128)S(1)} %get-tuple-element.132) | copy-start | bytes 2359300
  246.1 66.8 %copy-start.29 = (bf16[1536,22]{1,0:T(8,128)(2,1)S(1)}, bf16[1536,22]{1,0:T(8,128)(2,1)}, u32[]{:S(2)}) copy-start(bf16[1536,22]{1,0:T(8,128)(2,1)} %slice.220) | copy-start | bytes 202756
  247.0 66.7 %copy-start.30 = (bf16[1536,22]{1,0:T(8,128)(2,1)S(1)}, bf16[1536,22]{1,0:T(8,128)(2,1)}, u32[]{:S(2)}) copy-start(bf16[1536,22]{1,0:T(8,128)(2,1)} %slice.234) | copy-start | bytes 202756
  247.0 68.0 %copy-start.28 = (bf16[1536,1]{1,0:T(8,128)(2,1)S(1)}, bf16[1536,1]{1,0:T(8,128)(2,1)}, u32[]{:S(2)}) copy-start(bf16[1536,1]{1,0:T(8,128)(2,1)} %slice.236) | copy-start | bytes 9220
  419.6 67.7 %copy-start.9 = (bf16[16,96,256]{2,1,0:T(8,128)(2,1)S(1)}, bf16[16,96,256]{2,1,0:T(8,128)(2,1)}, u32[]{:S(2)}) copy-start(bf16[16,96,256]{2,1,0:T(8,128)(2,1)} %get-tuple-element.23) | copy-start | bytes 2359300
  419.6 67.7 %copy-start.82 = (f32[128]{0:T(128)}, f32[128]{0:T(128)S(1)}, u32[]{:S(2)}) copy-start(f32[128]{0:T(128)S(1)} %add_rsqrt_fusion) | copy-start | bytes 1540
  514.8 151.9 %all-to-all-start = ((f32[16,1,128]{2,1,0:T(1,128)}), f32[16,1,128]{2,1,0:T(1,128)}, u32[]{:S(2)}, u32[]{:S(2)}) async-start(f32[16,1,128]{2,1,0:T(1,128)} %copy.169), calls=%async_computation | async-start | bytes 16384 | tf_op jit(solution)/shard_map/all_to_all | solution.py:516
  604.9 63.3 %copy-start.67 = (f32[1536]{0:T(1024)S(1)}, f32[1536]{0:T(1024)}, u32[]{:S(2)}) copy-start(f32[1536]{0:T(1024)} %convert_reduce_fusion.3) | copy-start | bytes 18436
  699.3 62.7 %copy-start.77 = (f32[2048]{0:T(1024)S(1)}, f32[2048]{0:T(1024)}, u32[]{:S(2)}) copy-start(f32[2048]{0:T(1024)} %copy-done.76) | copy-start | bytes 24580
  700.4 70.3 %slice-start.8 = ((s8[6291456]{0:T(1024)(128)(4,1)}), s8[2097152]{0:T(1024)(128)(4,1)S(1)}, s32[]{:S(2)}) async-start(s8[6291456]{0:T(1024)(128)(4,1)} %bitcast.341), calls=%async_computation.10 | async-start | bytes 4194304
  770.7 29.9 %slice-start.4 = ((s8[6291456]{0:T(1024)(128)(4,1)}), s8[4194304]{0:T(1024)(128)(4,1)S(1)}, s32[]{:S(2)}) async-start(s8[6291456]{0:T(1024)(128)(4,1)} %bitcast.313), calls=%async_computation.6 | async-start | bytes 8388608
  776.5 326.0 %collective-permute-start.8 = (f32[512,1536]{1,0:T(8,128)}, f32[512,1536]{1,0:T(8,128)}, u32[]{:S(2)}, u32[]{:S(2)}) collective-permute-start(f32[512,1536]{1,0:T(8,128)} %get-tuple-element.153), channel_id=1, source_target_pairs={{0,16},{16,0},{1,17},{17,1},{2,18},{18,2},{3,19},{19,3},{4,20},{20... | collective-permute-start | bytes 9437192 | tf_op jit(solution)/shard_map/ppermute | solution.py:383
  812.1 295.1 %collective-permute-start.7 = (f32[1536,1024]{1,0:T(8,128)}, f32[1536,1024]{1,0:T(8,128)}, u32[]{:S(2)}, u32[]{:S(2)}) collective-permute-start(f32[1536,1024]{1,0:T(8,128)} %get-tuple-element.151), channel_id=1, source_target_pairs={{0,16},{16,0},{1,17},{17,1},{2,18},{18,2},{3,19},{19,3},{4,20},{20... | collective-permute-start | bytes 18874376 | tf_op jit(solution)/shard_map/ppermute | solution.py:383
  814.7 160.5 %all-to-all-start.1 = ((f32[16,1,128]{2,1,0:T(1,128)}), f32[16,1,128]{2,1,0:T(1,128)S(1)}, u32[]{:S(2)}, u32[]{:S(2)}) async-start(f32[16,1,128]{2,1,0:T(1,128)} %copy.175), calls=%async_computation.1 | async-start | bytes 16384 | tf_op jit(solution)/shard_map/all_to_all | solution.py:516
  902.8 72.4 %copy-start.68 = (f32[128,16]{0,1:T(8,128)S(1)}, f32[128,16]{0,1:T(8,128)}, u32[]{:S(2)}) copy-start(f32[128,16]{0,1:T(8,128)} %get-tuple-element.146) | copy-start | bytes 24580
  902.8 72.4 %copy-start.83 = (f32[128]{0:T(128)S(1)}, f32[128]{0:T(128)}, u32[]{:S(2)}) copy-start(f32[128]{0:T(128)} %get-tuple-element.145) | copy-start | bytes 1540
  902.8 72.4 %copy-start.65 = (f32[1536]{0:T(1024)S(1)}, f32[1536]{0:T(1024)}, u32[]{:S(2)}) copy-start(f32[1536]{0:T(1024)} %copy-done.64) | copy-start | bytes 18436
  902.8 72.4 %copy-start.81 = (f32[128]{0:T(128)S(1)}, f32[128]{0:T(128)}, u32[]{:S(2)}) copy-start(f32[128]{0:T(128)} %copy-done.80) | copy-start | bytes 1540
  1014.7 73.5 %copy-start.58 = (f32[96,128]{1,0:T(8,128)S(1)}, f32[96,128]{1,0:T(8,128)}, u32[]{:S(2)}) copy-start(f32[96,128]{1,0:T(8,128)} %get-tuple-element.31) | copy-start | bytes 147460
  1088.2 7.6 collective-permute-start.6
  1090.5 6.7 collective-permute-start.5
  1092.4 7.9 collective-permute-start.4
  1095.8 3.5 collective-permute-start.3
  (86 other events, 542.3 us)

commit v2 on v1

--- a/solution.py
+++ b/solution.py
@@ -378,6 +378,423 @@
         cost_estimate=pl.CostEstimate(flops=0, bytes_accessed=2 * sent, transcendentals=0),
         name="fold" if not pair else "fold_pair",
     )(*arrays)
+
+
+ROWS = 128
+TILE = 256
+STRIP = 32
+
+
+class Spread:
+    def __init__(self, axes, pairs, send, recv):
+        self.send, self.recv = send, recv
+        self.streams = []
+        for own, full in pairs:
+            for h in range(2):
+                rows = pl.ds(h * (ROWS // 2), ROWS // 2)
+                self.streams.append((Place(axes, h), own.at[rows], lambda b, f=full, r=rows: f.at[b, r]))
+        self.ids = range(len(self.streams))
+        self.sizes = self.streams[0][0].sizes
+
+    def copy(self, s, offs):
+        place, own, out = self.streams[s]
+        hop, base = last_hop(offs)
+        block = place.source(base)
+        f = place.flat(offs)
+        return pltpu.make_async_remote_copy(
+            src_ref=out(block) if any(base) else own, dst_ref=out(block), send_sem=self.send.at[s, f], recv_sem=self.recv.at[s, f],
+            device_id={"dp": place.target(hop)}, device_id_type=pl.DeviceIdType.MESH)
+
+    def begin(self):
+        for k in range(1, self.sizes[0]):
+            for s in self.ids:
+                self.copy(s, (k, 0, 0)).start()
+
+    def first(self, k):
+        for s in self.ids:
+            if k:
+                self.copy(s, (k, 0, 0)).wait_recv()
+            for j in range(1, self.sizes[1]):
+                self.copy(s, (k, j, 0)).start()
+            for i in range(1, self.sizes[2]):
+                self.copy(s, (k, 0, i)).start()
+
+    def second(self, k):
+        for j in range(1, self.sizes[1]):
+            for s in self.ids:
+                self.copy(s, (k, j, 0)).wait_recv()
+                for i in range(1, self.sizes[2]):
+                    self.copy(s, (k, j, i)).start()
+
+    def third(self, k):
+        for j in range(self.sizes[1]):
+            for i in range(1, self.sizes[2]):
+                for s in self.ids:
+                    self.copy(s, (k, j, i)).wait_recv()
+
+    def end(self):
+        for s in self.ids:
+            for offs in offsets(self.sizes):
+                if any(offs):
+                    self.copy(s, offs).wait_send()
+
+
+def add_rows(sources, dest, rows, step=16):
+    def one(r, _):
+        at = pl.ds(pl.multiple_of(r * step, step), step)
+        total = sources[0][at].astype(jnp.float32)
+        for source in sources[1:]:
+            total = total + source[at].astype(jnp.float32)
+        dest[at] = total.astype(dest.dtype)
+        return 0
+
+    lax.fori_loop(0, rows // step, one, 0)
+
+
+class Fold:
+    def __init__(self, axes, triples, send, recv):
+        self.send, self.recv = send, recv
+        self.streams = []
+        for share, got, out in triples:
+            for h in range(2):
+                rows = pl.ds(h * (ROWS // 2), ROWS // 2)
+                self.streams.append((Place(axes, h), lambda b, a=share, r=rows: a.at[b, r], got.at[h], out.at[rows]))
+        self.ids = range(len(self.streams))
+        self.sizes = self.streams[0][0].sizes
+
+    def copy(self, s, offs):
+        place, share, got, _ = self.streams[s]
+        hop, _ = last_hop(offs)
+        f = place.flat(offs)
+        return pltpu.make_async_remote_copy(
+            src_ref=share(place.target(offs)), dst_ref=got.at[f], send_sem=self.send.at[s, f], recv_sem=self.recv.at[s, f],
+            device_id={"dp": place.target(hop)}, device_id_type=pl.DeviceIdType.MESH)
+
+    def first(self, k):
+        for j in reversed(range(self.sizes[1])):
+            for i in range(1, self.sizes[2]):
+                for s in self.ids:
+                    self.copy(s, (k, j, i)).start()
+
+    def second(self, k):
+        for j in range(1, self.sizes[1]):
+            for s in self.ids:
+                self.settle(s, (k, j, 0), [(k, j, i) for i in range(1, self.sizes[2])])
+                self.copy(s, (k, j, 0)).start()
+
+    def third(self, k):
+        for s in self.ids:
+            arrived = [(k, 0, i) for i in range(1, self.sizes[2])] + [(k, j, 0) for j in range(1, self.sizes[1])]
+            if k:
+                self.settle(s, (k, 0, 0), arrived)
+                self.copy(s, (k, 0, 0)).start()
+            else:
+                self.settle(s, (0, 0, 0), arrived + [(q, 0, 0) for q in range(1, self.sizes[0])], last=True)
+
+    def settle(self, s, offs, arrived, last=False):
+        place, share, got, out = self.streams[s]
+        for o in arrived:
+            self.copy(s, o).wait_recv()
+        own = share(place.target(offs))
+        add_rows([own] + [got.at[place.flat(o)] for o in arrived], out if last else own, ROWS // 2)
+
+    def end(self):
+        for s in self.ids:
+            for offs in offsets(self.sizes):
+                if any(offs):
+                    self.copy(s, offs).wait_send()
+
+
+def greet_all(axes):
+    place = Place(axes, 0)
+    barrier = pltpu.get_barrier_semaphore()
+    peers = [offs for offs in offsets(place.sizes) if any(offs)]
+    for offs in peers:
+        pl.semaphore_signal(barrier, inc=1, device_id={"dp": place.target(offs)}, device_id_type=pl.DeviceIdType.MESH)
+    pl.semaphore_wait(barrier, len(peers))
+
+
+def contract(left, right, dims):
+    return lax.dot_general(left, right, ((dims[:1], dims[1:]), ((), ())), preferred_element_type=jnp.float32)
+
+
+def mixture_kernel(mode, axes, count, layer, *refs):
+    fore, back = "f" in mode, "b" in mode
+    refs = list(refs)
+    take = lambda n: [refs.pop(0) for _ in range(n)]
+    mask_ref, router_ref, up_own, up_other, down_own, down_other = take(6)
+    x_in = take(1)[0]
+    g_in = take(1)[0] if back else None
+    mixed_out = take(1)[0] if fore else None
+    saved_out = take(1)[0] if mode == "f" else None
+    if back:
+        grad_out, chance_out, up_grad_out, down_grad_out = take(4)
+    up, down, xg, gates_at, weight_at, local = take(6)
+    ag_send, ag_recv, rs_send, rs_recv = take(4)
+    spread_pairs, fold_triples = [], []
+    if fore:
+        share_f, got_f, act_at = take(3)
+        spread_pairs.append((x_in, xg))
+        fold_triples.append((share_f, got_f, mixed_out))
+    if back:
+        gg, share_b, got_b, plain_at, ggu_at, actw_at, high_at, low_at, up_sum, down_sum, chance_row, chance_got, c_send, c_recv = take(14)
+        spread_pairs.append((g_in, gg))
+        fold_triples.append((share_b, got_b, grad_out))
+    me, sec = lax.axis_index("dp"), lax.axis_index("section")
+    n0, n1, n2 = [size for _, size in axes]
+    plane = n1 * n2
+    if back:
+        greet_all(axes)
+    else:
+        greet(axes, False)
+    spread = Spread(axes, spread_pairs, ag_send, ag_recv)
+    fold = Fold(axes, fold_triples, rs_send, rs_recv)
+    spread.begin()
+    spread.first(0)
+    loads = []
+
+    @pl.when(sec == layer)
+    def _():
+        pltpu.make_async_copy(up_own, up, local.at[0]).start()
+        pltpu.make_async_copy(down_own, down, local.at[1]).start()
+
+    @pl.when(sec != layer)
+    def _():
+        pltpu.make_async_copy(up_other, up, local.at[0]).start()
+        pltpu.make_async_copy(down_other, down, local.at[1]).start()
+
+    if not fore:
+        bring = pltpu.make_async_copy(x_in, xg, local.at[2])
+        bring.start()
+    else:
+        xg[me] = x_in[...]
+    if back:
+        gg[me] = g_in[...]
+
+        def clear(r, _):
+            up_sum[pl.ds(pl.multiple_of(r * 8, 8), 8)] = jnp.zeros((8, up_sum.shape[1]), jnp.float32)
+            return 0
+
+        lax.fori_loop(0, up_sum.shape[0] // 8, clear, 0)
+
+        def clear_down(r, _):
+            down_sum[pl.ds(pl.multiple_of(r * 8, 8), 8)] = jnp.zeros((8, down_sum.shape[1]), jnp.float32)
+            return 0
+
+        lax.fori_loop(0, down_sum.shape[0] // 8, clear_down, 0)
+    pltpu.make_async_copy(up_own, up, local.at[0]).wait()
+    pltpu.make_async_copy(down_own, down, local.at[1]).wait()
+    if not fore:
+        bring.wait()
+
+    def span(n, size=TILE):
+        return pl.ds(pl.multiple_of(n * size, size), size)
+
+    def tile(b0):
+        blocks = pl.ds(b0, TILE // ROWS)
+        x = xg[blocks].reshape(TILE, MODEL_WIDTH)
+        lane = lax.broadcasted_iota(jnp.int32, (TILE, router_ref.shape[1]), 1)
+        chance = jnp.where(lane < count, jnp.exp(dot(x, router_ref[...])), 0.0)
+        total = jnp.sum(chance, axis=1, keepdims=True)
+        named = mask_ref[blocks].reshape(TILE, 1)
+        weight = jnp.sum(jnp.where(lane == me, chance, 0.0), axis=1, keepdims=True) / total * named
+        weight_at[...] = jnp.where(lane[:, :128] == 0, weight, named)
+
+        def gate_step(n, _):
+            gates_at[:, span(n)] = dot(xg[blocks].reshape(TILE, MODEL_WIDTH), up[:, span(n)])
+            return 0
+
+        lax.fori_loop(0, 2 * FFE // TILE, gate_step, 0)
+        if back:
+            def plain_step(n, _):
+                plain_at[:, span(n)] = contract(gg[blocks].reshape(TILE, MODEL_WIDTH), down[span(n), :], (1, 1))
+                return 0
+
+            lax.fori_loop(0, FFE // TILE, plain_step, 0)
+
+        def strip(r, _):
+            at = pl.ds(pl.multiple_of(r * STRIP, STRIP), STRIP)
+            gate, raise_ = gates_at[at, :FFE], gates_at[at, FFE:]
+            sigmoid = 1.0 / (1.0 + jnp.exp(-gate))
+            silu = gate * sigmoid
+            activated = silu * raise_
+            if fore:
+                act_at[at] = activated.astype(jnp.bfloat16)
+            if back:
+                w, m = weight_at[at, 0:1], weight_at[at, 1:2]
+                plain = plain_at[at]
+                grad_act = plain * w
+                ggu_at[at, :FFE] = (grad_act * raise_ * sigmoid * (1.0 + gate * (1.0 - sigmoid))).astype(jnp.bfloat16)
+                ggu_at[at, FFE:] = (grad_act * silu).astype(jnp.bfloat16)
+                actw_at[at] = (activated * w).astype(jnp.bfloat16)
+                product = activated * plain * m
+                high = product.astype(jnp.bfloat16)
+                high_at[at] = high
+                low_at[at] = (product - high.astype(jnp.float32)).astype(jnp.bfloat16)
+            return 0
+
+        lax.fori_loop(0, TILE // STRIP, strip, 0)
+        if fore:
+            def share_step(n, _):
+                part = dot(act_at[...], down[:, span(n)]) * weight_at[:, 0:1]
+                share_f[blocks, :, span(n)] = part.astype(jnp.bfloat16).reshape(TILE // ROWS, ROWS, TILE)
+                return 0
+
+            lax.fori_loop(0, MODEL_WIDTH // TILE, share_step, 0)
+        if back:
+            ones = jnp.ones((8, FFE), jnp.bfloat16)
+            row = contract(ones, high_at[...], (1, 1)) + contract(ones, low_at[...], (1, 1))
+            for b in range(TILE // ROWS):
+                chance_row[b0 + b] = row[:, b * ROWS : (b + 1) * ROWS]
+
+            def back_step(n, _):
+                part = contract(ggu_at[...], up[span(n), :], (1, 1))
+                share_b[blocks, :, span(n)] = part.astype(jnp.bfloat16).reshape(TILE // ROWS, ROWS, TILE)
+                return 0
+
+            lax.fori_loop(0, MODEL_WIDTH // TILE, back_step, 0)
+
+            def up_step(n, _):
+                left = xg[blocks, :, span(n)].reshape(TILE, TILE)
+                up_sum[span(n), :] += contract(left, ggu_at[...], (0, 0))
+                return 0
+
+            lax.fori_loop(0, MODEL_WIDTH // TILE, up_step, 0)
+
+            def down_step(n, _):
+                down_sum[span(n), :] += contract(actw_at[:, span(n)], gg[blocks].reshape(TILE, MODEL_WIDTH), (0, 0))
+                return 0
+
+            lax.fori_loop(0, FFE // TILE, down_step, 0)
+
+    long_stride = axes[0][0]
+    digit = lax.div(me, long_stride)
+
+    def chunk(c, _):
+        k = lax.rem(c + 1, n0)
+
+        @pl.when(c == 0)
+        def _():
+            spread.first(1)
+            spread.second(0)
+            for t in range(2, n0):
+                spread.first(t)
+                spread.second(t - 1)
+                spread.third(t - 2)
+
+        @pl.when(c == 1)
+        def _():
+            spread.second(n0 - 1)
+            spread.third(n0 - 2)
+
+        @pl.when(c == 2)
+        def _():
+            spread.third(n0 - 1)
+
+        source = lax.rem(digit - k + n0, n0)
+
+        def step(q, _):
+            tile(source * plane + q * (TILE // ROWS))
+            return 0
+
+        lax.fori_loop(0, plane * ROWS // TILE, step, 0)
+        order = [(n0 - (v + 1)) % n0 for v in range(n0)]
+        for v in range(n0):
+            @pl.when(c == v)
+            def _(v=v):
+                fold.first(order[v])
+                if v >= 1:
+                    fold.second(order[v - 1])
+                if v >= 2:
+                    fold.third(order[v - 2])
+        return 0
+
+    assert n0 == 4
+    lax.fori_loop(0, n0, chunk, 0)
+    order = [(n0 - (v + 1)) % n0 for v in range(n0)]
+    if back:
+        place = Place(axes, 0)
+
+        def chance_copy(offs):
+            f = place.flat(offs)
+            return pltpu.make_async_remote_copy(
+                src_ref=chance_row.at[place.target(offs)], dst_ref=chance_got.at[me], send_sem=c_send.at[f], recv_sem=c_recv.at[f],
+                device_id={"dp": place.target(offs)}, device_id_type=pl.DeviceIdType.MESH)
+
+        others = [offs for offs in offsets((n0, n1, n2)) if any(offs)]
+        for offs in others:
+            chance_copy(offs).start()
+        chance_got[me] = chance_row[me]
+        outs = [pltpu.make_async_copy(up_sum, up_grad_out, local.at[0]), pltpu.make_async_copy(down_sum, down_grad_out, local.at[1])]
+        for c in outs:
+            c.start()
+    if saved_out is not None:
+        save = pltpu.make_async_copy(xg, saved_out, local.at[2])
+        save.start()
+    fold.second(order[n0 - 1])
+    fold.third(order[n0 - 2])
+    fold.third(order[n0 - 1])
+    spread.end()
+    fold.end()
+    if back:
+        for offs in others:
+            chance_copy(offs).wait()
+        chance_out[...] = chance_got[...]
+        for c in outs:
+            c.wait()
+    if saved_out is not None:
+        save.wait()
+
+
+def mixture_call(mode, count, layer, cid, mask, router, expert, partner, x, g=None):
+    axes = torus_axes(count)
+    fore, back = "f" in mode, "b" in mode
+    vmem, anywhere = pl.BlockSpec(memory_space=pltpu.VMEM), pl.BlockSpec(memory_space=pl.ANY)
+    args = [mask, router, expert[0], partner[0], expert[1], partner[1], x]
+    in_specs = [vmem, vmem] + [anywhere] * 4 + [vmem if fore else anywhere]
+    if back:
+        args.append(g)
+        in_specs.append(vmem)
+    whole = (count, ROWS, MODEL_WIDTH)
+    out_shape, out_specs = [], []
+    block = jax.ShapeDtypeStruct((ROWS, MODEL_WIDTH), jnp.float32)
+    if fore:
+        out_shape.append(block)
+        out_specs.append(vmem)
+    if mode == "f":
+        out_shape.append(jax.ShapeDtypeStruct(whole, jnp.bfloat16))
+        out_specs.append(anywhere)
+    if back:
+        out_shape += [block, jax.ShapeDtypeStruct((count, 8, ROWS), jnp.float32)]
+        out_shape += [jax.ShapeDtypeStruct(w.shape, jnp.float32) for w in expert]
+        out_specs += [vmem, vmem, anywhere, anywhere]
+    streams = 2 * (fore + back)
+    dma = pltpu.SemaphoreType.DMA
+    scratch = [pltpu.VMEM(expert[0].shape, jnp.bfloat16), pltpu.VMEM(expert[1].shape, jnp.bfloat16), pltpu.VMEM(whole, jnp.bfloat16),
+               pltpu.VMEM((TILE, 2 * FFE), jnp.float32), pltpu.VMEM((TILE, 128), jnp.float32), dma((3,))]
+    ag = streams if mode != "b" else 2
+    scratch += [dma((ag, count)), dma((ag, count)), dma((streams, count)), dma((streams, count))]
+    half = pltpu.VMEM((2, count, ROWS // 2, MODEL_WIDTH), jnp.bfloat16)
+    low = lambda width: pltpu.VMEM((TILE, width), jnp.bfloat16)
+    if fore:
+        scratch += [pltpu.VMEM(whole, jnp.bfloat16), half, low(FFE)]
+    if back:
+        scratch += [pltpu.VMEM(whole, jnp.bfloat16), pltpu.VMEM(whole, jnp.bfloat16), half, pltpu.VMEM((TILE, FFE), jnp.float32),
+                    low(2 * FFE), low(FFE), low(FFE), low(FFE), pltpu.VMEM(expert[0].shape, jnp.float32),
+                    pltpu.VMEM(expert[1].shape, jnp.float32), pltpu.VMEM((count, 8, ROWS), jnp.float32),
+                    pltpu.VMEM((count, 8, ROWS), jnp.float32), dma((count,)), dma((count,))]
+    rows = count * ROWS
+    flops = rows * 6 * MODEL_WIDTH * FFE * (fore + 2 * back + (mode == "b"))
+    return pl.pallas_call(
+        functools.partial(mixture_kernel, mode, axes, count, layer),
+        out_shape=out_shape,
+        in_specs=in_specs,
+        out_specs=out_specs,
+        scratch_shapes=scratch,
+        compiler_params=pltpu.CompilerParams(collective_id=cid, has_side_effects=True, vmem_limit_bytes=VMEM_BYTES),
+        cost_estimate=pl.CostEstimate(flops=flops, bytes_accessed=4 * rows * MODEL_WIDTH, transcendentals=rows * FFE),
+        name="mixture_" + mode,
+    )(*args)
 
 def swapped(value):
     return lax.ppermute(value, "section", [(0, 1), (1, 0)])
@@ -582,8 +999,10 @@
     given = swapped(jnp.concatenate([jnp.where(leading, b, a) for a, b in halves], axis=1))
     packs = [jnp.where(leading, mine, given), jnp.where(leading, given, mine)]
     partner_expert = tuple(swapped(w[0, 0]) for w in (expert_gate_up, expert_down))
-    experts = []
-    for layer in range(layers):
+    own_expert = (expert_gate_up[0, 0], expert_down[0, 0])
+    fused = count * DEVICE_ROWS <= CHUNK_ROWS
+    experts, routers = [], []
+    for layer in range(0 if fused else layers):
         keep = sec == layer
         experts.append((jnp.where(keep, expert_gate_up[0, 0], partner_expert[0]), jnp.where(keep, expert_down[0, 0], partner_expert[1])))
 
@@ -598,6 +1017,7 @@
         tail = tail.reshape(MODEL_WIDTH, -1)
         second = tail[:, small_width:]
         weights = (joint, output, tail[:, : router_weight.shape[2]], second[:, 0].astype(jnp.float32), second[:, 1].astype(jnp.float32))
+        routers.append(tail[:, :small_width])
         code = second[:, 2 : 2 + codes.shape[1]].reshape(count, -1)[:, :code_count].reshape(count, -1, DEVICE_ROWS, TOPK)
         named = lax.dynamic_index_in_dim(code, sec, 1, keepdims=False).reshape(count * DEVICE_ROWS, TOPK)
         mask = jnp.any(named == me.astype(jnp.bfloat16), axis=-1, keepdims=True)
@@ -615,7 +1035,16 @@
         weights.append(got)
         masks.append(mask)
         middle, normed_two, kept = front(hidden.astype(jnp.float32), place, got)
-        mixed, kept_mixture = mixture_forward(normed_two, got[2], mask, experts[layer], count, me)
+        if not fused:
+            mixed, kept_mixture = mixture_forward(normed_two, got[2], mask, experts[layer], count, me)
+        else:
+            named = mask.astype(jnp.float32).reshape(count, DEVICE_ROWS, 1)
+            call = lambda mode, cid, *data: mixture_call(mode, count, layer, cid, named, routers[layer], own_expert, partner_expert, *data)
+            if layer < layers - 1:
+                mixed, everyone = call("f", 4, normed_two)
+                kept_mixture = (named, everyone)
+            else:
+                mixed, *kept_mixture = call("fb", 5, normed_two, micro(cotangent, 0))
         hidden = (middle + mixed).astype(jnp.bfloat16)
         stores.append((kept, kept_mixture))
     last = hidden
@@ -623,7 +1052,14 @@
     shares, expert_grads = [None] * layers, [None] * layers
     for layer in reversed(range(layers)):
         kept, kept_mixture = stores[layer]
-        mixed, grad_chance, grad_up, grad_down = mixture_backward(grad, masks[layer], kept_mixture, experts[layer], count)
+        if not fused:
+            mixed, grad_chance, grad_up, grad_down = mixture_backward(grad, masks[layer], kept_mixture, experts[layer], count)
+        else:
+            if layer < layers - 1:
+                named, everyone = kept_mixture
+                kept_mixture = mixture_call("b", count, layer, 6, named, routers[layer], own_expert, partner_expert, everyone, grad)
+            mixed, rows, grad_up, grad_down = kept_mixture
+            grad_chance = rows[:, 0].T
         expert_grads[layer] = (grad_up, grad_down)
         grad_hidden, parts = front_backward(grad.astype(jnp.float32), mixed, grad_chance, kept, place, weights[layer])
         grad = grad_hidden.astype(jnp.bfloat16)

time: 1130 us -> 965 us (0.85)
  matrix products: 200 us -> 72.5 us
  Pallas kernels: 811 us -> 783 us
  starting transfers between devices: 17.1 us -> 3.2 us
    pallas_call x0 -> x3, Pallas kernels: none -> 486 us  [mixture_call(): pl.pallas_call(functools.partial(mixture_kernel, mode, axes, count, layer...]
    pallas_call x6 -> x2, Pallas kernels: 405 us -> 146 us  [gather_all(): pl.pallas_call(functools.partial(gather_kernel, axes, pair, len(arrays)),...]
    pallas_call x6 -> x2, Pallas kernels: 406 us -> 150 us  [reduce_all(): pl.pallas_call(functools.partial(reduce_kernel, axes, pair, len(arrays)),...]
    dot_general x10 -> x6, matrix products: 70.4 us -> 19.1 us  [dot_columns(): lax.dot_general(left, right, (((1,), (1,)), ((), ())), preferred_element_...]
    dot_general x12 -> x6, matrix products: 61.3 us -> 18.1 us  [dot(): return jnp.dot(left, right, preferred_element_type=jnp.float32)]
    dot_general x10 -> x6, matrix products: 53.7 us -> 19 us  [dot_rows(): lax.dot_general(left, right, (((0,), (0,)), ((), ())), preferred_element_...]
    all_to_all x2 -> x0, starting transfers between devices: 13.5 us -> none  [mixture_backward(): lax.all_to_all(grad_weight.reshape(count, DEVICE_ROWS), 'dp', split_axis=...]
  transfers between devices with their start and end apart: 11 -> 9, of which waited for: 0 -> 1; matrix products, arithmetic and copies ran while one was open for 16% -> 9% of each run, Pallas kernels for 55% -> 31%
where the time goes in v2:
time: 965 us; the launch traced here: 951 us
  Pallas kernels  783 us (81%)
  matrix products  72.5 us (8%)
  other arithmetic  51.6 us (5%)
  local copies, waits for them, and re-layouts  37.8 us (4%)
    pallas_call x3, Pallas kernels, mixture_call(): pl.pallas_call(functools.partial(mixture_kernel, mode, axes, count, layer...  486 us
    pallas_call x2, Pallas kernels, reduce_all(): pl.pallas_call(functools.partial(reduce_kernel, axes, pair, len(arrays)),...  150 us
    pallas_call x2, Pallas kernels, gather_all(): pl.pallas_call(functools.partial(gather_kernel, axes, pair, len(arrays)),...  146 us
  transfers between devices with their start and end apart: 9, of which 1 were waited for; matrix products, arithmetic and copies ran while one was open for 9% of the time, Pallas kernels for 31%

profile of v2, /device:TPU:28, one launch (start us, length us, event | category | flops | bytes accessed | tf_op | source)
XLA Modules:
  0.0 951.2 jit_solution(7019901836578151859)
XLA Ops:
  11.6 73.4 %spread_pair.2 = (bf16[16,96,2560]{2,1,0:T(8,128)(2,1)}, bf16[16,96,1536]{2,1,0:T(8,128)(2,1)}, bf16[16,96,256]{2,1,0:T(8,128)(2,1)}) custom-call(bf16[96,1280]{1,0:T(8,128)(2,1)} %slice.206.refs_0_, bf16[96,768]{1,0:T(8,128)(2,1)} %slice.207.refs_1_, bf16[96,128]{1,0:T(8,128)(2,1)} %slice.208.refs_2_), custom_call_target="tpu_custom_call" | custom-call | bytes 12533760 | tf_op jit(solution)/shard_map/spread_pair/pallas_call | solution.py:204
  84.9 2.1 convert_reduce_fusion.2
  87.1 4.5 fusion.45
  95.4 2.3 copy.159
  99.5 72.9 %spread_pair.3 = (bf16[16,96,2560]{2,1,0:T(8,128)(2,1)}, bf16[16,96,1536]{2,1,0:T(8,128)(2,1)}, bf16[16,96,256]{2,1,0:T(8,128)(2,1)}) custom-call(bf16[96,1280]{1,0:T(8,128)(2,1)} %slice.221.refs_0_, bf16[96,768]{1,0:T(8,128)(2,1)} %slice.222.refs_1_, bf16[96,128]{1,0:T(8,128)(2,1)} %slice.223.refs_2_), custom_call_target="tpu_custom_call" | custom-call | bytes 12533760 | tf_op jit(solution)/shard_map/spread_pair/pallas_call | solution.py:204
  189.2 2.3 convolution_convert_fusion.9
  191.5 3.4 multiply_reduce_fusion.5
  196.5 122.4 %mixture_f.1 = (f32[128,1536]{1,0:T(8,128)}, bf16[16,128,1536]{2,1,0:T(8,128)(2,1)}) custom-call(f32[16,128,1]{2,1,0:T(8,128)} %copy.163.refs_0_, bf16[1536,128]{1,0:T(8,128)(2,1)} %slice.219.refs_1_, bf16[1536,1024]{1,0:T(8,128)(2,1)} %bitcast.334, bf16[1536,1024]{1,0:T(8,128)(2,1)} %collective-permute-done.1.refs_3_, bf16[512,1536]{1,0:T(8,128)(2,1)} %bitcast.338, ...), custom_call_target="tpu_custom_call" | custom-call | flops 9663676416 | bytes 12582912 | tf_op jit(solution)/shard_map/mixture_f/pallas_call | solution.py:788
  320.3 4.6 fusion.71
  327.5 2.3 convolution_convert_fusion.8
  329.8 3.4 multiply_reduce_fusion.4
  335.4 227.2 %mixture_fb.1 = (f32[128,1536]{1,0:T(8,128)}, f32[128,1536]{1,0:T(8,128)}, f32[16,8,128]{2,1,0:T(8,128)}, f32[1536,1024]{1,0:T(8,128)}, f32[512,1536]{1,0:T(8,128)}) custom-call(f32[16,128,1]{2,1,0:T(8,128)} %copy.170.refs_0_, bf16[1536,128]{1,0:T(8,128)(2,1)} %slice.234.refs_1_, bf16[1536,1024]{1,0:T(8,128)(2,1)} %bitcast.335, ...), custom_call_target="tpu_custom_call" | custom-call | flops 28991029248 | bytes 12582912 | tf_op jit(solution)/shard_map/mixture_fb/pallas_call | solution.py:788
  565.0 2.3 multiply_reduce_fusion
  567.7 4.3 convolution_convert_fusion.5
  572.2 3.1 fusion.14
  581.1 3.4 fusion.38
  585.6 136.4 %mixture_b.1 = (f32[128,1536]{1,0:T(8,128)}, f32[16,8,128]{2,1,0:T(8,128)}, f32[1536,1024]{1,0:T(8,128)}, f32[512,1536]{1,0:T(8,128)}) custom-call(f32[16,128,1]{2,1,0:T(8,128)} %copy.163.refs_0_, bf16[1536,128]{1,0:T(8,128)(2,1)} %slice.219.refs_1_, bf16[1536,1024]{1,0:T(8,128)(2,1)} %bitcast.336, bf16[1536,1024]{1,0:T(8,128)(2,1)} %collective-permute-done.1.refs_3_, ...), custom_call_target="tpu_custom_call" | custom-call | flops 28991029248 | bytes 12582912 | tf_op jit(solution)/shard_map/mixture_b/pallas_call | solution.py:788
  724.4 1.9 multiply_reduce_fusion.1
  726.7 4.3 convolution_convert_fusion.4
  731.2 3.1 fusion.15
  740.7 2.9 fusion.28
  745.2 4.2 broadcast_select_fusion
  750.0 2.2 broadcast_select_fusion.1
  755.2 3.5 convolution_convert_fusion.2
  758.7 5.5 convolution_convert_fusion
  764.2 77.2 %fold_pair.3 = (f32[96,1280]{1,0:T(8,128)}, f32[96,768]{1,0:T(8,128)}, f32[96,128]{1,0:T(8,128)}) custom-call(bf16[16,96,2560]{2,1,0:T(8,128)(2,1)} %bitcast.245, bf16[16,96,1536]{2,1,0:T(8,128)(2,1)} %bitcast.247, bf16[16,96,256]{2,1,0:T(8,128)(2,1)} %pad_maximum_fusion.1.refs_2_), custom_call_target="tpu_custom_call" | custom-call | bytes 26738688 | tf_op jit(solution)/shard_map/fold_pair/pallas_call | solution.py:371
  842.9 3.5 convolution_convert_fusion.3
  846.5 5.5 convolution_convert_fusion.1
  852.0 73.1 %fold_pair.2 = (f32[96,1280]{1,0:T(8,128)}, f32[96,768]{1,0:T(8,128)}, f32[96,128]{1,0:T(8,128)}) custom-call(bf16[16,96,2560]{2,1,0:T(8,128)(2,1)} %bitcast.246, bf16[16,96,1536]{2,1,0:T(8,128)(2,1)} %bitcast.248, bf16[16,96,256]{2,1,0:T(8,128)(2,1)} %pad_maximum_fusion.refs_2_), custom_call_target="tpu_custom_call" | custom-call | bytes 26738688 | tf_op jit(solution)/shard_map/fold_pair/pallas_call | solution.py:371
  931.3 2.3 maximum_select_fusion
  935.9 5.3 add_bitcast_fusion.1
  941.2 9.6 %add_bitcast_fusion = f32[1,1,1536,1024]{3,2,1,0:T(8,128)} fusion(f32[1536,1024]{1,0:T(8,128)} %collective-permute-done.7, f32[1536,1024]{1,0:T(8,128)} %get-tuple-element.50, f32[1536,1024]{1,0:T(8,128)S(1)} %bitcast.252, pred[]{:T(512)S(6)} %eq.41), kind=kLoop, calls=%fused_computation.4 | loop fusion | flops 3145728 | bytes 25165824 | tf_op jit(solution)/shard_map/broadcast_in_dim | solution.py:1079
  (374 shorter events, 74.0 us)
Async XLA Ops:
  0.6 6.6 copy-start.16
  2.3 5.0 copy-start.94
  2.5 6.1 copy-start.46
  6.5 2.9 collective-permute-start
  6.6 189.9 %collective-permute-start.1 = (bf16[1536,1024]{1,0:T(8,128)(2,1)}, bf16[1536,1024]{1,0:T(8,128)(2,1)}, u32[]{:S(2)}, u32[]{:S(2)}) collective-permute-start(bf16[1536,1024]{1,0:T(8,128)(2,1)} %bitcast.333), channel_id=1, source_target_pairs={{0,16},{16,0},{1,17},{17,1},{2,18},{18,2},{3,19},{19,3},{4,20},{20... | collective-permute-start | bytes 9437192 | tf_op jit(solution)/shard_map/ppermute | solution.py:800
  7.1 189.4 %collective-permute-start.2 = (bf16[512,1536]{1,0:T(8,128)(2,1)}, bf16[512,1536]{1,0:T(8,128)(2,1)}, u32[]{:S(2)}, u32[]{:S(2)}) collective-permute-start(bf16[512,1536]{1,0:T(8,128)(2,1)} %bitcast.337), channel_id=1, source_target_pairs={{0,16},{16,0},{1,17},{17,1},{2,18},{18,2},{3,19},{19,3},{4,20},{20... | collective-permute-start | bytes 4718600 | tf_op jit(solution)/shard_map/ppermute | solution.py:800
  8.6 78.5 %copy-start.83 = (f32[128]{0:T(128)}, f32[128]{0:T(128)S(1)}, u32[]{:S(2)}) copy-start(f32[128]{0:T(128)S(1)} %add_rsqrt_fusion.3) | copy-start | bytes 1540
  177.2 5.0 copy-start.81
  186.4 5.0 copy-start.49
  194.9 124.0 %copy-start = (f32[128,1536]{1,0:T(8,128)}, f32[128,1536]{1,0:T(8,128)S(1)}, u32[]{:S(2)}) copy-start(f32[128,1536]{1,0:T(8,128)S(1)} %get-tuple-element.147) | copy-start | bytes 2359300
  320.2 9.5 %copy-start.2 = (bf16[128,1536]{1,0:T(8,128)(2,1)}, bf16[128,1536]{1,0:T(8,128)(2,1)S(1)}, u32[]{:S(2)}) copy-start(bf16[128,1536]{1,0:T(8,128)(2,1)S(1)} %get-tuple-element.114) | copy-start | bytes 1179652
  329.8 4.8 copy-start.15
  562.7 4.7 copy-start.23
  562.7 4.7 copy-start.47
  567.7 16.8 %copy-start.9 = (f32[128,1536]{1,0:T(8,128)}, f32[128,1536]{1,0:T(8,128)S(1)}, u32[]{:S(2)}) copy-start(f32[128,1536]{1,0:T(8,128)S(1)} %multiply_add_fusion.1) | copy-start | bytes 2359300
  585.6 137.4 %copy-start.75 = (f32[128,16]{0,1:T(8,128)S(1)}, f32[128,16]{0,1:T(8,128)}, u32[]{:S(2)}) copy-start(f32[128,16]{0,1:T(8,128)} %get-tuple-element.157) | copy-start | bytes 24580
  585.6 138.8 %copy-start.71 = (f32[1536]{0:T(1024)S(1)}, f32[1536]{0:T(1024)}, u32[]{:S(2)}) copy-start(f32[1536]{0:T(1024)} %get-tuple-element.104) | copy-start | bytes 18436
  726.7 16.9 %copy-start.11 = (f32[128,1536]{1,0:T(8,128)}, f32[128,1536]{1,0:T(8,128)S(1)}, u32[]{:S(2)}) copy-start(f32[128,1536]{1,0:T(8,128)S(1)} %multiply_add_fusion) | copy-start | bytes 2359300
  735.7 4.9 slice-start.6
  739.6 5.5 slice-start.4
  745.1 186.2 %collective-permute-start.3 = (bf16[128,1536]{1,0:T(8,128)(2,1)}, bf16[128,1536]{1,0:T(8,128)(2,1)}, u32[]{:S(2)}, u32[]{:S(2)}) collective-permute-start(bf16[128,1536]{1,0:T(8,128)(2,1)} %get-tuple-element.110), channel_id=1, source_target_pairs={{0,16},{16,0},{1,17},{17,1},{2,18},{18,2},{3,19},{19,3},{4,20},{20... | collective-permute-start | bytes 1179656 | tf_op jit(solution)/shard_map/ppermute | solution.py:800
  745.2 4.8 copy-start.5
  745.2 4.8 copy-start.7
  749.5 191.7 %collective-permute-start.7 = (f32[1536,1024]{1,0:T(8,128)}, f32[1536,1024]{1,0:T(8,128)}, u32[]{:S(2)}, u32[]{:S(2)}) collective-permute-start(f32[1536,1024]{1,0:T(8,128)} %broadcast_select_fusion), channel_id=1, source_target_pairs={{0,16},{16,0},{1,17},{17,1},{2,18},{18,2},{3,19},{19,3},{4,20},{20... | collective-permute-start | bytes 18874376 | tf_op jit(solution)/shard_map/ppermute | solution.py:800
  754.1 180.7 %collective-permute-start.8 = (f32[512,1536]{1,0:T(8,128)}, f32[512,1536]{1,0:T(8,128)}, u32[]{:S(2)}, u32[]{:S(2)}) collective-permute-start(f32[512,1536]{1,0:T(8,128)} %broadcast_select_fusion.1), channel_id=1, source_target_pairs={{0,16},{16,0},{1,17},{17,1},{2,18},{18,2},{3,19},{19,3},{4,20},{20... | collective-permute-start | bytes 9437192 | tf_op jit(solution)/shard_map/ppermute | solution.py:800
  852.0 73.2 %copy-start.29 = (f32[96,1280]{1,0:T(8,128)S(1)}, f32[96,1280]{1,0:T(8,128)}, u32[]{:S(2)}) copy-start(f32[96,1280]{1,0:T(8,128)} %get-tuple-element.45) | copy-start | bytes 1474564
  852.0 74.9 %copy-start.66 = (f32[96,128]{1,0:T(8,128)S(1)}, f32[96,128]{1,0:T(8,128)}, u32[]{:S(2)}) copy-start(f32[96,128]{1,0:T(8,128)} %get-tuple-element.49) | copy-start | bytes 147460
  926.0 7.6 collective-permute-start.4
  926.8 1.8 collective-permute-start.6
  928.6 1.8 collective-permute-start.5
  933.6 7.6 slice-start.2
  934.8 6.4 slice-start.3
  (84 other events, 224.0 us)

commit v3 on v2

--- a/solution.py
+++ b/solution.py
@@ -381,62 +381,107 @@
 
 
 ROWS = 128
-TILE = 256
-STRIP = 32
+TILE = 512
+STRIP = 16
+SPAN = 512
+SKIP = set()
+PIECE = 256
+MESH = pl.DeviceIdType.MESH
+TOKEN_PARTS = (((0, 1, 2), 0, 64), ((0, 2, 1), 64, 64))
+
+
+class Route:
+    def __init__(self, axes, order):
+        self.axes, self.order = axes, order
+        self.sizes = [size for _, size in axes]
+        self.me = lax.axis_index("dp")
+        self.all = offsets(self.sizes)
+        self.others = [o for o in self.all if any(o)]
+
+    def moved(self, steps):
+        out = self.me
+        for (stride, size), step in zip(self.axes, steps):
+            if step % size:
+                digit = lax.rem(lax.div(self.me, stride), size)
+                out = out + (lax.rem(digit + (step % size), size) - digit) * stride
+        return out
+
+    def source(self, offs):
+        return self.moved([-o for o in offs])
+
+    def target(self, offs):
+        return self.moved(list(offs))
+
+    def flat(self, offs):
+        return (offs[0] * self.sizes[1] + offs[1]) * self.sizes[2] + offs[2]
+
+    def last_axis(self, offs):
+        for axis in reversed(self.order):
+            if offs[axis]:
+                return axis
+
+    def base(self, offs):
+        out = list(offs)
+        out[self.last_axis(offs)] = 0
+        return tuple(out)
+
+    def hop(self, offs):
+        axis = self.last_axis(offs)
+        out = [0, 0, 0]
+        out[axis] = offs[axis]
+        return tuple(out)
+
+    def children(self, offs):
+        return [o for o in self.others if self.base(o) == offs]
 
 
 class Spread:
-    def __init__(self, axes, pairs, send, recv):
-        self.send, self.recv = send, recv
-        self.streams = []
-        for own, full in pairs:
-            for h in range(2):
-                rows = pl.ds(h * (ROWS // 2), ROWS // 2)
-                self.streams.append((Place(axes, h), own.at[rows], lambda b, f=full, r=rows: f.at[b, r]))
-        self.ids = range(len(self.streams))
-        self.sizes = self.streams[0][0].sizes
+    def __init__(self, streams, send, recv, psend=None, precv=None):
+        self.streams, self.send, self.recv, self.psend, self.precv = streams, send, recv, psend, precv
+        self.ids = range(len(streams))
 
     def copy(self, s, offs):
-        place, own, out = self.streams[s]
-        hop, base = last_hop(offs)
-        block = place.source(base)
-        f = place.flat(offs)
+        route, own, out = self.streams[s]
+        base = route.base(offs)
+        block, f = route.source(base), route.flat(offs)
         return pltpu.make_async_remote_copy(
             src_ref=out(block) if any(base) else own, dst_ref=out(block), send_sem=self.send.at[s, f], recv_sem=self.recv.at[s, f],
-            device_id={"dp": place.target(hop)}, device_id_type=pl.DeviceIdType.MESH)
-
-    def begin(self):
-        for k in range(1, self.sizes[0]):
-            for s in self.ids:
-                self.copy(s, (k, 0, 0)).start()
-
-    def first(self, k):
+            device_id={"dp": route.target(route.hop(offs))}, device_id_type=MESH)
+
+    def share(self, s, offs):
+        route, own, out = self.streams[s]
+        block, f = route.source(offs), route.flat(offs)
+        return pltpu.make_async_remote_copy(
+            src_ref=out(block) if any(offs) else own, dst_ref=out(block), send_sem=self.psend.at[s, f], recv_sem=self.precv.at[s, f],
+            device_id={"section": 1 - lax.axis_index("section")}, device_id_type=MESH)
+
+    def step(self, t):
+        if "comm" in SKIP:
+            return
+        work = [(offs, s) for s in self.ids for offs in self.streams[s][0].all if offs[0] + (offs[1] > 0) + (offs[2] > 0) == t]
+        kids = {(offs, s): self.streams[s][0].children(offs) for offs, s in work}
+        if t == 0:
+            for child, s in sorted([(child, s) for offs, s in work for child in kids[offs, s]], key=lambda e: (e[0][0], e[0], e[1])):
+                self.copy(s, child).start()
+            kids = {e: [] for e in work}
+        for offs, s in sorted(work, key=lambda e: (not kids[e], -e[0][0], e[0], e[1])):
+            if any(offs):
+                self.copy(s, offs).wait_recv()
+            for child in kids[offs, s]:
+                self.copy(s, child).start()
+            if self.psend is not None:
+                self.share(s, offs).start()
+
+    def end(self):
+        if "comm" in SKIP:
+            return
         for s in self.ids:
-            if k:
-                self.copy(s, (k, 0, 0)).wait_recv()
-            for j in range(1, self.sizes[1]):
-                self.copy(s, (k, j, 0)).start()
-            for i in range(1, self.sizes[2]):
-                self.copy(s, (k, 0, i)).start()
-
-    def second(self, k):
-        for j in range(1, self.sizes[1]):
-            for s in self.ids:
-                self.copy(s, (k, j, 0)).wait_recv()
-                for i in range(1, self.sizes[2]):
-                    self.copy(s, (k, j, i)).start()
-
-    def third(self, k):
-        for j in range(self.sizes[1]):
-            for i in range(1, self.sizes[2]):
-                for s in self.ids:
-                    self.copy(s, (k, j, i)).wait_recv()
-
-    def end(self):
-        for s in self.ids:
-            for offs in offsets(self.sizes):
+            route = self.streams[s][0]
+            for offs in route.all:
                 if any(offs):
                     self.copy(s, offs).wait_send()
+                if self.psend is not None:
+                    self.share(s, offs).wait()
 
 
 def add_rows(sources, dest, rows, step=16):
@@ -452,106 +497,349 @@
 
 
 class Fold:
-    def __init__(self, axes, triples, send, recv):
-        self.send, self.recv = send, recv
-        self.streams = []
-        for share, got, out in triples:
-            for h in range(2):
-                rows = pl.ds(h * (ROWS // 2), ROWS // 2)
-                self.streams.append((Place(axes, h), lambda b, a=share, r=rows: a.at[b, r], got.at[h], out.at[rows]))
-        self.ids = range(len(self.streams))
-        self.sizes = self.streams[0][0].sizes
+    def __init__(self, streams, send, recv, chunks):
+        self.streams, self.send, self.recv = streams, send, recv
+        self.ids = range(len(streams))
+        self.turn = {k: c for c, k in enumerate(chunks)}
+
+    def when(self, route, offs):
+        return max([self.turn[offs[0]]] + [self.when(route, o) + 1 for o in route.children(offs)])
 
     def copy(self, s, offs):
-        place, share, got, _ = self.streams[s]
-        hop, _ = last_hop(offs)
-        f = place.flat(offs)
+        route, share, got, _, _ = self.streams[s]
+        f = route.flat(offs)
         return pltpu.make_async_remote_copy(
-            src_ref=share(place.target(offs)), dst_ref=got.at[f], send_sem=self.send.at[s, f], recv_sem=self.recv.at[s, f],
-            device_id={"dp": place.target(hop)}, device_id_type=pl.DeviceIdType.MESH)
-
-    def first(self, k):
-        for j in reversed(range(self.sizes[1])):
-            for i in range(1, self.sizes[2]):
-                for s in self.ids:
-                    self.copy(s, (k, j, i)).start()
-
-    def second(self, k):
-        for j in range(1, self.sizes[1]):
-            for s in self.ids:
-                self.settle(s, (k, j, 0), [(k, j, i) for i in range(1, self.sizes[2])])
-                self.copy(s, (k, j, 0)).start()
-
-    def third(self, k):
+            src_ref=share(offs), dst_ref=got(f), send_sem=self.send.at[s, f], recv_sem=self.recv.at[s, f],
+            device_id={"dp": route.target(route.hop(offs))}, device_id_type=MESH)
+
+    def step(self, t):
+        if "comm" in SKIP:
+            return
+        work = [(offs, s) for s in self.ids for offs in self.streams[s][0].all if self.when(self.streams[s][0], offs) == t]
+        kids = {(offs, s): self.streams[s][0].children(offs) for offs, s in work}
+        for offs, s in sorted(work, key=lambda e: (bool(kids[e]), not (e[0][1] or e[0][2]), [-o for o in e[0]], e[1])):
+            route, share, got, out, rows = self.streams[s]
+            for o in kids[offs, s]:
+                self.copy(s, o).wait_recv()
+            if kids[offs, s]:
+                own = share(offs)
+                add_rows([own] + [got(route.flat(o)) for o in kids[offs, s]], own if any(offs) else out, rows)
+            if any(offs):
+                self.copy(s, offs).start()
+
+    def steps(self):
+        return 1 + max(self.when(self.streams[s][0], (0, 0, 0)) for s in self.ids)
+
+    def end(self):
+        if "comm" in SKIP:
+            return
         for s in self.ids:
-            arrived = [(k, 0, i) for i in range(1, self.sizes[2])] + [(k, j, 0) for j in range(1, self.sizes[1])]
-            if k:
-                self.settle(s, (k, 0, 0), arrived)
-                self.copy(s, (k, 0, 0)).start()
-            else:
-                self.settle(s, (0, 0, 0), arrived + [(q, 0, 0) for q in range(1, self.sizes[0])], last=True)
-
-    def settle(self, s, offs, arrived, last=False):
-        place, share, got, out = self.streams[s]
-        for o in arrived:
-            self.copy(s, o).wait_recv()
-        own = share(place.target(offs))
-        add_rows([own] + [got.at[place.flat(o)] for o in arrived], out if last else own, ROWS // 2)
-
-    def end(self):
-        for s in self.ids:
-            for offs in offsets(self.sizes):
-                if any(offs):
-                    self.copy(s, offs).wait_send()
-
-
-def greet_all(axes):
-    place = Place(axes, 0)
+            for offs in self.streams[s][0].others:
+                self.copy(s, offs).wait_send()
+
+
+def meet(axes, everyone, pair):
+    route = Route(axes, (0, 1, 2))
     barrier = pltpu.get_barrier_semaphore()
-    peers = [offs for offs in offsets(place.sizes) if any(offs)]
+    peers = [o for o in route.others if everyone or sum(1 for v in o if v) == 1]
     for offs in peers:
-        pl.semaphore_signal(barrier, inc=1, device_id={"dp": place.target(offs)}, device_id_type=pl.DeviceIdType.MESH)
-    pl.semaphore_wait(barrier, len(peers))
+        pl.semaphore_signal(barrier, inc=1, device_id={"dp": route.target(offs)}, device_id_type=MESH)
+    if pair:
+        pl.semaphore_signal(barrier, inc=1, device_id={"section": 1 - lax.axis_index("section")}, device_id_type=MESH)
+    pl.semaphore_wait(barrier, len(peers) + (1 if pair else 0))
 
 
 def contract(left, right, dims):
     return lax.dot_general(left, right, ((dims[:1], dims[1:]), ((), ())), preferred_element_type=jnp.float32)
 
 
-def mixture_kernel(mode, axes, count, layer, *refs):
+def weight_parts(rows):
+    half = rows // 2
+    return (((0, 1, 2), 0, half), ((0, 2, 1), half, half))
+
+
+def weight_columns(half):
+    sec = lax.axis_index("section")
+    return pl.ds(pl.multiple_of(sec * half, 128), half), pl.ds(pl.multiple_of((1 - sec) * half, 128), half)
+
+
+def weight_streams(axes, ins, outs):
+    streams = []
+    for own, full in zip(ins, outs):
+        rows, half = own.shape
+        cols, _ = weight_columns(half)
+        for order, at, size in weight_parts(rows):
+            span = pl.ds(at, size)
+            streams.append((Route(axes, order), own.at[span], lambda b, o=full, r=span, c=cols: o.at[b, r, c]))
+    return streams
+
+
+def weight_stream_count(arrays):
+    return sum(len(weight_parts(a.shape[0])) for a in arrays)
+
+
+class WeightFold:
+    def __init__(self, axes, raws, sums, gots, loads, outs, sems, chunks):
+        self.send, self.recv, self.psend, self.precv, self.local = sems
+        self.arrays = list(zip(raws, sums, loads, outs))
+        self.chunks = chunks
+        streams = []
+        for raw, total, load, got, out in zip(raws, sums, loads, gots, outs):
+            for order, at, size in weight_parts(out.shape[0]):
+                rows, route = pl.ds(at, size), Route(axes, order)
+                streams.append((route, lambda o, t=total, r=rows, w=route: t.at[w.flat(o), r], lambda f, g=got, r=rows: g.at[f, r],
+                                out.at[rows], size))
+        self.route = Route(axes, (0, 1, 2))
+        self.fold = Fold(streams, self.send, self.recv, chunks)
+
+    def block(self, c):
+        return [o for o in self.route.all if o[0] == self.chunks[c]]
+
+    def give(self, a, offs):
+        raw, total, _, out = self.arrays[a]
+        f = self.route.flat(offs)
+        return pltpu.make_async_remote_copy(
+            src_ref=raw.at[self.route.target(offs), :, weight_columns(out.shape[1])[1]], dst_ref=total.at[f],
+            send_sem=self.psend.at[a, f], recv_sem=self.precv.at[a, f], device_id={"section": 1 - lax.axis_index("section")},
+            device_id_type=MESH)
+
+    def load(self, a, offs):
+        raw, _, load, out = self.arrays[a]
+        slot = offs[1] * self.route.sizes[2] + offs[2]
+        return pltpu.make_async_copy(raw.at[self.route.target(offs), :, weight_columns(out.shape[1])[0]], load.at[slot],
+                                     self.local.at[a, self.route.flat(offs)])
+
+    def begin(self):
+        for c in range(len(self.chunks)):
+            for offs in self.block(c):
+                for a in range(len(self.arrays)):
+                    self.give(a, offs).start()
+                    if c == 0:
+                        self.load(a, offs).start()
+
+    def step(self, t):
+        if t < len(self.chunks):
+            for a, (_, total, load, out) in enumerate(self.arrays):
+                for offs in self.block(t):
+                    self.load(a, offs).wait()
+                    self.give(a, offs).wait_recv()
+                    here = total.at[self.route.flat(offs)]
+                    add_rows([load.at[offs[1] * self.route.sizes[2] + offs[2]], here], here, out.shape[0])
+            if t + 1 < len(self.chunks):
+                for offs in self.block(t + 1):
+                    for a in range(len(self.arrays)):
+                        self.load(a, offs).start()
+        self.fold.step(t)
+
+    def steps(self):
+        return self.fold.steps()
+
+    def end(self):
+        self.fold.end()
+        for a in range(len(self.arrays)):
+            for offs in self.route.all:
+                self.give(a, offs).wait_send()
+
+
+def fold_scratch(arrays, axes):
+    count, dma = arrays[0].shape[0], pltpu.SemaphoreType.DMA
+    half = [(a.shape[1], a.shape[2] // 2) for a in arrays]
+    full = [pltpu.VMEM((count, *h), jnp.bfloat16) for h in half]
+    loads = [pltpu.VMEM((axes[1][1] * axes[2][1], *h), jnp.bfloat16) for h in half]
+    streams = sum(len(weight_parts(rows)) for rows, _ in half)
+    return full + full + loads + [dma((streams, count))] * 2 + [dma((len(arrays), count))] * 3
+
+
+def closing_kernel(axes, count, *refs):
+    refs = list(refs)
+    take = lambda n: [refs.pop(0) for _ in range(n)]
+    raws, others = take(count), take(count)
+    first_up, first_down, last_up, last_down, grad_in, last_in = take(6)
+    outs = take(count)
+    up_out, down_out, edge_out = take(3)
+    sums, gots, loads = take(count), take(count), take(count)
+    sems = take(5)
+    results, given, taken = take(count), take(count), take(count)
+    own_up, own_down, got_up, got_down, edge_give, edge_got, x_send, x_recv, x_local, h_send, h_recv = take(11)
+    sec = lax.axis_index("section")
+    partner = {"section": 1 - sec}
+    chunks = [axes[0][1] - 1 - c for c in range(axes[0][1])]
+    meet(axes, False, True)
+    fold = WeightFold(axes, raws, sums, gots, loads, results, sems, chunks)
+    fold.begin()
+    leading = sec == 0
+
+    def remote(src, dst, n):
+        return pltpu.make_async_remote_copy(src_ref=src, dst_ref=dst, send_sem=x_send.at[n], recv_sem=x_recv.at[n], device_id=partner,
+                                            device_id_type=MESH)
+
+    edge_give[...] = jnp.where(leading, last_in[...], grad_in[...])
+    edge = remote(edge_give, edge_got, 2)
+    edge.start()
+    edge_out[sec] = jnp.where(leading, grad_in[...], last_in[...])
+
+    @pl.when(leading)
+    def _():
+        remote(last_up, got_up, 0).start()
+        remote(last_down, got_down, 1).start()
+        pltpu.make_async_copy(first_up, own_up, x_local.at[0]).start()
+        pltpu.make_async_copy(first_down, own_down, x_local.at[1]).start()
+
+    @pl.when(jnp.logical_not(leading))
+    def _():
+        remote(first_up, got_up, 0).start()
+        remote(first_down, got_down, 1).start()
+        pltpu.make_async_copy(last_up, own_up, x_local.at[0]).start()
+        pltpu.make_async_copy(last_down, own_down, x_local.at[1]).start()
+
+    steps = fold.steps()
+    for t in range(steps - 1):
+        fold.step(t)
+        if t == 3:
+            for n, (own, got, out, src) in enumerate(((own_up, got_up, up_out, first_up), (own_down, got_down, down_out, first_down))):
+                pltpu.make_async_copy(src, own, x_local.at[n]).wait()
+                remote(src, got, n).wait_recv()
+                add_rows([own, got], own, own.shape[0], 8)
+                pltpu.make_async_copy(own, out, x_local.at[n]).start()
+            edge.wait_recv()
+            edge_out[1 - sec] = edge_got[...]
+    fold.step(steps - 1)
+    hands = []
+    for a in range(count):
+        half = results[a].shape[1]
+        mine, theirs = weight_columns(half)
+        given[a][...] = jnp.where(leading, others[a][...], results[a][...])
+        c = pltpu.make_async_remote_copy(src_ref=given[a], dst_ref=taken[a], send_sem=h_send.at[a], recv_sem=h_recv.at[a],
+                                         device_id=partner, device_id_type=MESH)
+        c.start()
+        hands.append(c)
+        outs[a][:, mine] = jnp.where(leading, results[a][...], others[a][...])
+    fold.end()
+    edge.wait_send()
+    for n, (own, got, out, src) in enumerate(((own_up, got_up, up_out, first_up), (own_down, got_down, down_out, first_down))):
+        remote(src, got, n).wait_send()
+        pltpu.make_async_copy(own, out, x_local.at[n]).wait()
+    for a in range(count):
+        hands[a].wait()
+        outs[a][:, weight_columns(results[a].shape[1])[1]] = taken[a][...]
+
+
+def closing(raws, others, first, last, grad, final, count, cid):
+    axes, n = torus_axes(count), len(raws)
+    vmem, anywhere = pl.BlockSpec(memory_space=pltpu.VMEM), pl.BlockSpec(memory_space=pl.ANY)
+    dma, f32 = pltpu.SemaphoreType.DMA, jnp.float32
+    halves = [pltpu.VMEM((a.shape[1], a.shape[2] // 2), f32) for a in raws]
+    experts = [pltpu.VMEM(w.shape, f32) for w in first]
+    block = pltpu.VMEM(grad.shape, grad.dtype)
+    return pl.pallas_call(
+        functools.partial(closing_kernel, axes, n),
+        out_shape=[jax.ShapeDtypeStruct(a.shape[1:], f32) for a in raws] + [jax.ShapeDtypeStruct(w.shape, f32) for w in first]
+        + [jax.ShapeDtypeStruct((2, *grad.shape), grad.dtype)],
+        in_specs=[anywhere] * n + [vmem] * n + [anywhere] * 4 + [vmem] * 2,
+        out_specs=[vmem] * n + [anywhere] * 2 + [vmem],
+        scratch_shapes=fold_scratch(raws, axes) + halves * 3 + experts * 2 + [block, block, dma((3,)), dma((3,)), dma((2,)), dma((n,)), dma((n,))],
+        compiler_params=pltpu.CompilerParams(collective_id=cid, has_side_effects=True, vmem_limit_bytes=VMEM_BYTES),
+        cost_estimate=pl.CostEstimate(flops=0, bytes_accessed=100_000_000, transcendentals=0),
+        name="closing",
+    )(*raws, *others, *first, *last, grad, final)
+
+
+def weight_spread_kernel(axes, count, *refs):
+    ins, outs = refs[:count], refs[count : 2 * count]
+    send, recv, psend, precv, local = refs[2 * count :]
+    meet(axes, False, True)
+    spread = Spread(weight_streams(axes, ins, outs), send, recv, psend, precv)
+    spread.step(0)
+    keep = own_copies(ins, outs, local)
+    for t in range(1, axes[0][1] + 2):
+        spread.step(t)
+    spread.end()
+    for c in keep:
+        c.wait()
+
+
+def own_copies(ins, outs, local):
+    keep = []
+    me, sec = lax.axis_index("dp"), lax.axis_index("section")
+    for a, (own, full) in enumerate(zip(ins, outs)):
+        half = own.shape[1]
+        c = pltpu.make_async_copy(own, full.at[me, :, pl.ds(pl.multiple_of(sec * half, 128), half)], local.at[a])
+        c.start()
+        keep.append(c)
+    return keep
+
+
+def weight_shapes(arrays, count):
+    return [jax.ShapeDtypeStruct((count, a.shape[0], 2 * a.shape[1]), a.dtype) for a in arrays]
+
+
+def weight_sems(arrays, count):
+    sem = pltpu.SemaphoreType.DMA((weight_stream_count(arrays), count))
+    return [sem] * 4 + [pltpu.SemaphoreType.DMA((len(arrays),))]
+
+
+def weight_spread(arrays, count, cid):
+    return pl.pallas_call(
+        functools.partial(weight_spread_kernel, torus_axes(count), len(arrays)),
+        out_shape=weight_shapes(arrays, count),
+        in_specs=[pl.BlockSpec(memory_space=pltpu.VMEM)] * len(arrays),
+        out_specs=[pl.BlockSpec(memory_space=pl.ANY)] * len(arrays),
+        scratch_shapes=weight_sems(arrays, count),
+        compiler_params=pltpu.CompilerParams(collective_id=cid, has_side_effects=True),
+        name="weight_spread",
+    )(*arrays)
+
+
+def mixture_kernel(mode, axes, count, layer, extra, folded, *refs):
     fore, back = "f" in mode, "b" in mode
     refs = list(refs)
     take = lambda n: [refs.pop(0) for _ in range(n)]
-    mask_ref, router_ref, up_own, up_other, down_own, down_other = take(6)
-    x_in = take(1)[0]
+    mask_ref, router_ref, up_own, up_other, down_own, down_other, x_in = take(7)
     g_in = take(1)[0] if back else None
+    next_in = take(extra)
+    raws = take(folded)
     mixed_out = take(1)[0] if fore else None
     saved_out = take(1)[0] if mode == "f" else None
     if back:
         grad_out, chance_out, up_grad_out, down_grad_out = take(4)
+    next_out = take(extra)
+    raw_outs = take(folded)
     up, down, xg, gates_at, weight_at, local = take(6)
     ag_send, ag_recv, rs_send, rs_recv = take(4)
-    spread_pairs, fold_triples = [], []
+    gathers, folds = [], []
     if fore:
         share_f, got_f, act_at = take(3)
-        spread_pairs.append((x_in, xg))
-        fold_triples.append((share_f, got_f, mixed_out))
+        gathers.append((x_in, xg))
+        folds.append((share_f, got_f, mixed_out))
     if back:
-        gg, share_b, got_b, plain_at, ggu_at, actw_at, high_at, low_at, up_sum, down_sum, chance_row, chance_got, c_send, c_recv = take(14)
-        spread_pairs.append((g_in, gg))
-        fold_triples.append((share_b, got_b, grad_out))
+        (gg, share_b, got_b, plain_at, ggu_at, actw_at, high_at, low_at, up_sum, down_sum, chance_row, chance_got, c_send, c_recv,
+         out_sem) = take(15)
+        gathers.append((g_in, gg))
+        folds.append((share_b, got_b, grad_out))
     me, sec = lax.axis_index("dp"), lax.axis_index("section")
     n0, n1, n2 = [size for _, size in axes]
     plane = n1 * n2
-    if back:
-        greet_all(axes)
-    else:
-        greet(axes, False)
-    spread = Spread(axes, spread_pairs, ag_send, ag_recv)
-    fold = Fold(axes, fold_triples, rs_send, rs_recv)
-    spread.begin()
-    spread.first(0)
-    loads = []
+    assert n0 == 4
+    meet(axes, back, bool(extra or folded))
+    spread_streams, fold_streams = [], []
+    for own, full in gathers:
+        for order, at, size in TOKEN_PARTS:
+            rows = pl.ds(at, size)
+            spread_streams.append((Route(axes, order), own.at[rows], lambda b, f=full, r=rows: f.at[b, r]))
+    for share, got, out in folds:
+        for order, at, size in TOKEN_PARTS:
+            rows, route = pl.ds(at, size), Route(axes, order)
+            fold_streams.append((route, lambda o, a=share, r=rows, w=route: a.at[w.target(o), r], lambda f, g=got, r=rows: g.at[f, r],
+                                 out.at[rows], size))
+    spread = Spread(spread_streams, ag_send, ag_recv)
+    fold = Fold(fold_streams, rs_send, rs_recv, [3, 2, 1, 0])
+    spread.step(0)
+    if extra:
+        w_send, w_recv, w_psend, w_precv, w_local = take(5)
+        other = Spread(weight_streams(axes, next_in, next_out), w_send, w_recv, w_psend, w_precv)
+    if folded:
+        aside = WeightFold(axes, raws, take(folded), take(folded), take(folded), raw_outs, take(5), [3, 2, 1, 0])
+        aside.begin()
 
     @pl.when(sec == layer)
     def _():
@@ -570,28 +858,17 @@
         xg[me] = x_in[...]
     if back:
         gg[me] = g_in[...]
-
-        def clear(r, _):
-            up_sum[pl.ds(pl.multiple_of(r * 8, 8), 8)] = jnp.zeros((8, up_sum.shape[1]), jnp.float32)
-            return 0
-
-        lax.fori_loop(0, up_sum.shape[0] // 8, clear, 0)
-
-        def clear_down(r, _):
-            down_sum[pl.ds(pl.multiple_of(r * 8, 8), 8)] = jnp.zeros((8, down_sum.shape[1]), jnp.float32)
-            return 0
-
-        lax.fori_loop(0, down_sum.shape[0] // 8, clear_down, 0)
     pltpu.make_async_copy(up_own, up, local.at[0]).wait()
     pltpu.make_async_copy(down_own, down, local.at[1]).wait()
     if not fore:
         bring.wait()
 
-    def span(n, size=TILE):
+    def span(n, size=SPAN):
         return pl.ds(pl.multiple_of(n * size, size), size)
 
     def tile(b0):
         blocks = pl.ds(b0, TILE // ROWS)
+        here = pl.ds(pl.multiple_of(b0 * ROWS, TILE), TILE)
         x = xg[blocks].reshape(TILE, MODEL_WIDTH)
         lane = lax.broadcasted_iota(jnp.int32, (TILE, router_ref.shape[1]), 1)
         chance = jnp.where(lane < count, jnp.exp(dot(x, router_ref[...])), 0.0)
@@ -604,13 +881,13 @@
             gates_at[:, span(n)] = dot(xg[blocks].reshape(TILE, MODEL_WIDTH), up[:, span(n)])
             return 0
 
-        lax.fori_loop(0, 2 * FFE // TILE, gate_step, 0)
+        lax.fori_loop(0, 2 * FFE // SPAN, gate_step, 0)
         if back:
             def plain_step(n, _):
                 plain_at[:, span(n)] = contract(gg[blocks].reshape(TILE, MODEL_WIDTH), down[span(n), :], (1, 1))
                 return 0
 
-            lax.fori_loop(0, FFE // TILE, plain_step, 0)
+            lax.fori_loop(0, FFE // SPAN, plain_step, 0)
 
         def strip(r, _):
             at = pl.ds(pl.multiple_of(r * STRIP, STRIP), STRIP)
@@ -621,12 +898,13 @@
             if fore:
                 act_at[at] = activated.astype(jnp.bfloat16)
             if back:
+                row = pl.ds(pl.multiple_of(b0 * ROWS + r * STRIP, STRIP), STRIP)
                 w, m = weight_at[at, 0:1], weight_at[at, 1:2]
                 plain = plain_at[at]
                 grad_act = plain * w
-                ggu_at[at, :FFE] = (grad_act * raise_ * sigmoid * (1.0 + gate * (1.0 - sigmoid))).astype(jnp.bfloat16)
-                ggu_at[at, FFE:] = (grad_act * silu).astype(jnp.bfloat16)
-                actw_at[at] = (activated * w).astype(jnp.bfloat16)
+                ggu_at[row, :FFE] = (grad_act * raise_ * sigmoid * (1.0 + gate * (1.0 - sigmoid))).astype(jnp.bfloat16)
+                ggu_at[row, FFE:] = (grad_act * silu).astype(jnp.bfloat16)
+                actw_at[row] = (activated * w).astype(jnp.bfloat16)
                 product = activated * plain * m
                 high = product.astype(jnp.bfloat16)
                 high_at[at] = high
@@ -634,119 +912,147 @@
             return 0
 
         lax.fori_loop(0, TILE // STRIP, strip, 0)
+        if back:
+            def back_step(n, _):
+                part = contract(ggu_at[here], up[span(n), :], (1, 1))
+                share_b[blocks, :, span(n)] = part.astype(jnp.bfloat16).reshape(TILE // ROWS, ROWS, SPAN)
+                return 0
+
+            lax.fori_loop(0, MODEL_WIDTH // SPAN, back_step, 0)
         if fore:
             def share_step(n, _):
                 part = dot(act_at[...], down[:, span(n)]) * weight_at[:, 0:1]
-                share_f[blocks, :, span(n)] = part.astype(jnp.bfloat16).reshape(TILE // ROWS, ROWS, TILE)
+                share_f[blocks, :, span(n)] = part.astype(jnp.bfloat16).reshape(TILE // ROWS, ROWS, SPAN)
                 return 0
 
-            lax.fori_loop(0, MODEL_WIDTH // TILE, share_step, 0)
+            lax.fori_loop(0, MODEL_WIDTH // SPAN, share_step, 0)
         if back:
             ones = jnp.ones((8, FFE), jnp.bfloat16)
             row = contract(ones, high_at[...], (1, 1)) + contract(ones, low_at[...], (1, 1))
             for b in range(TILE // ROWS):
                 chance_row[b0 + b] = row[:, b * ROWS : (b + 1) * ROWS]
 
-            def back_step(n, _):
-                part = contract(ggu_at[...], up[span(n), :], (1, 1))
-                share_b[blocks, :, span(n)] = part.astype(jnp.bfloat16).reshape(TILE // ROWS, ROWS, TILE)
-                return 0
-
-            lax.fori_loop(0, MODEL_WIDTH // TILE, back_step, 0)
-
-            def up_step(n, _):
-                left = xg[blocks, :, span(n)].reshape(TILE, TILE)
-                up_sum[span(n), :] += contract(left, ggu_at[...], (0, 0))
-                return 0
-
-            lax.fori_loop(0, MODEL_WIDTH // TILE, up_step, 0)
-
-            def down_step(n, _):
-                down_sum[span(n), :] += contract(actw_at[:, span(n)], gg[blocks].reshape(TILE, MODEL_WIDTH), (0, 0))
-                return 0
-
-            lax.fori_loop(0, FFE // TILE, down_step, 0)
-
-    long_stride = axes[0][0]
-    digit = lax.div(me, long_stride)
+    digit = lax.div(me, axes[0][0])
 
     def chunk(c, _):
         k = lax.rem(c + 1, n0)
 
         @pl.when(c == 0)
         def _():
-            spread.first(1)
-            spread.second(0)
-            for t in range(2, n0):
-                spread.first(t)
-                spread.second(t - 1)
-                spread.third(t - 2)
+            for t in range(1, 4):
+                spread.step(t)
+                if folded and t < 3:
+                    aside.step(t - 1)
 
         @pl.when(c == 1)
         def _():
-            spread.second(n0 - 1)
-            spread.third(n0 - 2)
+            spread.step(4)
+            if extra:
+                other.step(0)
+            if folded:
+                aside.step(2)
 
         @pl.when(c == 2)
         def _():
-            spread.third(n0 - 1)
+            spread.step(5)
+            if folded:
+                aside.step(3)
 
         source = lax.rem(digit - k + n0, n0)
 
         def step(q, _):
-            tile(source * plane + q * (TILE // ROWS))
+            if "tile" not in SKIP:
+                tile(source * plane + q * (TILE // ROWS))
             return 0
 
         lax.fori_loop(0, plane * ROWS // TILE, step, 0)
-        order = [(n0 - (v + 1)) % n0 for v in range(n0)]
         for v in range(n0):
             @pl.when(c == v)
             def _(v=v):
-                fold.first(order[v])
-                if v >= 1:
-                    fold.second(order[v - 1])
-                if v >= 2:
-                    fold.third(order[v - 2])
+                fold.step(v)
+                if extra and v >= 2:
+                    other.step(v - 1)
         return 0
 
-    assert n0 == 4
     lax.fori_loop(0, n0, chunk, 0)
-    order = [(n0 - (v + 1)) % n0 for v in range(n0)]
     if back:
-        place = Place(axes, 0)
+        route = Route(axes, (0, 1, 2))
 
         def chance_copy(offs):
-            f = place.flat(offs)
+            f = route.flat(offs)
             return pltpu.make_async_remote_copy(
-                src_ref=chance_row.at[place.target(offs)], dst_ref=chance_got.at[me], send_sem=c_send.at[f], recv_sem=c_recv.at[f],
-                device_id={"dp": place.target(offs)}, device_id_type=pl.DeviceIdType.MESH)
-
-        others = [offs for offs in offsets((n0, n1, n2)) if any(offs)]
-        for offs in others:
+                src_ref=chance_row.at[route.target(offs)], dst_ref=chance_got.at[me], send_sem=c_send.at[f], recv_sem=c_recv.at[f],
+                device_id={"dp": route.target(offs)}, device_id_type=MESH)
+
+        for offs in route.others:
             chance_copy(offs).start()
         chance_got[me] = chance_row[me]
-        outs = [pltpu.make_async_copy(up_sum, up_grad_out, local.at[0]), pltpu.make_async_copy(down_sum, down_grad_out, local.at[1])]
-        for c in outs:
-            c.start()
+
+        def up_piece(n):
+            return pltpu.make_async_copy(up_sum.at[n % 2], up_grad_out.at[pl.ds(n * PIECE, PIECE)], out_sem.at[0, n % 2])
+
+        def down_piece(n):
+            return pltpu.make_async_copy(down_sum.at[0], down_grad_out.at[pl.ds(n * PIECE, PIECE)], out_sem.at[1, 0])
+
+        ups, downs = MODEL_WIDTH // PIECE, FFE // PIECE
+
+        def gradient(n):
+            if n < ups:
+                if n >= 2:
+                    up_piece(n - 2).wait()
+                left = xg[:, :, n * PIECE : (n + 1) * PIECE].reshape(count * ROWS, PIECE)
+                up_sum[n % 2] = contract(left, ggu_at[...], (0, 0))
+                up_piece(n).start()
+            else:
+                n -= ups
+                if n:
+                    down_piece(n - 1).wait()
+                down_sum[0] = contract(actw_at[:, n * PIECE : (n + 1) * PIECE], gg[...].reshape(count * ROWS, MODEL_WIDTH), (0, 0))
+                down_piece(n).start()
+
+        work = list(range(ups + downs))
+    else:
+        work = []
     if saved_out is not None:
         save = pltpu.make_async_copy(xg, saved_out, local.at[2])
         save.start()
-    fold.second(order[n0 - 1])
-    fold.third(order[n0 - 2])
-    fold.third(order[n0 - 1])
+    keep = own_copies(next_in, next_out, w_local) if extra else []
+    last = fold.steps()
+    for t in range(n0, last):
+        share = -(-len(work) // (last - t))
+        for _ in range(share):
+            n = work.pop(0)
+            if "grad" not in SKIP:
+                gradient(n)
+        fold.step(t)
+        if extra:
+            other.step(t - 1)
+        if folded:
+            aside.step(t)
+    if folded:
+        assert aside.steps() == last
+        aside.end()
+    if extra:
+        for t in range(last - 1, n0 + 2):
+            other.step(t)
+        other.end()
+        for c in keep:
+            c.wait()
     spread.end()
     fold.end()
     if back:
-        for offs in others:
+        for n in range(max(0, ups - 2), ups) if "grad" not in SKIP else ():
+            up_piece(n).wait()
+        for n in range(downs - 1, downs) if "grad" not in SKIP else ():
+            down_piece(n).wait()
+        for offs in route.others:
             chance_copy(offs).wait()
         chance_out[...] = chance_got[...]
-        for c in outs:
-            c.wait()
     if saved_out is not None:
         save.wait()
 
 
-def mixture_call(mode, count, layer, cid, mask, router, expert, partner, x, g=None):
+def mixture_call(mode, count, layer, cid, mask, router, expert, partner, x, g=None, following=(), summed=()):
     axes = torus_axes(count)
     fore, back = "f" in mode, "b" in mode
     vmem, anywhere = pl.BlockSpec(memory_space=pltpu.VMEM), pl.BlockSpec(memory_space=pl.ANY)
@@ -755,6 +1061,8 @@
     if back:
         args.append(g)
         in_specs.append(vmem)
+    args += list(following) + list(summed)
+    in_specs += [vmem] * len(following) + [anywhere] * len(summed)
     whole = (count, ROWS, MODEL_WIDTH)
     out_shape, out_specs = [], []
     block = jax.ShapeDtypeStruct((ROWS, MODEL_WIDTH), jnp.float32)
@@ -768,25 +1076,33 @@
         out_shape += [block, jax.ShapeDtypeStruct((count, 8, ROWS), jnp.float32)]
         out_shape += [jax.ShapeDtypeStruct(w.shape, jnp.float32) for w in expert]
         out_specs += [vmem, vmem, anywhere, anywhere]
-    streams = 2 * (fore + back)
+    out_shape += weight_shapes(following, count)
+    out_specs += [anywhere] * len(following) + [vmem] * len(summed)
+    out_shape += [jax.ShapeDtypeStruct((a.shape[1], a.shape[2] // 2), jnp.float32) for a in summed]
     dma = pltpu.SemaphoreType.DMA
     scratch = [pltpu.VMEM(expert[0].shape, jnp.bfloat16), pltpu.VMEM(expert[1].shape, jnp.bfloat16), pltpu.VMEM(whole, jnp.bfloat16),
                pltpu.VMEM((TILE, 2 * FFE), jnp.float32), pltpu.VMEM((TILE, 128), jnp.float32), dma((3,))]
-    ag = streams if mode != "b" else 2
-    scratch += [dma((ag, count)), dma((ag, count)), dma((streams, count)), dma((streams, count))]
-    half = pltpu.VMEM((2, count, ROWS // 2, MODEL_WIDTH), jnp.bfloat16)
-    low = lambda width: pltpu.VMEM((TILE, width), jnp.bfloat16)
+    parts = len(TOKEN_PARTS)
+    ag, rs = parts * (1 if mode == "b" else fore + back), parts * (fore + back)
+    scratch += [dma((ag, count)), dma((ag, count)), dma((rs, count)), dma((rs, count))]
+    blocks = pltpu.VMEM(whole, jnp.bfloat16)
+    low = lambda rows, width: pltpu.VMEM((rows, width), jnp.bfloat16)
     if fore:
-        scratch += [pltpu.VMEM(whole, jnp.bfloat16), half, low(FFE)]
+        scratch += [blocks, blocks, low(TILE, FFE)]
     if back:
-        scratch += [pltpu.VMEM(whole, jnp.bfloat16), pltpu.VMEM(whole, jnp.bfloat16), half, pltpu.VMEM((TILE, FFE), jnp.float32),
-                    low(2 * FFE), low(FFE), low(FFE), low(FFE), pltpu.VMEM(expert[0].shape, jnp.float32),
-                    pltpu.VMEM(expert[1].shape, jnp.float32), pltpu.VMEM((count, 8, ROWS), jnp.float32),
-                    pltpu.VMEM((count, 8, ROWS), jnp.float32), dma((count,)), dma((count,))]
+        scratch += [blocks, blocks, blocks, pltpu.VMEM((TILE, FFE), jnp.float32),
+                    low(count * ROWS, 2 * FFE), low(count * ROWS, FFE), low(TILE, FFE), low(TILE, FFE),
+                    pltpu.VMEM((2, PIECE, 2 * FFE), jnp.float32), pltpu.VMEM((1, PIECE, MODEL_WIDTH), jnp.float32),
+                    pltpu.VMEM((count, 8, ROWS), jnp.float32), pltpu.VMEM((count, 8, ROWS), jnp.float32), dma((count,)), dma((count,)),
+                    dma((2, 2))]
+    if following:
+        scratch += weight_sems(following, count)
+    if summed:
+        scratch += fold_scratch(summed, axes)
     rows = count * ROWS
     flops = rows * 6 * MODEL_WIDTH * FFE * (fore + 2 * back + (mode == "b"))
     return pl.pallas_call(
-        functools.partial(mixture_kernel, mode, axes, count, layer),
+        functools.partial(mixture_kernel, mode, axes, count, layer, len(following), len(summed)),
         out_shape=out_shape,
         in_specs=in_specs,
         out_specs=out_specs,
@@ -1006,15 +1322,15 @@
         keep = sec == layer
         experts.append((jnp.where(keep, expert_gate_up[0, 0], partner_expert[0]), jnp.where(keep, expert_down[0, 0], partner_expert[1])))
 
-    def layer_weights(layer):
+    def layer_parts(layer):
         at, parts = 0, []
         for w in widths:
             parts.append(packs[layer][:, at : at + w])
             at += w
-        joint, output, tail = gather_all(parts, count, 2, pair=True)
-        joint = joint.reshape(MODEL_WIDTH, -1)
-        output = output.reshape(MODEL_WIDTH, -1)
-        tail = tail.reshape(MODEL_WIDTH, -1)
+        return parts
+
+    def layer_weights(arrays):
+        joint, output, tail = [a.reshape(MODEL_WIDTH, -1) for a in arrays]
         second = tail[:, small_width:]
         weights = (joint, output, tail[:, : router_weight.shape[2]], second[:, 0].astype(jnp.float32), second[:, 1].astype(jnp.float32))
         routers.append(tail[:, :small_width])
@@ -1031,7 +1347,11 @@
     weights, masks, stores = [], [], []
     hidden = micro(tokens, 0)
     for layer in range(layers):
-        got, mask = layer_weights(layer)
+        if not fused:
+            arrays = gather_all(layer_parts(layer), count, 2, pair=True)
+        elif layer == 0:
+            arrays = weight_spread(layer_parts(layer), count, 2)
+        got, mask = layer_weights(arrays)
         weights.append(got)
         masks.append(mask)
         middle, normed_two, kept = front(hidden.astype(jnp.float32), place, got)
@@ -1039,9 +1359,10 @@
             mixed, kept_mixture = mixture_forward(normed_two, got[2], mask, experts[layer], count, me)
         else:
             named = mask.astype(jnp.float32).reshape(count, DEVICE_ROWS, 1)
-            call = lambda mode, cid, *data: mixture_call(mode, count, layer, cid, named, routers[layer], own_expert, partner_expert, *data)
+            call = lambda mode, cid, *data, **more: mixture_call(
+                mode, count, layer, cid, named, routers[layer], own_expert, partner_expert, *data, **more)
             if layer < layers - 1:
-                mixed, everyone = call("f", 4, normed_two)
+                mixed, everyone, *arrays = call("f", 4, normed_two, following=layer_parts(layer + 1))
                 kept_mixture = (named, everyone)
             else:
                 mixed, *kept_mixture = call("fb", 5, normed_two, micro(cotangent, 0))
@@ -1057,16 +1378,33 @@
         else:
             if layer < layers - 1:
                 named, everyone = kept_mixture
-                kept_mixture = mixture_call("b", count, layer, 6, named, routers[layer], own_expert, partner_expert, everyone, grad)
-            mixed, rows, grad_up, grad_down = kept_mixture
+                kept_mixture = mixture_call("b", count, layer, 6, named, routers[layer], own_expert, partner_expert, everyone, grad,
+                                            summed=packs[layer + 1])
+            mixed, rows, grad_up, grad_down, *more = kept_mixture
+            if layer < layers - 1:
+                shares[layer + 1] = more
             grad_chance = rows[:, 0].T
         expert_grads[layer] = (grad_up, grad_down)
         grad_hidden, parts = front_backward(grad.astype(jnp.float32), mixed, grad_chance, kept, place, weights[layer])
         grad = grad_hidden.astype(jnp.bfloat16)
         tail = small_halves(MODEL_WIDTH, parts[2], jnp.stack([parts[3], parts[4]], axis=1), parts[2][:, :0])
         packed = [parts[0], parts[1], jnp.concatenate(tail, axis=1)]
-        packed = [a.astype(jnp.bfloat16).reshape(count, shard, -1) for a in packed]
-        shares[layer] = reduce_all(packed, count, 3, pair=True)
+        packs[layer] = [a.astype(jnp.bfloat16).reshape(count, shard, -1) for a in packed]
+        if not fused:
+            shares[layer] = reduce_all(packs[layer], count, 3, pair=True)
+    if fused:
+        *outs, grad_up, grad_down, boundary = closing(packs[0], shares[1], expert_grads[0], expert_grads[1], grad, last, count, 3)
+        half = outs[2].shape[1] // 2
+        return (
+            boundary[None],
+            outs[0][None],
+            outs[1][None],
+            outs[2][None, :, : router_weight.shape[2]],
+            outs[2][None, :, half],
+            outs[2][None, :, half + 1],
+            grad_up[None, None],
+            grad_down[None, None],
+        )
     outs = []
     for a in range(3):
         kept_half = jnp.where(leading, shares[0][a], shares[1][a])

time: 965 us -> 908 us (0.941)
  Pallas kernels: 783 us -> 739 us
  other arithmetic: 51.6 us -> 25.2 us
  local copies, waits for them, and re-layouts: 37.8 us -> 49.3 us
    pallas_call x4 -> x2, Pallas kernels: 297 us -> 157 us  [the longest x1 83.6 us: closing(): pl.pallas_call(functools.partial(closing_kernel, axes, n), out_shape=[jax...]
    pallas_call x3, Pallas kernels: 486 us -> 582 us  [mixture_call(): pl.pallas_call(functools.partial(mixture_kernel, mode, axes, count, layer...]
    broadcast_in_dim x5 -> x0, other arithmetic: 16.8 us -> none  [the longest x2 14.9 us: body(): expert_outs.append((kept_sum + got_sum)[None, None])]
    select_n x10 -> x0, other arithmetic: 11.2 us -> none  [the longest x2 6.49 us: body(): jnp.where(leading, expert_grads[1][a], expert_grads[0][a])]
    unnamed x220 -> x163, local copies, waits for them, and re-layouts: 10.6 us -> 20 us
  transfers between devices with their start and end apart: 9 -> 3, of which waited for: 1 -> 0; matrix products, arithmetic and copies ran while one was open for 9% -> 4% of each run, Pallas kernels for 31% -> 8%
where the time goes in v3:
time: 908 us; the launch traced here: 897 us
  Pallas kernels  739 us (81%)
  matrix products  80.7 us (9%)
  local copies, waits for them, and re-layouts  49.3 us (5%)
  other arithmetic  25.2 us (3%)
    pallas_call x3, Pallas kernels, mixture_call(): pl.pallas_call(functools.partial(mixture_kernel, mode, axes, count, layer...  582 us
    pallas_call x1, Pallas kernels, closing(): pl.pallas_call(functools.partial(closing_kernel, axes, n), out_shape=[jax...  83.6 us
    pallas_call x1, Pallas kernels, weight_spread(): pl.pallas_call(functools.partial(weight_spread_kernel, torus_axes(count),...  73.2 us
    dot_general x6, matrix products, dot_columns(): lax.dot_general(left, right, (((1,), (1,)), ((), ())), preferred_element_...  24.7 us
    dot_general x6, matrix products, dot_rows(): lax.dot_general(left, right, (((0,), (0,)), ((), ())), preferred_element_...  20.2 us
    unnamed x163, local copies, waits for them, and re-layouts  20 us
  transfers between devices with their start and end apart: 3, of which 0 were waited for; matrix products, arithmetic and copies ran while one was open for 4% of the time, Pallas kernels for 8%

profile of v3, /device:TPU:28, one launch (start us, length us, event | category | flops | bytes accessed | tf_op | source)
XLA Modules:
  0.0 896.8 jit_solution(10400382885676072313)
XLA Ops:
  8.9 73.2 %weight_spread.1 = (bf16[16,96,2560]{2,1,0:T(8,128)(2,1)}, bf16[16,96,1536]{2,1,0:T(8,128)(2,1)}, bf16[16,96,256]{2,1,0:T(8,128)(2,1)}) custom-call(bf16[96,1280]{1,0:T(8,128)(2,1)} %slice.206.refs_0_, bf16[96,768]{1,0:T(8,128)(2,1)} %slice.207.refs_1_, bf16[96,128]{1,0:T(8,128)(2,1)} %slice.208.refs_2_), custom_call_target="tpu_custom_call" | custom-call | tf_op jit(solution)/shard_map/weight_spread/pallas_call | solution.py:782
  83.7 4.5 fusion.45
  90.9 2.3 copy.158
  93.1 1.8 copy.157
  101.6 2.3 bitcast_select_fusion.1
  109.4 2.3 convolution_convert_fusion.9
  111.7 3.4 multiply_reduce_fusion.5
  116.7 176.8 %mixture_f.1 = (f32[128,1536]{1,0:T(8,128)}, bf16[16,128,1536]{2,1,0:T(8,128)(2,1)}, bf16[16,96,2560]{2,1,0:T(8,128)(2,1)}, bf16[16,96,1536]{2,1,0:T(8,128)(2,1)}, bf16[16,96,256]{2,1,0:T(8,128)(2,1)}) custom-call(f32[16,128,1]{2,1,0:T(8,128)} %copy.163.refs_0_, bf16[1536,128]{1,0:T(8,128)(2,1)} %slice.219.refs_1_, bf16[1536,1024]{1,0:T(8,128)(2,1)} %bitcast.320, ...), custom_call_target="tpu_custom_call" | custom-call | flops 9663676416 | bytes 12582912 | tf_op jit(solution)/shard_map/mixture_f/pallas_call | solution.py:1104
  295.4 4.5 fusion.71
  306.8 2.3 convolution_convert_fusion.8
  309.1 3.4 multiply_reduce_fusion.4
  316.3 231.1 %mixture_fb.1 = (f32[128,1536]{1,0:T(8,128)}, f32[128,1536]{1,0:T(8,128)}, f32[16,8,128]{2,1,0:T(8,128)}, f32[1536,1024]{1,0:T(8,128)}, f32[512,1536]{1,0:T(8,128)}) custom-call(f32[16,128,1]{2,1,0:T(8,128)} %copy.170.refs_0_, bf16[1536,128]{1,0:T(8,128)(2,1)} %slice.234.refs_1_, bf16[1536,1024]{1,0:T(8,128)(2,1)} %bitcast.321, ...), custom_call_target="tpu_custom_call" | custom-call | flops 28991029248 | bytes 12582912 | tf_op jit(solution)/shard_map/mixture_fb/pallas_call | solution.py:1104
  549.6 1.9 convolution_convert_fusion.7
  551.6 2.0 multiply_reduce_fusion.2
  554.7 4.0 convolution_convert_fusion.5
  565.0 3.1 fusion.14
  568.1 3.6 convolution_convert_fusion.3
  572.7 6.8 fusion.38
  579.6 5.5 convolution_convert_fusion.1
  586.8 2.2 fusion.37.refs_7_
  589.0 173.9 %mixture_b.1 = (f32[128,1536]{1,0:T(8,128)}, f32[16,8,128]{2,1,0:T(8,128)}, f32[1536,1024]{1,0:T(8,128)}, f32[512,1536]{1,0:T(8,128)}, f32[96,1280]{1,0:T(8,128)}, /*index=5*/f32[96,768]{1,0:T(8,128)}, f32[96,128]{1,0:T(8,128)}) custom-call(f32[16,128,1]{2,1,0:T(8,128)} %copy.163.refs_0_, bf16[1536,128]{1,0:T(8,128)(2,1)} %slice.219.refs_1_, ...), custom_call_target="tpu_custom_call" | custom-call | flops 28991029248 | bytes 12582912 | tf_op jit(solution)/shard_map/mixture_b/pallas_call | solution.py:1104
  763.9 1.7 multiply_reduce_fusion
  766.0 4.0 convolution_convert_fusion.4
  771.7 1.7 fusion
  775.7 2.4 fusion.15
  778.3 3.6 convolution_convert_fusion.2
  783.0 6.1 fusion.24
  789.1 5.4 convolution_convert_fusion
  797.3 83.6 %closing.1 = (f32[96,2560]{1,0:T(8,128)}, f32[96,1536]{1,0:T(8,128)}, f32[96,256]{1,0:T(8,128)}, f32[1536,1024]{1,0:T(8,128)}, f32[512,1536]{1,0:T(8,128)}, /*index=5*/bf16[2,128,1536]{2,1,0:T(8,128)(2,1)}) custom-call(bf16[16,96,2560]{2,1,0:T(8,128)(2,1)} %bitcast.238, bf16[16,96,1536]{2,1,0:T(8,128)(2,1)} %bitcast.239, ...), custom_call_target="tpu_custom_call" | custom-call | bytes 100000000 | tf_op jit(solution)/shard_map/closing/pallas_call | solution.py:734
  884.0 2.1 copy.210
  887.9 6.8 copy.213
  894.7 1.7 copy.214
  (287 shorter events, 64.5 us)
Async XLA Ops:
  0.7 3.9 copy-start.6
  0.7 4.1 copy-start.73
  0.7 5.3 copy-start.31
  3.9 2.9 collective-permute-start
  4.0 112.7 %collective-permute-start.1 = (bf16[1536,1024]{1,0:T(8,128)(2,1)}, bf16[1536,1024]{1,0:T(8,128)(2,1)}, u32[]{:S(2)}, u32[]{:S(2)}) collective-permute-start(bf16[1536,1024]{1,0:T(8,128)(2,1)} %bitcast.319), channel_id=1, source_target_pairs={{0,16},{16,0},{1,17},{17,1},{2,18},{18,2},{3,19},{19,3},{4,20},{20... | collective-permute-start | bytes 9437192 | tf_op jit(solution)/shard_map/ppermute | solution.py:1116
  4.5 112.2 %collective-permute-start.2 = (bf16[512,1536]{1,0:T(8,128)(2,1)}, bf16[512,1536]{1,0:T(8,128)(2,1)}, u32[]{:S(2)}, u32[]{:S(2)}) collective-permute-start(bf16[512,1536]{1,0:T(8,128)(2,1)} %bitcast.323), channel_id=1, source_target_pairs={{0,16},{16,0},{1,17},{17,1},{2,18},{18,2},{3,19},{19,3},{4,20},{20... | collective-permute-start | bytes 4718600 | tf_op jit(solution)/shard_map/ppermute | solution.py:1116
  6.0 77.7 %copy-start.59 = (f32[128]{0:T(128)}, f32[128]{0:T(128)S(1)}, u32[]{:S(2)}) copy-start(f32[128]{0:T(128)S(1)} %add_rsqrt_fusion.3) | copy-start | bytes 1540
  83.7 4.6 copy-start.40
  83.7 31.4 %copy-start.51 = (f32[1536]{0:T(1024)}, f32[1536]{0:T(1024)S(1)}, u32[]{:S(2)}) copy-start(f32[1536]{0:T(1024)S(1)} %get-tuple-element.110) | copy-start | bytes 18436
  101.5 4.4 copy-start.24
  108.0 3.7 copy-start.34
  294.9 14.2 %copy-start = (bf16[128,1536]{1,0:T(8,128)(2,1)}, bf16[128,1536]{1,0:T(8,128)(2,1)S(1)}, u32[]{:S(2)}) copy-start(bf16[128,1536]{1,0:T(8,128)(2,1)S(1)} %get-tuple-element.115) | copy-start | bytes 1179652
  294.9 5.0 copy-start.61
  295.3 17.2 %copy-start.53 = (f32[1536]{0:T(1024)}, f32[1536]{0:T(1024)S(1)}, u32[]{:S(2)}) copy-start(f32[1536]{0:T(1024)S(1)} %get-tuple-element.108) | copy-start | bytes 18436
  305.0 4.0 copy-start.46
  305.1 4.0 copy-start.48
  305.2 3.9 copy-start.36
  316.3 235.2 %copy-start.54 = (f32[1536]{0:T(1024)S(1)}, f32[1536]{0:T(1024)}, u32[]{:S(2)}) copy-start(f32[1536]{0:T(1024)} %copy-done.53) | copy-start | bytes 18436
  549.6 4.0 copy-start.3
  549.6 4.0 copy-start.15
  549.6 4.0 copy-start.30
  549.6 4.0 copy-start.32
  549.6 4.0 copy-start.68
  554.7 4.3 copy-start.37
  568.1 3.7 copy-start.22
  579.6 5.5 copy-start.50
  589.0 174.9 %copy-start.56 = (f32[128,16]{0,1:T(8,128)S(1)}, f32[128,16]{0,1:T(8,128)}, u32[]{:S(2)}) copy-start(f32[128,16]{0,1:T(8,128)} %get-tuple-element.156) | copy-start | bytes 24580
  589.0 174.9 %copy-start.69 = (f32[128]{0:T(128)S(1)}, f32[128]{0:T(128)}, u32[]{:S(2)}) copy-start(f32[128]{0:T(128)} %get-tuple-element.155) | copy-start | bytes 1540
  589.0 175.0 %copy-start.52 = (f32[1536]{0:T(1024)S(1)}, f32[1536]{0:T(1024)}, u32[]{:S(2)}) copy-start(f32[1536]{0:T(1024)} %copy-done.51) | copy-start | bytes 18436
  766.0 4.3 copy-start.35
  880.9 5.3 copy-start.23
  887.9 6.8 copy-start.12
  (48 other events, 98.0 us)

commit v4 on v3

--- a/solution.py
+++ b/solution.py
@@ -21,7 +21,7 @@
 norm_epsilon = 1e-06
 CHUNK_ROWS = 2048
 
-VMEM_BYTES = 66_000_000
+VMEM_BYTES = 67_000_000
 
 
 def torus_axes(count):
@@ -387,33 +387,49 @@
 SKIP = set()
 PIECE = 256
 MESH = pl.DeviceIdType.MESH
-TOKEN_PARTS = (((0, 1, 2), 0, 64), ((0, 2, 1), 64, 64))
+ORDERS = ((0, 1, 2), (0, 2, 1), (1, 0, 2), (2, 0, 1))
+TOKEN_PARTS = tuple((order, 32 * n, 32) for n, order in enumerate(ORDERS))
 
 
 class Route:
     def __init__(self, axes, order):
         self.axes, self.order = axes, order
         self.sizes = [size for _, size in axes]
+        assert self.sizes == [4, 2, 2]
         self.me = lax.axis_index("dp")
         self.all = offsets(self.sizes)
         self.others = [o for o in self.all if any(o)]
-
-    def moved(self, steps):
-        out = self.me
-        for (stride, size), step in zip(self.axes, steps):
-            if step % size:
-                digit = lax.rem(lax.div(self.me, stride), size)
-                out = out + (lax.rem(digit + (step % size), size) - digit) * stride
+        self.z = lax.div(self.me, axes[0][0])
+        self.inner = jnp.logical_and(self.z >= 1, self.z <= 2)
+        later = order[order.index(0) + 1 :]
+        self.lines = [(j, i) for j in range(2) for i in range(2) if all((0, j, i)[a] == 0 for a in later)]
+
+    def digit(self, axis):
+        stride, size = self.axes[axis]
+        return lax.rem(lax.div(self.me, stride), size)
+
+    def plane(self, rank):
+        z = self.z
+        if rank == 1:
+            return z + 1 - 2 * lax.rem(z, 2)
+        if rank == 2:
+            return 2 - lax.div(z, 2)
+        if rank == 3:
+            return 3 - 3 * lax.div(z, 2)
+        return z
+
+    def block(self, offs):
+        out = self.me + (self.plane(offs[0]) - self.z) * self.axes[0][0]
+        for axis in (1, 2):
+            if offs[axis]:
+                out = out + (1 - 2 * self.digit(axis)) * self.axes[axis][0]
         return out
 
-    def source(self, offs):
-        return self.moved([-o for o in offs])
-
-    def target(self, offs):
-        return self.moved(list(offs))
-
     def flat(self, offs):
-        return (offs[0] * self.sizes[1] + offs[1]) * self.sizes[2] + offs[2]
+        return (offs[0] * 2 + offs[1]) * 2 + offs[2]
+
+    def extra(self, line, n):
+        return 16 + 2 * self.lines.index(line) + n
 
     def last_axis(self, offs):
         for axis in reversed(self.order):
@@ -425,113 +441,199 @@
         out[self.last_axis(offs)] = 0
         return tuple(out)
 
-    def hop(self, offs):
-        axis = self.last_axis(offs)
-        out = [0, 0, 0]
-        out[axis] = offs[axis]
-        return tuple(out)
-
-    def children(self, offs):
-        return [o for o in self.others if self.base(o) == offs]
+    def across(self, offs):
+        return [o for o in self.others if self.last_axis(o) and self.base(o) == offs]
+
+
+def remote(src, dst, send, recv, peer):
+    return pltpu.make_async_remote_copy(src_ref=src, dst_ref=dst, send_sem=send, recv_sem=recv, device_id=peer, device_id_type=MESH)
 
 
 class Spread:
-    def __init__(self, streams, send, recv, psend=None, precv=None):
-        self.streams, self.send, self.recv, self.psend, self.precv = streams, send, recv, psend, precv
+    def __init__(self, streams, send, recv):
+        self.streams, self.send, self.recv = streams, send, recv
         self.ids = range(len(streams))
 
-    def copy(self, s, offs):
+    def copy(self, s, offs, target, key, slot):
         route, own, out = self.streams[s]
-        base = route.base(offs)
-        block, f = route.source(base), route.flat(offs)
-        return pltpu.make_async_remote_copy(
-            src_ref=out(block) if any(base) else own, dst_ref=out(block), send_sem=self.send.at[s, f], recv_sem=self.recv.at[s, f],
-            device_id={"dp": route.target(route.hop(offs))}, device_id_type=MESH)
-
-    def share(self, s, offs):
+        block = route.block(offs)
+        return remote(out(block) if any(offs) else own, out(block), self.send.at[s, slot], self.recv.at[s, route.flat(key)], {"dp": target})
+
+    def arrival(self, s, offs):
         route, own, out = self.streams[s]
-        block, f = route.source(offs), route.flat(offs)
-        return pltpu.make_async_remote_copy(
-            src_ref=out(block) if any(offs) else own, dst_ref=out(block), send_sem=self.psend.at[s, f], recv_sem=self.precv.at[s, f],
-            device_id={"section": 1 - lax.axis_index("section")}, device_id_type=MESH)
+        f = route.flat(offs)
+        return remote(own, out(route.block(offs)), self.send.at[s, f], self.recv.at[s, f], {"dp": route.block(offs)})
+
+    def onward(self, s, offs):
+        route = self.streams[s][0]
+        k, line = offs[0], offs[1:]
+        out = [(o, False, self.copy(s, offs, route.block((0, *[int(o[a] != offs[a]) for a in (1, 2)])), o, route.flat(o)))
+               for o in route.across(offs)]
+        if line in route.lines:
+            near, facing = route.block((1, 0, 0)), route.block((2, 0, 0))
+            if k == 0:
+                out.append(((1, *line), False, self.copy(s, offs, near, (1, *line), route.flat((1, *line)))))
+                out.append(((2, *line), True, self.copy(s, offs, facing, (2, *line), route.extra(line, 0))))
+            elif k == 1:
+                out.append(((3, *line), True, self.copy(s, offs, facing, (3, *line), route.extra(line, 1))))
+            else:
+                out.append((offs, True, self.copy(s, offs, near, offs, route.flat(offs))))
+        return out
+
+    def launch(self, items):
+        for s, (_, inner, copy) in items:
+            if inner:
+                pl.when(self.streams[s][0].inner)(copy.start)
+            else:
+                copy.start()
 
     def step(self, t):
-        if "comm" in SKIP:
+        if "comm" in SKIP or "ag" in SKIP:
             return
-        work = [(offs, s) for s in self.ids for offs in self.streams[s][0].all if offs[0] + (offs[1] > 0) + (offs[2] > 0) == t]
-        kids = {(offs, s): self.streams[s][0].children(offs) for offs, s in work}
+        work = [(offs, s) for s in self.ids for offs in self.streams[s][0].all if offs[0] + offs[1] + offs[2] == t]
         if t == 0:
-            for child, s in sorted([(child, s) for offs, s in work for child in kids[offs, s]], key=lambda e: (e[0][0], e[0], e[1])):
-                self.copy(s, child).start()
-            kids = {e: [] for e in work}
-        for offs, s in sorted(work, key=lambda e: (not kids[e], -e[0][0], e[0], e[1])):
-            if any(offs):
-                self.copy(s, offs).wait_recv()
-            for child in kids[offs, s]:
-                self.copy(s, child).start()
-            if self.psend is not None:
-                self.share(s, offs).start()
+            first = [(s, item) for offs, s in work for item in self.onward(s, offs)]
+            self.launch(sorted(first, key=lambda e: (e[1][0][0], e[1][0], e[0])))
+            return
+        ends = lambda e: not self.streams[e[1]][0].across(e[0]) and e[0][1:] not in self.streams[e[1]][0].lines
+        for offs, s in sorted(work, key=lambda e: (ends(e), -e[0][0], e[0], e[1])):
+            self.arrival(s, offs).wait_recv()
+            self.launch([(s, item) for item in sorted(self.onward(s, offs), key=lambda e: (e[1], e[0]))])
 
     def end(self):
-        if "comm" in SKIP:
+        if "comm" in SKIP or "ag" in SKIP:
             return
+        for s in self.ids:
+            for offs in self.streams[s][0].all:
+                for _, inner, copy in self.onward(s, offs):
+                    if inner:
+                        pl.when(self.streams[s][0].inner)(copy.wait_send)
+                    else:
+                        copy.wait_send()
+
+
+SPREAD_STEPS = 6
+
+
+def add_rows(sources, dest, rows, step=16):
+    cols = dest.shape[-1]
+    width = next(w for w in (640, 512, 384, 128) if cols % w == 0)
+
+    def one(r, _):
+        at = pl.ds(pl.multiple_of(r * step, step), step)
+
+        def part(c, _):
+            span = pl.ds(pl.multiple_of(c * width, width), width)
+            total = sources[0][at, span].astype(jnp.float32)
+            for source in sources[1:]:
+                total = total + source[at, span].astype(jnp.float32)
+            dest[at, span] = total.astype(dest.dtype)
+            return 0
+
+        return lax.fori_loop(0, cols // width, part, 0)
+
+    lax.fori_loop(0, rows // step, one, 0)
+
+
+class Fold:
+    def __init__(self, streams, send, recv, ranks):
+        self.streams, self.send, self.recv = streams, send, recv
+        self.ids = range(len(streams))
+        self.turn = {k: c for c, k in enumerate(ranks)}
+        self.plan = []
         for s in self.ids:
             route = self.streams[s][0]
             for offs in route.all:
-                if any(offs):
-                    self.copy(s, offs).wait_send()
-                if self.psend is not None:
-                    self.share(s, offs).wait()
-
-
-def add_rows(sources, dest, rows, step=16):
-    def one(r, _):
-        at = pl.ds(pl.multiple_of(r * step, step), step)
-        total = sources[0][at].astype(jnp.float32)
-        for source in sources[1:]:
-            total = total + source[at].astype(jnp.float32)
-        dest[at] = total.astype(dest.dtype)
-        return 0
-
-    lax.fori_loop(0, rows // step, one, 0)
-
-
-class Fold:
-    def __init__(self, streams, send, recv, chunks):
-        self.streams, self.send, self.recv = streams, send, recv
-        self.ids = range(len(streams))
-        self.turn = {k: c for c, k in enumerate(chunks)}
-
-    def when(self, route, offs):
-        return max([self.turn[offs[0]]] + [self.when(route, o) + 1 for o in route.children(offs)])
+                if offs[0] and offs[1:] in route.lines:
+                    self.plan.append((self.ready(route, offs), 1, -offs[0], s, offs, self.outer))
+                    self.plan.append((self.passed(route, offs), 2, -offs[0], s, offs, self.middle))
+                else:
+                    when = self.done(route, offs)
+                    rank = 3 if not any(offs) else 1 if self.near(route, offs) or not offs[0] and offs[1:] in route.lines else 0
+                    self.plan.append((when, rank, -offs[0], s, offs, self.plain))
+        self.plan.sort(key=lambda e: e[:5])
+
+    def near(self, route, offs):
+        return [o for o in route.across(offs) if o[0] == offs[0]]
+
+    def ready(self, route, offs):
+        return max([self.turn[offs[0]]] + [self.done(route, o) + 1 for o in self.near(route, offs)])
+
+    def passed(self, route, offs):
+        line = offs[1:]
+        return self.ready(route, offs) + 1 if offs[0] > 1 else max(self.ready(route, offs), self.ready(route, (3, *line)) + 2)
+
+    def done(self, route, offs):
+        when = self.ready(route, offs)
+        if not offs[0] and offs[1:] in route.lines:
+            when = max(when, self.passed(route, (1, *offs[1:])) + 1, self.passed(route, (2, *offs[1:])) + 1)
+        return when
+
+    def arrival(self, s, slot):
+        route, share, got, _, _ = self.streams[s]
+        return remote(share((0, 0, 0)), got(slot), self.send.at[s, slot], self.recv.at[s, slot], {"dp": route.block((1, 0, 0))})
 
     def copy(self, s, offs):
         route, share, got, _, _ = self.streams[s]
         f = route.flat(offs)
-        return pltpu.make_async_remote_copy(
-            src_ref=share(offs), dst_ref=got(f), send_sem=self.send.at[s, f], recv_sem=self.recv.at[s, f],
-            device_id={"dp": route.target(route.hop(offs))}, device_id_type=MESH)
+        if route.last_axis(offs):
+            hop = [0, 0, 0]
+            hop[route.last_axis(offs)] = 1
+            return remote(share(offs), got(f), self.send.at[s, f], self.recv.at[s, f], {"dp": route.block(hop)})
+        near, facing = route.block((1, 0, 0)), route.block((2, 0, 0))
+        if offs[0] == 1:
+            return remote(share(offs), got(f), self.send.at[s, f], self.recv.at[s, f], {"dp": near})
+        slot = f + (route.extra(offs[1:], offs[0] - 2) - f) * route.inner.astype(jnp.int32)
+        return remote(share(offs), got(slot), self.send.at[s, f], self.recv.at[s, slot], {"dp": jnp.where(route.inner, facing, near)})
+
+    def settle(self, s, offs, slots, out=None):
+        route, share, got, _, rows = self.streams[s]
+        if slots:
+            for f in slots:
+                self.arrival(s, f).wait_recv()
+            own = share(offs)
+            add_rows([own] + [got(f) for f in slots], own if out is None else out, rows)
+
+    def outer(self, s, offs):
+        route = self.streams[s][0]
+        self.settle(s, offs, [route.flat(o) for o in self.near(route, offs)])
+        pl.when(jnp.logical_not(route.inner))(self.copy(s, offs).start)
+
+    def middle(self, s, offs):
+        route = self.streams[s][0]
+
+        @pl.when(route.inner)
+        def _():
+            self.settle(s, offs, [route.flat(offs) if offs[0] > 1 else route.extra(offs[1:], 1)])
+            self.copy(s, offs).start()
+
+    def plain(self, s, offs):
+        route, share, got, out, rows = self.streams[s]
+        slots = [route.flat(o) for o in self.near(route, offs)]
+        if not offs[0] and offs[1:] in route.lines:
+            slots.append(route.flat((1, *offs[1:])))
+            facing = route.extra(offs[1:], 0)
+
+            @pl.when(route.inner)
+            def _():
+                self.settle(s, offs, [facing])
+
+        self.settle(s, offs, slots, None if any(offs) else out)
+        if any(offs):
+            self.copy(s, offs).start()
 
     def step(self, t):
-        if "comm" in SKIP:
+        if "comm" in SKIP or "rs" in SKIP:
             return
-        work = [(offs, s) for s in self.ids for offs in self.streams[s][0].all if self.when(self.streams[s][0], offs) == t]
-        kids = {(offs, s): self.streams[s][0].children(offs) for offs, s in work}
-        for offs, s in sorted(work, key=lambda e: (bool(kids[e]), not (e[0][1] or e[0][2]), [-o for o in e[0]], e[1])):
-            route, share, got, out, rows = self.streams[s]
-            for o in kids[offs, s]:
-                self.copy(s, o).wait_recv()
-            if kids[offs, s]:
-                own = share(offs)
-                add_rows([own] + [got(route.flat(o)) for o in kids[offs, s]], own if any(offs) else out, rows)
-            if any(offs):
-                self.copy(s, offs).start()
+        for when, _, _, s, offs, action in self.plan:
+            if when == t:
+                action(s, offs)
 
     def steps(self):
-        return 1 + max(self.when(self.streams[s][0], (0, 0, 0)) for s in self.ids)
+        return 1 + max(e[0] for e in self.plan)
 
     def end(self):
-        if "comm" in SKIP:
+        if "comm" in SKIP or "rs" in SKIP:
             return
         for s in self.ids:
             for offs in self.streams[s][0].others:
@@ -539,14 +641,22 @@
 
 
 def meet(axes, everyone, pair):
-    route = Route(axes, (0, 1, 2))
+    route = Route(axes, ORDERS[0])
     barrier = pltpu.get_barrier_semaphore()
-    peers = [o for o in route.others if everyone or sum(1 for v in o if v) == 1]
-    for offs in peers:
-        pl.semaphore_signal(barrier, inc=1, device_id={"dp": route.target(offs)}, device_id_type=MESH)
+    if everyone:
+        for offs in route.others:
+            pl.semaphore_signal(barrier, inc=1, device_id={"dp": route.block(offs)}, device_id_type=MESH)
+    else:
+        for offs in ((0, 0, 1), (0, 1, 0), (1, 0, 0)):
+            pl.semaphore_signal(barrier, inc=1, device_id={"dp": route.block(offs)}, device_id_type=MESH)
+
+        @pl.when(route.inner)
+        def _():
+            pl.semaphore_signal(barrier, inc=1, device_id={"dp": route.block((2, 0, 0))}, device_id_type=MESH)
+
     if pair:
         pl.semaphore_signal(barrier, inc=1, device_id={"section": 1 - lax.axis_index("section")}, device_id_type=MESH)
-    pl.semaphore_wait(barrier, len(peers) + (1 if pair else 0))
+    pl.semaphore_wait(barrier, (len(route.others) if everyone else 3 + route.inner.astype(jnp.int32)) + (1 if pair else 0))
 
 
 def contract(left, right, dims):
@@ -554,8 +664,9 @@
 
 
 def weight_parts(rows):
-    half = rows // 2
-    return (((0, 1, 2), 0, half), ((0, 2, 1), half, half))
+    third = rows // 3
+    sizes = (third, third, third // 2, third // 2)
+    return tuple((order, sum(sizes[:n]), sizes[n]) for n, order in enumerate(ORDERS))
 
 
 def weight_columns(half):
@@ -563,72 +674,119 @@
     return pl.ds(pl.multiple_of(sec * half, 128), half), pl.ds(pl.multiple_of((1 - sec) * half, 128), half)
 
 
-def weight_streams(axes, ins, outs):
-    streams = []
-    for own, full in zip(ins, outs):
-        rows, half = own.shape
-        cols, _ = weight_columns(half)
-        for order, at, size in weight_parts(rows):
-            span = pl.ds(at, size)
-            streams.append((Route(axes, order), own.at[span], lambda b, o=full, r=span, c=cols: o.at[b, r, c]))
-    return streams
-
-
-def weight_stream_count(arrays):
-    return sum(len(weight_parts(a.shape[0])) for a in arrays)
+def packed_columns(widths):
+    return [pl.ds(sum(widths[:n]), w) for n, w in enumerate(widths)]
+
+
+class WeightSpread:
+    def __init__(self, axes, own, full, outs, sems):
+        send, recv, self.psend, self.precv, self.local = sems
+        self.own, self.full, self.outs = own, full, outs
+        self.route = Route(axes, ORDERS[0])
+        streams = []
+        for order, at, size in weight_parts(own.shape[0]):
+            rows = pl.ds(at, size)
+            streams.append((Route(axes, order), own.at[rows], lambda b, r=rows: full.at[b, r]))
+        self.spread = Spread(streams, send, recv)
+        self.widths = [out.shape[2] // 2 for out in outs]
+
+    def deliveries(self, offs):
+        block, f = self.route.block(offs), self.route.flat(offs)
+        for a, cols in enumerate(packed_columns(self.widths)):
+            src = self.full.at[block, :, cols] if any(offs) else self.own.at[:, cols]
+            dst = self.outs[a].at[block, :, weight_columns(self.widths[a])[0]]
+            yield pltpu.make_async_copy(src, dst, self.local.at[a, f])
+            yield remote(src, dst, self.psend.at[a, f], self.precv.at[a, f], {"section": 1 - lax.axis_index("section")})
+
+    def step(self, t):
+        self.spread.step(t)
+        for offs in self.route.all:
+            if sum(offs) == t:
+                for copy in self.deliveries(offs):
+                    copy.start()
+
+    def end(self):
+        self.spread.end()
+        for offs in self.route.all:
+            for copy in self.deliveries(offs):
+                copy.wait()
+
+
+def weight_shapes(pack, widths, count):
+    return [jax.ShapeDtypeStruct((count, pack.shape[0], 2 * w), pack.dtype) for w in widths]
+
+
+def weight_scratch(pack, widths, count):
+    dma = pltpu.SemaphoreType.DMA
+    return [pltpu.VMEM((count, *pack.shape), pack.dtype)] + [dma((len(ORDERS), count + 4))] * 2 + [dma((len(widths), count))] * 3
+
+
+def weight_spread_kernel(axes, arrays, *refs):
+    own, outs, full, sems = refs[0], refs[1 : 1 + arrays], refs[1 + arrays], refs[2 + arrays :]
+    meet(axes, False, True)
+    spread = WeightSpread(axes, own, full, outs, sems)
+    for t in range(SPREAD_STEPS):
+        spread.step(t)
+    spread.end()
+
+
+def weight_spread(pack, widths, count, cid):
+    return pl.pallas_call(
+        functools.partial(weight_spread_kernel, torus_axes(count), len(widths)),
+        out_shape=weight_shapes(pack, widths, count),
+        in_specs=[pl.BlockSpec(memory_space=pltpu.VMEM)],
+        out_specs=[pl.BlockSpec(memory_space=pl.ANY)] * len(widths),
+        scratch_shapes=weight_scratch(pack, widths, count),
+        compiler_params=pltpu.CompilerParams(collective_id=cid, has_side_effects=True),
+        name="weight_spread",
+    )(pack)
 
 
 class WeightFold:
-    def __init__(self, axes, raws, sums, gots, loads, outs, sems, chunks):
-        self.send, self.recv, self.psend, self.precv, self.local = sems
-        self.arrays = list(zip(raws, sums, loads, outs))
-        self.chunks = chunks
+    def __init__(self, axes, raws, total, got, load, out, sems, ranks):
+        send, recv, self.psend, self.precv, self.local = sems
+        self.raws, self.total, self.held, self.rows = raws, total, load, out.shape[0]
+        self.widths = [raw.shape[2] // 2 for raw in raws]
+        self.ranks = ranks
         streams = []
-        for raw, total, load, got, out in zip(raws, sums, loads, gots, outs):
-            for order, at, size in weight_parts(out.shape[0]):
-                rows, route = pl.ds(at, size), Route(axes, order)
-                streams.append((route, lambda o, t=total, r=rows, w=route: t.at[w.flat(o), r], lambda f, g=got, r=rows: g.at[f, r],
-                                out.at[rows], size))
-        self.route = Route(axes, (0, 1, 2))
-        self.fold = Fold(streams, self.send, self.recv, chunks)
-
-    def block(self, c):
-        return [o for o in self.route.all if o[0] == self.chunks[c]]
-
-    def give(self, a, offs):
-        raw, total, _, out = self.arrays[a]
+        for order, at, size in weight_parts(self.rows):
+            rows, route = pl.ds(at, size), Route(axes, order)
+            streams.append((route, lambda o, r=rows, w=route: total.at[w.flat(o), r], lambda f, r=rows: got.at[f, r], out.at[rows], size))
+        self.route = Route(axes, ORDERS[0])
+        self.fold = Fold(streams, send, recv, ranks)
+
+    def pieces(self, c):
+        cols = packed_columns(self.widths)
+        return [(o, a, cols[a]) for o in self.route.all if o[0] == self.ranks[c] for a in range(len(self.raws))]
+
+    def give(self, offs, a, cols):
         f = self.route.flat(offs)
-        return pltpu.make_async_remote_copy(
-            src_ref=raw.at[self.route.target(offs), :, weight_columns(out.shape[1])[1]], dst_ref=total.at[f],
-            send_sem=self.psend.at[a, f], recv_sem=self.precv.at[a, f], device_id={"section": 1 - lax.axis_index("section")},
-            device_id_type=MESH)
-
-    def load(self, a, offs):
-        raw, _, load, out = self.arrays[a]
-        slot = offs[1] * self.route.sizes[2] + offs[2]
-        return pltpu.make_async_copy(raw.at[self.route.target(offs), :, weight_columns(out.shape[1])[0]], load.at[slot],
-                                     self.local.at[a, self.route.flat(offs)])
+        src = self.raws[a].at[self.route.block(offs), :, weight_columns(self.widths[a])[1]]
+        return remote(src, self.total.at[f, :, cols], self.psend.at[a, f], self.precv.at[a, f], {"section": 1 - lax.axis_index("section")})
+
+    def load(self, offs, a, cols):
+        src = self.raws[a].at[self.route.block(offs), :, weight_columns(self.widths[a])[0]]
+        return pltpu.make_async_copy(src, self.held.at[offs[1] * 2 + offs[2], :, cols], self.local.at[a, self.route.flat(offs)])
 
     def begin(self):
-        for c in range(len(self.chunks)):
-            for offs in self.block(c):
-                for a in range(len(self.arrays)):
-                    self.give(a, offs).start()
-                    if c == 0:
-                        self.load(a, offs).start()
+        for c in range(len(self.ranks)):
+            for piece in self.pieces(c):
+                self.give(*piece).start()
+                if c == 0:
+                    self.load(*piece).start()
 
     def step(self, t):
-        if t < len(self.chunks):
-            for a, (_, total, load, out) in enumerate(self.arrays):
-                for offs in self.block(t):
-                    self.load(a, offs).wait()
-                    self.give(a, offs).wait_recv()
-                    here = total.at[self.route.flat(offs)]
-                    add_rows([load.at[offs[1] * self.route.sizes[2] + offs[2]], here], here, out.shape[0])
-            if t + 1 < len(self.chunks):
-                for offs in self.block(t + 1):
-                    for a in range(len(self.arrays)):
-                        self.load(a, offs).start()
+        if t < len(self.ranks):
+            for piece in self.pieces(t):
+                self.load(*piece).wait()
+                self.give(*piece).wait_recv()
+            for offs in self.route.all:
+                if offs[0] == self.ranks[t]:
+                    here = self.total.at[self.route.flat(offs)]
+                    add_rows([self.held.at[offs[1] * 2 + offs[2]], here], here, self.rows)
+            if t + 1 < len(self.ranks):
+                for piece in self.pieces(t + 1):
+                    self.load(*piece).start()
         self.fold.step(t)
 
     def steps(self):
@@ -636,158 +794,114 @@
 
     def end(self):
         self.fold.end()
-        for a in range(len(self.arrays)):
-            for offs in self.route.all:
-                self.give(a, offs).wait_send()
+        for c in range(len(self.ranks)):
+            for piece in self.pieces(c):
+                self.give(*piece).wait_send()
+
+
+def fold_shape(arrays):
+    return jax.ShapeDtypeStruct((arrays[0].shape[1], sum(a.shape[2] // 2 for a in arrays)), jnp.float32)
 
 
 def fold_scratch(arrays, axes):
-    count, dma = arrays[0].shape[0], pltpu.SemaphoreType.DMA
-    half = [(a.shape[1], a.shape[2] // 2) for a in arrays]
-    full = [pltpu.VMEM((count, *h), jnp.bfloat16) for h in half]
-    loads = [pltpu.VMEM((axes[1][1] * axes[2][1], *h), jnp.bfloat16) for h in half]
-    streams = sum(len(weight_parts(rows)) for rows, _ in half)
-    return full + full + loads + [dma((streams, count))] * 2 + [dma((len(arrays), count))] * 3
+    count, dma, block = arrays[0].shape[0], pltpu.SemaphoreType.DMA, fold_shape(arrays).shape
+    blocks = [pltpu.VMEM((n, *block), jnp.bfloat16) for n in (count, count + 4, axes[1][1] * axes[2][1])]
+    return blocks + [dma((len(ORDERS), count + 4))] * 2 + [dma((len(arrays), count))] * 3
 
 
 def closing_kernel(axes, count, *refs):
     refs = list(refs)
     take = lambda n: [refs.pop(0) for _ in range(n)]
-    raws, others = take(count), take(count)
+    raws = take(count)
+    other = take(1)[0]
     first_up, first_down, last_up, last_down, grad_in, last_in = take(6)
     outs = take(count)
     up_out, down_out, edge_out = take(3)
-    sums, gots, loads = take(count), take(count), take(count)
-    sems = take(5)
-    results, given, taken = take(count), take(count), take(count)
+    blocks, sems = take(3), take(5)
+    result, given, taken = take(3)
     own_up, own_down, got_up, got_down, edge_give, edge_got, x_send, x_recv, x_local, h_send, h_recv = take(11)
     sec = lax.axis_index("section")
     partner = {"section": 1 - sec}
     chunks = [axes[0][1] - 1 - c for c in range(axes[0][1])]
     meet(axes, False, True)
-    fold = WeightFold(axes, raws, sums, gots, loads, results, sems, chunks)
+    fold = WeightFold(axes, raws, *blocks, result, sems, chunks)
     fold.begin()
     leading = sec == 0
 
-    def remote(src, dst, n):
-        return pltpu.make_async_remote_copy(src_ref=src, dst_ref=dst, send_sem=x_send.at[n], recv_sem=x_recv.at[n], device_id=partner,
-                                            device_id_type=MESH)
+    def cross(src, dst, n):
+        return remote(src, dst, x_send.at[n], x_recv.at[n], partner)
 
     edge_give[...] = jnp.where(leading, last_in[...], grad_in[...])
-    edge = remote(edge_give, edge_got, 2)
+    edge = cross(edge_give, edge_got, 2)
     edge.start()
     edge_out[sec] = jnp.where(leading, grad_in[...], last_in[...])
 
     @pl.when(leading)
     def _():
-        remote(last_up, got_up, 0).start()
-        remote(last_down, got_down, 1).start()
+        cross(last_up, got_up, 0).start()
+        cross(last_down, got_down, 1).start()
         pltpu.make_async_copy(first_up, own_up, x_local.at[0]).start()
         pltpu.make_async_copy(first_down, own_down, x_local.at[1]).start()
 
     @pl.when(jnp.logical_not(leading))
     def _():
-        remote(first_up, got_up, 0).start()
-        remote(first_down, got_down, 1).start()
+        cross(first_up, got_up, 0).start()
+        cross(first_down, got_down, 1).start()
         pltpu.make_async_copy(last_up, own_up, x_local.at[0]).start()
         pltpu.make_async_copy(last_down, own_down, x_local.at[1]).start()
 
     steps = fold.steps()
     for t in range(steps - 1):
         fold.step(t)
-        if t == 3:
-            for n, (own, got, out, src) in enumerate(((own_up, got_up, up_out, first_up), (own_down, got_down, down_out, first_down))):
+        for n, (own, got, out, src) in enumerate(((own_up, got_up, up_out, first_up), (own_down, got_down, down_out, first_down))):
+            if t == 2:
                 pltpu.make_async_copy(src, own, x_local.at[n]).wait()
-                remote(src, got, n).wait_recv()
-                add_rows([own, got], own, own.shape[0], 8)
+                cross(src, got, n).wait_recv()
+            if t in (2, 3):
+                size = own.shape[0] // 2
+                rows = pl.ds((t - 2) * size, size)
+                add_rows([own.at[rows], got.at[rows]], own.at[rows], size, 8)
+            if t == 3:
                 pltpu.make_async_copy(own, out, x_local.at[n]).start()
+        if t == 2:
             edge.wait_recv()
             edge_out[1 - sec] = edge_got[...]
+    assert steps > 4
     fold.step(steps - 1)
-    hands = []
+    given[...] = jnp.where(leading, other[...], result[...])
+    hand = remote(given, taken, h_send.at[0], h_recv.at[0], partner)
+    hand.start()
+    packed = packed_columns(fold.widths)
     for a in range(count):
-        half = results[a].shape[1]
-        mine, theirs = weight_columns(half)
-        given[a][...] = jnp.where(leading, others[a][...], results[a][...])
-        c = pltpu.make_async_remote_copy(src_ref=given[a], dst_ref=taken[a], send_sem=h_send.at[a], recv_sem=h_recv.at[a],
-                                         device_id=partner, device_id_type=MESH)
-        c.start()
-        hands.append(c)
-        outs[a][:, mine] = jnp.where(leading, results[a][...], others[a][...])
+        outs[a][:, weight_columns(fold.widths[a])[0]] = jnp.where(leading, result[:, packed[a]], other[:, packed[a]])
     fold.end()
     edge.wait_send()
     for n, (own, got, out, src) in enumerate(((own_up, got_up, up_out, first_up), (own_down, got_down, down_out, first_down))):
-        remote(src, got, n).wait_send()
+        cross(src, got, n).wait_send()
         pltpu.make_async_copy(own, out, x_local.at[n]).wait()
+    hand.wait()
     for a in range(count):
-        hands[a].wait()
-        outs[a][:, weight_columns(results[a].shape[1])[1]] = taken[a][...]
-
-
-def closing(raws, others, first, last, grad, final, count, cid):
+        outs[a][:, weight_columns(fold.widths[a])[1]] = taken[:, packed[a]]
+
+
+def closing(raws, other, first, last, grad, final, count, cid):
     axes, n = torus_axes(count), len(raws)
     vmem, anywhere = pl.BlockSpec(memory_space=pltpu.VMEM), pl.BlockSpec(memory_space=pl.ANY)
     dma, f32 = pltpu.SemaphoreType.DMA, jnp.float32
-    halves = [pltpu.VMEM((a.shape[1], a.shape[2] // 2), f32) for a in raws]
+    half = pltpu.VMEM(fold_shape(raws).shape, f32)
     experts = [pltpu.VMEM(w.shape, f32) for w in first]
     block = pltpu.VMEM(grad.shape, grad.dtype)
     return pl.pallas_call(
         functools.partial(closing_kernel, axes, n),
         out_shape=[jax.ShapeDtypeStruct(a.shape[1:], f32) for a in raws] + [jax.ShapeDtypeStruct(w.shape, f32) for w in first]
         + [jax.ShapeDtypeStruct((2, *grad.shape), grad.dtype)],
-        in_specs=[anywhere] * n + [vmem] * n + [anywhere] * 4 + [vmem] * 2,
+        in_specs=[anywhere] * n + [vmem] + [anywhere] * 4 + [vmem] * 2,
         out_specs=[vmem] * n + [anywhere] * 2 + [vmem],
-        scratch_shapes=fold_scratch(raws, axes) + halves * 3 + experts * 2 + [block, block, dma((3,)), dma((3,)), dma((2,)), dma((n,)), dma((n,))],
+        scratch_shapes=fold_scratch(raws, axes) + [half] * 3 + experts * 2 + [block, block, dma((3,)), dma((3,)), dma((2,)), dma((1,)), dma((1,))],
         compiler_params=pltpu.CompilerParams(collective_id=cid, has_side_effects=True, vmem_limit_bytes=VMEM_BYTES),
         cost_estimate=pl.CostEstimate(flops=0, bytes_accessed=100_000_000, transcendentals=0),
         name="closing",
-    )(*raws, *others, *first, *last, grad, final)
-
-
-def weight_spread_kernel(axes, count, *refs):
-    ins, outs = refs[:count], refs[count : 2 * count]
-    send, recv, psend, precv, local = refs[2 * count :]
-    meet(axes, False, True)
-    spread = Spread(weight_streams(axes, ins, outs), send, recv, psend, precv)
-    spread.step(0)
-    keep = own_copies(ins, outs, local)
-    for t in range(1, axes[0][1] + 2):
-        spread.step(t)
-    spread.end()
-    for c in keep:
-        c.wait()
-
-
-def own_copies(ins, outs, local):
-    keep = []
-    me, sec = lax.axis_index("dp"), lax.axis_index("section")
-    for a, (own, full) in enumerate(zip(ins, outs)):
-        half = own.shape[1]
-        c = pltpu.make_async_copy(own, full.at[me, :, pl.ds(pl.multiple_of(sec * half, 128), half)], local.at[a])
-        c.start()
-        keep.append(c)
-    return keep
-
-
-def weight_shapes(arrays, count):
-    return [jax.ShapeDtypeStruct((count, a.shape[0], 2 * a.shape[1]), a.dtype) for a in arrays]
-
-
-def weight_sems(arrays, count):
-    sem = pltpu.SemaphoreType.DMA((weight_stream_count(arrays), count))
-    return [sem] * 4 + [pltpu.SemaphoreType.DMA((len(arrays),))]
-
-
-def weight_spread(arrays, count, cid):
-    return pl.pallas_call(
-        functools.partial(weight_spread_kernel, torus_axes(count), len(arrays)),
-        out_shape=weight_shapes(arrays, count),
-        in_specs=[pl.BlockSpec(memory_space=pltpu.VMEM)] * len(arrays),
-        out_specs=[pl.BlockSpec(memory_space=pl.ANY)] * len(arrays),
-        scratch_shapes=weight_sems(arrays, count),
-        compiler_params=pltpu.CompilerParams(collective_id=cid, has_side_effects=True),
-        name="weight_spread",
-    )(*arrays)
+    )(*raws, other, *first, *last, grad, final)
 
 
 def mixture_kernel(mode, axes, count, layer, extra, folded, *refs):
@@ -796,14 +910,14 @@
     take = lambda n: [refs.pop(0) for _ in range(n)]
     mask_ref, router_ref, up_own, up_other, down_own, down_other, x_in = take(7)
     g_in = take(1)[0] if back else None
-    next_in = take(extra)
+    next_in = take(1)[0] if extra else None
     raws = take(folded)
     mixed_out = take(1)[0] if fore else None
     saved_out = take(1)[0] if mode == "f" else None
     if back:
         grad_out, chance_out, up_grad_out, down_grad_out = take(4)
     next_out = take(extra)
-    raw_outs = take(folded)
+    raw_out = take(1)[0] if folded else None
     up, down, xg, gates_at, weight_at, local = take(6)
     ag_send, ag_recv, rs_send, rs_recv = take(4)
     gathers, folds = [], []
@@ -829,16 +943,16 @@
     for share, got, out in folds:
         for order, at, size in TOKEN_PARTS:
             rows, route = pl.ds(at, size), Route(axes, order)
-            fold_streams.append((route, lambda o, a=share, r=rows, w=route: a.at[w.target(o), r], lambda f, g=got, r=rows: g.at[f, r],
+            fold_streams.append((route, lambda o, a=share, r=rows, w=route: a.at[w.block(o), r], lambda f, g=got, r=rows: g.at[f, r],
                                  out.at[rows], size))
     spread = Spread(spread_streams, ag_send, ag_recv)
-    fold = Fold(fold_streams, rs_send, rs_recv, [3, 2, 1, 0])
+    ranks = [3, 2, 1, 0]
+    fold = Fold(fold_streams, rs_send, rs_recv, ranks)
     spread.step(0)
     if extra:
-        w_send, w_recv, w_psend, w_precv, w_local = take(5)
-        other = Spread(weight_streams(axes, next_in, next_out), w_send, w_recv, w_psend, w_precv)
+        other = WeightSpread(axes, next_in, take(1)[0], next_out, take(5))
     if folded:
-        aside = WeightFold(axes, raws, take(folded), take(folded), take(folded), raw_outs, take(5), [3, 2, 1, 0])
+        aside = WeightFold(axes, raws, *take(3), raw_out, take(5), ranks)
         aside.begin()
 
     @pl.when(sec == layer)
@@ -873,7 +987,7 @@
         lane = lax.broadcasted_iota(jnp.int32, (TILE, router_ref.shape[1]), 1)
         chance = jnp.where(lane < count, jnp.exp(dot(x, router_ref[...])), 0.0)
         total = jnp.sum(chance, axis=1, keepdims=True)
-        named = mask_ref[blocks].reshape(TILE, 1)
+        named = mask_ref[blocks].reshape(TILE, 1).astype(jnp.float32)
         weight = jnp.sum(jnp.where(lane == me, chance, 0.0), axis=1, keepdims=True) / total * named
         weight_at[...] = jnp.where(lane[:, :128] == 0, weight, named)
 
@@ -932,33 +1046,19 @@
             for b in range(TILE // ROWS):
                 chance_row[b0 + b] = row[:, b * ROWS : (b + 1) * ROWS]
 
-    digit = lax.div(me, axes[0][0])
+    for t in range(1, SPREAD_STEPS):
+        spread.step(t)
+        if folded:
+            aside.step(t - 1)
+    if extra:
+        other.step(0)
+    route = Route(axes, ORDERS[0])
+    sources = [route.plane(k) for k in ranks]
 
     def chunk(c, _):
-        k = lax.rem(c + 1, n0)
-
-        @pl.when(c == 0)
-        def _():
-            for t in range(1, 4):
-                spread.step(t)
-                if folded and t < 3:
-                    aside.step(t - 1)
-
-        @pl.when(c == 1)
-        def _():
-            spread.step(4)
-            if extra:
-                other.step(0)
-            if folded:
-                aside.step(2)
-
-        @pl.when(c == 2)
-        def _():
-            spread.step(5)
-            if folded:
-                aside.step(3)
-
-        source = lax.rem(digit - k + n0, n0)
+        source = sources[0]
+        for v in range(1, n0):
+            source = jnp.where(c == v, sources[v], source)
 
         def step(q, _):
             if "tile" not in SKIP:
@@ -970,26 +1070,25 @@
             @pl.when(c == v)
             def _(v=v):
                 fold.step(v)
-                if extra and v >= 2:
-                    other.step(v - 1)
+                if extra and v:
+                    other.step(v)
+                if folded:
+                    aside.step(SPREAD_STEPS - 1 + v)
         return 0
 
     lax.fori_loop(0, n0, chunk, 0)
     if back:
-        route = Route(axes, (0, 1, 2))
-
-        def chance_copy(offs):
-            f = route.flat(offs)
-            return pltpu.make_async_remote_copy(
-                src_ref=chance_row.at[route.target(offs)], dst_ref=chance_got.at[me], send_sem=c_send.at[f], recv_sem=c_recv.at[f],
-                device_id={"dp": route.target(offs)}, device_id_type=MESH)
+
+        def chance_copy(offs, sender):
+            block = route.block(offs)
+            return remote(chance_row.at[block], chance_got.at[sender], c_send.at[route.flat(offs)], c_recv.at[sender], {"dp": block})
 
         for offs in route.others:
-            chance_copy(offs).start()
+            chance_copy(offs, me).start()
         chance_got[me] = chance_row[me]
 
         def up_piece(n):
-            return pltpu.make_async_copy(up_sum.at[n % 2], up_grad_out.at[pl.ds(n * PIECE, PIECE)], out_sem.at[0, n % 2])
+            return pltpu.make_async_copy(up_sum.at[0], up_grad_out.at[pl.ds(n * PIECE, PIECE)], out_sem.at[0, 0])
 
         def down_piece(n):
             return pltpu.make_async_copy(down_sum.at[0], down_grad_out.at[pl.ds(n * PIECE, PIECE)], out_sem.at[1, 0])
@@ -998,10 +1097,10 @@
 
         def gradient(n):
             if n < ups:
-                if n >= 2:
-                    up_piece(n - 2).wait()
+                if n:
+                    up_piece(n - 1).wait()
                 left = xg[:, :, n * PIECE : (n + 1) * PIECE].reshape(count * ROWS, PIECE)
-                up_sum[n % 2] = contract(left, ggu_at[...], (0, 0))
+                up_sum[0] = contract(left, ggu_at[...], (0, 0))
                 up_piece(n).start()
             else:
                 n -= ups
@@ -1016,7 +1115,6 @@
     if saved_out is not None:
         save = pltpu.make_async_copy(xg, saved_out, local.at[2])
         save.start()
-    keep = own_copies(next_in, next_out, w_local) if extra else []
     last = fold.steps()
     for t in range(n0, last):
         share = -(-len(work) // (last - t))
@@ -1026,33 +1124,30 @@
                 gradient(n)
         fold.step(t)
         if extra:
-            other.step(t - 1)
+            other.step(t)
         if folded:
-            aside.step(t)
+            aside.step(SPREAD_STEPS - 1 + t)
     if folded:
-        assert aside.steps() == last
+        assert aside.steps() <= SPREAD_STEPS - 1 + last
         aside.end()
     if extra:
-        for t in range(last - 1, n0 + 2):
-            other.step(t)
+        assert last >= SPREAD_STEPS
         other.end()
-        for c in keep:
-            c.wait()
     spread.end()
     fold.end()
     if back:
-        for n in range(max(0, ups - 2), ups) if "grad" not in SKIP else ():
+        for n in range(ups - 1, ups) if "grad" not in SKIP else ():
             up_piece(n).wait()
         for n in range(downs - 1, downs) if "grad" not in SKIP else ():
             down_piece(n).wait()
         for offs in route.others:
-            chance_copy(offs).wait()
+            chance_copy(offs, route.block(offs)).wait()
         chance_out[...] = chance_got[...]
     if saved_out is not None:
         save.wait()
 
 
-def mixture_call(mode, count, layer, cid, mask, router, expert, partner, x, g=None, following=(), summed=()):
+def mixture_call(mode, count, layer, cid, mask, router, expert, partner, x, g=None, following=None, widths=(), summed=()):
     axes = torus_axes(count)
     fore, back = "f" in mode, "b" in mode
     vmem, anywhere = pl.BlockSpec(memory_space=pltpu.VMEM), pl.BlockSpec(memory_space=pl.ANY)
@@ -1061,8 +1156,8 @@
     if back:
         args.append(g)
         in_specs.append(vmem)
-    args += list(following) + list(summed)
-    in_specs += [vmem] * len(following) + [anywhere] * len(summed)
+    args += ([following] if widths else []) + list(summed)
+    in_specs += ([vmem] if widths else []) + [anywhere] * len(summed)
     whole = (count, ROWS, MODEL_WIDTH)
     out_shape, out_specs = [], []
     block = jax.ShapeDtypeStruct((ROWS, MODEL_WIDTH), jnp.float32)
@@ -1076,33 +1171,37 @@
         out_shape += [block, jax.ShapeDtypeStruct((count, 8, ROWS), jnp.float32)]
         out_shape += [jax.ShapeDtypeStruct(w.shape, jnp.float32) for w in expert]
         out_specs += [vmem, vmem, anywhere, anywhere]
-    out_shape += weight_shapes(following, count)
-    out_specs += [anywhere] * len(following) + [vmem] * len(summed)
-    out_shape += [jax.ShapeDtypeStruct((a.shape[1], a.shape[2] // 2), jnp.float32) for a in summed]
+    if widths:
+        out_shape += weight_shapes(following, widths, count)
+        out_specs += [anywhere] * len(widths)
+    if summed:
+        out_shape.append(fold_shape(summed))
+        out_specs.append(vmem)
     dma = pltpu.SemaphoreType.DMA
     scratch = [pltpu.VMEM(expert[0].shape, jnp.bfloat16), pltpu.VMEM(expert[1].shape, jnp.bfloat16), pltpu.VMEM(whole, jnp.bfloat16),
                pltpu.VMEM((TILE, 2 * FFE), jnp.float32), pltpu.VMEM((TILE, 128), jnp.float32), dma((3,))]
     parts = len(TOKEN_PARTS)
     ag, rs = parts * (1 if mode == "b" else fore + back), parts * (fore + back)
-    scratch += [dma((ag, count)), dma((ag, count)), dma((rs, count)), dma((rs, count))]
+    scratch += [dma((ag, count + 4)), dma((ag, count + 4)), dma((rs, count + 4)), dma((rs, count + 4))]
     blocks = pltpu.VMEM(whole, jnp.bfloat16)
+    arrivals = pltpu.VMEM((count + 4, *whole[1:]), jnp.bfloat16)
     low = lambda rows, width: pltpu.VMEM((rows, width), jnp.bfloat16)
     if fore:
-        scratch += [blocks, blocks, low(TILE, FFE)]
+        scratch += [blocks, arrivals, low(TILE, FFE)]
     if back:
-        scratch += [blocks, blocks, blocks, pltpu.VMEM((TILE, FFE), jnp.float32),
+        scratch += [blocks, blocks, arrivals, pltpu.VMEM((TILE, FFE), jnp.float32),
                     low(count * ROWS, 2 * FFE), low(count * ROWS, FFE), low(TILE, FFE), low(TILE, FFE),
-                    pltpu.VMEM((2, PIECE, 2 * FFE), jnp.float32), pltpu.VMEM((1, PIECE, MODEL_WIDTH), jnp.float32),
+                    pltpu.VMEM((1, PIECE, 2 * FFE), jnp.float32), pltpu.VMEM((1, PIECE, MODEL_WIDTH), jnp.float32),
                     pltpu.VMEM((count, 8, ROWS), jnp.float32), pltpu.VMEM((count, 8, ROWS), jnp.float32), dma((count,)), dma((count,)),
                     dma((2, 2))]
-    if following:
-        scratch += weight_sems(following, count)
+    if widths:
+        scratch += weight_scratch(following, widths, count)
     if summed:
         scratch += fold_scratch(summed, axes)
     rows = count * ROWS
     flops = rows * 6 * MODEL_WIDTH * FFE * (fore + 2 * back + (mode == "b"))
     return pl.pallas_call(
-        functools.partial(mixture_kernel, mode, axes, count, layer, len(following), len(summed)),
+        functools.partial(mixture_kernel, mode, axes, count, layer, len(widths), len(summed)),
         out_shape=out_shape,
         in_specs=in_specs,
         out_specs=out_specs,
@@ -1350,7 +1449,7 @@
         if not fused:
             arrays = gather_all(layer_parts(layer), count, 2, pair=True)
         elif layer == 0:
-            arrays = weight_spread(layer_parts(layer), count, 2)
+            arrays = weight_spread(packs[layer], widths, count, 2)
         got, mask = layer_weights(arrays)
         weights.append(got)
         masks.append(mask)
@@ -1358,11 +1457,11 @@
         if not fused:
             mixed, kept_mixture = mixture_forward(normed_two, got[2], mask, experts[layer], count, me)
         else:
-            named = mask.astype(jnp.float32).reshape(count, DEVICE_ROWS, 1)
+            named = mask.astype(jnp.bfloat16).reshape(count, DEVICE_ROWS, 1)
             call = lambda mode, cid, *data, **more: mixture_call(
                 mode, count, layer, cid, named, routers[layer], own_expert, partner_expert, *data, **more)
             if layer < layers - 1:
-                mixed, everyone, *arrays = call("f", 4, normed_two, following=layer_parts(layer + 1))
+                mixed, everyone, *arrays = call("f", 4, normed_two, following=packs[layer + 1], widths=tuple(widths))
                 kept_mixture = (named, everyone)
             else:
                 mixed, *kept_mixture = call("fb", 5, normed_two, micro(cotangent, 0))
@@ -1381,8 +1480,8 @@
                 kept_mixture = mixture_call("b", count, layer, 6, named, routers[layer], own_expert, partner_expert, everyone, grad,
                                             summed=packs[layer + 1])
             mixed, rows, grad_up, grad_down, *more = kept_mixture
-            if layer < layers - 1:
-                shares[layer + 1] = more
+            if more:
+                shares[layer + 1] = more[0]
             grad_chance = rows[:, 0].T
         expert_grads[layer] = (grad_up, grad_down)
         grad_hidden, parts = front_backward(grad.astype(jnp.float32), mixed, grad_chance, kept, place, weights[layer])

time: 908 us -> 832 us (0.916)
  Pallas kernels: 739 us -> 670 us
    pallas_call x3, Pallas kernels: 582 us -> 532 us  [mixture_call(): pl.pallas_call(functools.partial(mixture_kernel, mode, axes, count, layer...]
    pallas_call x1, Pallas kernels: 73.2 us -> 57.5 us  [weight_spread(): pl.pallas_call(functools.partial(weight_spread_kernel, torus_axes(count),...]
    unnamed x163 -> x155, local copies, waits for them, and re-layouts: 20 us -> 22.9 us
  transfers between devices with their start and end apart: 3 -> 3, of which waited for: 0 -> 0; matrix products, arithmetic and copies ran while one was open for 4% -> 4% of each run, Pallas kernels for 8% -> 7%
where the time goes in v4:
time: 832 us; the launch traced here: 820 us
  Pallas kernels  670 us (81%)
  matrix products  77.9 us (9%)
  local copies, waits for them, and re-layouts  46 us (6%)
  other arithmetic  24 us (3%)
    pallas_call x3, Pallas kernels, mixture_call(): pl.pallas_call(functools.partial(mixture_kernel, mode, axes, count, layer...  532 us
    pallas_call x1, Pallas kernels, closing(): pl.pallas_call(functools.partial(closing_kernel, axes, n), out_shape=[jax...  80.5 us
    pallas_call x1, Pallas kernels, weight_spread(): pl.pallas_call(functools.partial(weight_spread_kernel, torus_axes(count),...  57.5 us
    dot_general x6, matrix products, dot_columns(): lax.dot_general(left, right, (((1,), (1,)), ((), ())), preferred_element_...  24.1 us
    unnamed x155, local copies, waits for them, and re-layouts  22.9 us
    dot_general x6, matrix products, dot_rows(): lax.dot_general(left, right, (((0,), (0,)), ((), ())), preferred_element_...  19.6 us
    dot_general x6, matrix products, dot(): return jnp.dot(left, right, preferred_element_type=jnp.float32)  18.5 us
  transfers between devices with their start and end apart: 3, of which 0 were waited for; matrix products, arithmetic and copies ran while one was open for 4% of the time, Pallas kernels for 7%

profile of v4, /device:TPU:28, one launch (start us, length us, event | category | flops | bytes accessed | tf_op | source)
XLA Modules:
  0.0 820.5 jit_solution(10836181838296604931)
XLA Ops:
  7.8 57.5 %weight_spread.1 = (bf16[16,96,2560]{2,1,0:T(8,128)(2,1)}, bf16[16,96,1536]{2,1,0:T(8,128)(2,1)}, bf16[16,96,256]{2,1,0:T(8,128)(2,1)}) custom-call(bf16[96,2176]{1,0:T(8,128)(2,1)} %get-tuple-element.113.refs_0_), custom_call_target="tpu_custom_call" | custom-call | tf_op jit(solution)/shard_map/weight_spread/pallas_call | solution.py:734
  65.3 1.6 convert_reduce_fusion.2
  67.0 4.5 fusion.45
  73.3 2.3 copy.158
  75.6 1.8 copy.157
  82.3 2.3 bitcast_select_fusion.1
  88.2 2.3 convolution_convert_fusion.9
  90.5 3.4 multiply_reduce_fusion.5
  96.3 151.3 %mixture_f.1 = (f32[128,1536]{1,0:T(8,128)}, bf16[16,128,1536]{2,1,0:T(8,128)(2,1)}, bf16[16,96,2560]{2,1,0:T(8,128)(2,1)}, bf16[16,96,1536]{2,1,0:T(8,128)(2,1)}, bf16[16,96,256]{2,1,0:T(8,128)(2,1)}) custom-call(bf16[16,128,1]{2,1,0:T(8,128)(2,1)} %copy.163.refs_0_, bf16[1536,128]{1,0:T(8,128)(2,1)} %slice.192.refs_1_, bf16[1536,1024]{1,0:T(8,128)(2,1)} %bitcast.320, ...), custom_call_target="tpu_custom_call" | custom-call | flops 9663676416 | bytes 12582912 | tf_op jit(solution)/shard_map/mixture_f/pallas_call | solution.py:1203
  247.6 1.6 fusion.39
  249.7 4.5 fusion.71
  259.1 2.3 convolution_convert_fusion.8
  261.4 3.4 multiply_reduce_fusion.4
  270.1 213.0 %mixture_fb.1 = (f32[128,1536]{1,0:T(8,128)}, f32[128,1536]{1,0:T(8,128)}, f32[16,8,128]{2,1,0:T(8,128)}, f32[1536,1024]{1,0:T(8,128)}, f32[512,1536]{1,0:T(8,128)}) custom-call(bf16[16,128,1]{2,1,0:T(8,128)(2,1)} %copy.170.refs_0_, bf16[1536,128]{1,0:T(8,128)(2,1)} %slice.204.refs_1_, bf16[1536,1024]{1,0:T(8,128)(2,1)} %bitcast.321, ...), custom_call_target="tpu_custom_call" | custom-call | flops 28991029248 | bytes 12582912 | tf_op jit(solution)/shard_map/mixture_fb/pallas_call | solution.py:1203
  486.7 1.9 multiply_reduce_fusion.2
  489.8 4.0 convolution_convert_fusion.5
  495.5 1.7 fusion.3
  499.6 2.4 fusion.14
  502.0 3.6 convolution_convert_fusion.3
  506.6 6.1 fusion.38
  512.6 5.5 convolution_convert_fusion.1
  521.0 167.4 %mixture_b.1 = (f32[128,1536]{1,0:T(8,128)}, f32[16,8,128]{2,1,0:T(8,128)}, f32[1536,1024]{1,0:T(8,128)}, f32[512,1536]{1,0:T(8,128)}, f32[96,2176]{1,0:T(8,128)}) custom-call(bf16[16,128,1]{2,1,0:T(8,128)(2,1)} %copy.163.refs_0_, bf16[1536,128]{1,0:T(8,128)(2,1)} %slice.192.refs_1_, bf16[1536,1024]{1,0:T(8,128)(2,1)} %bitcast.322, ...), custom_call_target="tpu_custom_call" | custom-call | flops 28991029248 | bytes 12582912 | tf_op jit(solution)/shard_map/mixture_b/pallas_call | solution.py:1203
  690.8 2.0 multiply_reduce_fusion
  693.1 4.0 convolution_convert_fusion.4
  702.6 2.4 fusion.15
  705.3 3.6 convolution_convert_fusion.2
  710.0 6.1 fusion.24
  716.0 5.4 convolution_convert_fusion
  724.2 80.5 %closing.1 = (f32[96,2560]{1,0:T(8,128)}, f32[96,1536]{1,0:T(8,128)}, f32[96,256]{1,0:T(8,128)}, f32[1536,1024]{1,0:T(8,128)}, f32[512,1536]{1,0:T(8,128)}, /*index=5*/bf16[2,128,1536]{2,1,0:T(8,128)(2,1)}) custom-call(bf16[16,96,2560]{2,1,0:T(8,128)(2,1)} %bitcast.238, bf16[16,96,1536]{2,1,0:T(8,128)(2,1)} %bitcast.239, ...), custom_call_target="tpu_custom_call" | custom-call | bytes 100000000 | tf_op jit(solution)/shard_map/closing/pallas_call | solution.py:894
  807.9 2.1 copy.210
  811.8 6.8 copy.213
  818.6 1.7 copy.214
  (273 shorter events, 59.4 us)
Async XLA Ops:
  0.7 3.9 copy-start.8
  0.7 4.1 copy-start.69
  0.7 5.3 copy-start.33
  3.9 2.9 collective-permute-start
  4.0 92.3 %collective-permute-start.1 = (bf16[1536,1024]{1,0:T(8,128)(2,1)}, bf16[1536,1024]{1,0:T(8,128)(2,1)}, u32[]{:S(2)}, u32[]{:S(2)}) collective-permute-start(bf16[1536,1024]{1,0:T(8,128)(2,1)} %bitcast.319), channel_id=1, source_target_pairs={{0,16},{16,0},{1,17},{17,1},{2,18},{18,2},{3,19},{19,3},{4,20},{20... | collective-permute-start | bytes 9437192 | tf_op jit(solution)/shard_map/ppermute | solution.py:1215
  4.5 91.8 %collective-permute-start.2 = (bf16[512,1536]{1,0:T(8,128)(2,1)}, bf16[512,1536]{1,0:T(8,128)(2,1)}, u32[]{:S(2)}, u32[]{:S(2)}) collective-permute-start(bf16[512,1536]{1,0:T(8,128)(2,1)} %bitcast.323), channel_id=1, source_target_pairs={{0,16},{16,0},{1,17},{17,1},{2,18},{18,2},{3,19},{19,3},{4,20},{20... | collective-permute-start | bytes 4718600 | tf_op jit(solution)/shard_map/ppermute | solution.py:1215
  6.0 75.0 %copy-start.40 = (f32[128,32]{0,1:T(8,128)}, f32[128,32]{0,1:T(8,128)S(1)}, u32[]{:S(2)}) copy-start(f32[128,32]{0,1:T(8,128)S(1)} %get-tuple-element.139) | copy-start | bytes 49156
  6.0 60.9 %copy-start.57 = (f32[128]{0:T(128)}, f32[128]{0:T(128)S(1)}, u32[]{:S(2)}) copy-start(f32[128]{0:T(128)S(1)} %add_rsqrt_fusion.3) | copy-start | bytes 1540
  66.9 4.5 copy-start.42
  66.9 27.0 %copy-start.52 = (f32[1536]{0:T(1024)}, f32[1536]{0:T(1024)S(1)}, u32[]{:S(2)}) copy-start(f32[1536]{0:T(1024)S(1)} %get-tuple-element.106) | copy-start | bytes 18436
  80.9 3.7 copy-start.44
  81.0 3.6 copy-start.46
  82.2 3.8 copy-start.24
  82.3 3.8 copy-start.26
  87.1 3.4 copy-start.36
  90.5 3.4 copy-start.19
  249.3 12.2 %copy-start.2 = (bf16[128,1536]{1,0:T(8,128)(2,1)}, bf16[128,1536]{1,0:T(8,128)(2,1)S(1)}, u32[]{:S(2)}) copy-start(bf16[128,1536]{1,0:T(8,128)(2,1)S(1)} %get-tuple-element.111) | copy-start | bytes 1179652
  249.3 5.0 copy-start.59
  249.7 15.1 %copy-start.54 = (f32[1536]{0:T(1024)}, f32[1536]{0:T(1024)S(1)}, u32[]{:S(2)}) copy-start(f32[1536]{0:T(1024)S(1)} %get-tuple-element.104) | copy-start | bytes 18436
  257.4 4.0 copy-start.48
  257.5 3.9 copy-start.38
  261.4 3.4 copy-start.17
  264.8 3.9 copy-start.64
  489.8 4.3 copy-start.39
  520.9 169.9 %copy-start.53 = (f32[1536]{0:T(1024)S(1)}, f32[1536]{0:T(1024)}, u32[]{:S(2)}) copy-start(f32[1536]{0:T(1024)} %copy-done.52) | copy-start | bytes 18436
  688.4 4.4 copy-start.1
  688.4 4.4 copy-start.15
  688.4 4.4 copy-start.22
  688.4 4.4 copy-start.63
  693.1 4.3 copy-start.37
  804.8 5.3 copy-start.23
  811.8 6.8 copy-start.14
  (44 other events, 80.7 us)

commit v5 on v4

--- a/solution.py
+++ b/solution.py
@@ -517,7 +517,7 @@
 
 def add_rows(sources, dest, rows, step=16):
     cols = dest.shape[-1]
-    width = next(w for w in (640, 512, 384, 128) if cols % w == 0)
+    width = 768 if cols % 768 == 0 else cols
 
     def one(r, _):
         at = pl.ds(pl.multiple_of(r * step, step), step)
@@ -854,19 +854,19 @@
     for t in range(steps - 1):
         fold.step(t)
         for n, (own, got, out, src) in enumerate(((own_up, got_up, up_out, first_up), (own_down, got_down, down_out, first_down))):
-            if t == 2:
+            if t == 3:
                 pltpu.make_async_copy(src, own, x_local.at[n]).wait()
                 cross(src, got, n).wait_recv()
-            if t in (2, 3):
+            if t in (3, 4):
                 size = own.shape[0] // 2
-                rows = pl.ds((t - 2) * size, size)
+                rows = pl.ds((t - 3) * size, size)
                 add_rows([own.at[rows], got.at[rows]], own.at[rows], size, 8)
-            if t == 3:
+            if t == 4:
                 pltpu.make_async_copy(own, out, x_local.at[n]).start()
         if t == 2:
             edge.wait_recv()
             edge_out[1 - sec] = edge_got[...]
-    assert steps > 4
+    assert steps > 5
     fold.step(steps - 1)
     given[...] = jnp.where(leading, other[...], result[...])
     hand = remote(given, taken, h_send.at[0], h_recv.at[0], partner)
@@ -987,9 +987,10 @@
         lane = lax.broadcasted_iota(jnp.int32, (TILE, router_ref.shape[1]), 1)
         chance = jnp.where(lane < count, jnp.exp(dot(x, router_ref[...])), 0.0)
         total = jnp.sum(chance, axis=1, keepdims=True)
-        named = mask_ref[blocks].reshape(TILE, 1).astype(jnp.float32)
-        weight = jnp.sum(jnp.where(lane == me, chance, 0.0), axis=1, keepdims=True) / total * named
-        weight_at[...] = jnp.where(lane[:, :128] == 0, weight, named)
+        ones = jnp.ones((8, 128), jnp.bfloat16)
+        named = jnp.concatenate([contract(mask_ref[b0 + b], ones, (0, 0)) for b in range(TILE // ROWS)], axis=0)
+        weight = jnp.sum(jnp.where(lane == me, chance, 0.0), axis=1, keepdims=True) / total
+        weight_at[...] = jnp.where(lane[:, :128] == 0, weight * named, named)
 
         def gate_step(n, _):
             gates_at[:, span(n)] = dot(xg[blocks].reshape(TILE, MODEL_WIDTH), up[:, span(n)])
@@ -1402,7 +1403,14 @@
     codes = routes[0].astype(jnp.bfloat16).reshape(-1)
     code_count = codes.shape[0]
     codes = jnp.pad(codes, (0, -code_count % shard)).reshape(shard, -1)
-    small = small_halves(shard, router_weight[0], gains, codes)
+    fused = count * DEVICE_ROWS <= CHUNK_ROWS
+    if fused:
+        member = jnp.any(routes[0][:, None] == jnp.arange(count, dtype=jnp.int32)[None, :, None, None], axis=-1)
+        member = member.astype(jnp.bfloat16).reshape(-1, DEVICE_ROWS)
+        small = small_halves(shard, jnp.concatenate([router_weight[0], gains], axis=1), gains[:, :0], gains[:, :0])
+        small = (small[0], jnp.pad(member, ((0, shard - member.shape[0]), (0, 0))))
+    else:
+        small = small_halves(shard, router_weight[0], gains, codes)
     small_width = small[0].shape[1]
     halves = [
         (combined_weight[0, :, : combined_weight.shape[2] // 2], combined_weight[0, :, combined_weight.shape[2] // 2 :]),
@@ -1415,7 +1423,6 @@
     packs = [jnp.where(leading, mine, given), jnp.where(leading, given, mine)]
     partner_expert = tuple(swapped(w[0, 0]) for w in (expert_gate_up, expert_down))
     own_expert = (expert_gate_up[0, 0], expert_down[0, 0])
-    fused = count * DEVICE_ROWS <= CHUNK_ROWS
     experts, routers = [], []
     for layer in range(0 if fused else layers):
         keep = sec == layer
@@ -1430,9 +1437,13 @@
 
     def layer_weights(arrays):
         joint, output, tail = [a.reshape(MODEL_WIDTH, -1) for a in arrays]
-        second = tail[:, small_width:]
-        weights = (joint, output, tail[:, : router_weight.shape[2]], second[:, 0].astype(jnp.float32), second[:, 1].astype(jnp.float32))
+        experts_wide = router_weight.shape[2]
+        second = tail[:, small_width:] if not fused else tail[:, experts_wide:]
+        weights = (joint, output, tail[:, :experts_wide], second[:, 0].astype(jnp.float32), second[:, 1].astype(jnp.float32))
         routers.append(tail[:, :small_width])
+        if fused:
+            rows = lax.dynamic_slice(arrays[2], (0, sec * count + me, small_width), (count, 1, DEVICE_ROWS))
+            return weights, jnp.pad(rows, ((0, 0), (0, 7), (0, 0)))
         code = second[:, 2 : 2 + codes.shape[1]].reshape(count, -1)[:, :code_count].reshape(count, -1, DEVICE_ROWS, TOPK)
         named = lax.dynamic_index_in_dim(code, sec, 1, keepdims=False).reshape(count * DEVICE_ROWS, TOPK)
         mask = jnp.any(named == me.astype(jnp.bfloat16), axis=-1, keepdims=True)
@@ -1457,7 +1468,7 @@
         if not fused:
             mixed, kept_mixture = mixture_forward(normed_two, got[2], mask, experts[layer], count, me)
         else:
-            named = mask.astype(jnp.bfloat16).reshape(count, DEVICE_ROWS, 1)
+            named = mask
             call = lambda mode, cid, *data, **more: mixture_call(
                 mode, count, layer, cid, named, routers[layer], own_expert, partner_expert, *data, **more)
             if layer < layers - 1:

time: 832 us -> 808 us (0.971)
  Pallas kernels: 670 us -> 657 us
  local copies, waits for them, and re-layouts: 46 us -> 35.4 us
    unnamed x155 -> x154, local copies, waits for them, and re-layouts: 22.9 us -> 22.2 us
  transfers between devices with their start and end apart: 3 -> 3, of which waited for: 0 -> 0; matrix products, arithmetic and copies ran while one was open for 4% -> 3% of each run, Pallas kernels for 7% -> 7%
where the time goes in v5:
time: 808 us; the launch traced here: 795 us
  Pallas kernels  657 us (81%)
  matrix products  77.1 us (10%)
  local copies, waits for them, and re-layouts  35.4 us (4%)
  other arithmetic  22.3 us (3%)
    pallas_call x3, Pallas kernels, mixture_call(): pl.pallas_call(functools.partial(mixture_kernel, mode, axes, count, layer...  526 us
    pallas_call x1, Pallas kernels, closing(): pl.pallas_call(functools.partial(closing_kernel, axes, n), out_shape=[jax...  73.8 us
    pallas_call x1, Pallas kernels, weight_spread(): pl.pallas_call(functools.partial(weight_spread_kernel, torus_axes(count),...  57.5 us
    dot_general x6, matrix products, dot_columns(): lax.dot_general(left, right, (((1,), (1,)), ((), ())), preferred_element_...  24.1 us
    unnamed x154, local copies, waits for them, and re-layouts  22.2 us
    dot_general x6, matrix products, dot_rows(): lax.dot_general(left, right, (((0,), (0,)), ((), ())), preferred_element_...  19.6 us
    dot_general x6, matrix products, dot(): return jnp.dot(left, right, preferred_element_type=jnp.float32)  18.5 us
  transfers between devices with their start and end apart: 3, of which 0 were waited for; matrix products, arithmetic and copies ran while one was open for 3% of the time, Pallas kernels for 7%

profile of v5, /device:TPU:28, one launch (start us, length us, event | category | flops | bytes accessed | tf_op | source)
XLA Modules:
  0.0 794.8 jit_solution(136836082064840577)
XLA Ops:
  6.6 57.5 %weight_spread.1 = (bf16[16,96,2560]{2,1,0:T(8,128)(2,1)}, bf16[16,96,1536]{2,1,0:T(8,128)(2,1)}, bf16[16,96,256]{2,1,0:T(8,128)(2,1)}) custom-call(bf16[96,2176]{1,0:T(8,128)(2,1)} %get-tuple-element.105.refs_0_), custom_call_target="tpu_custom_call" | custom-call | tf_op jit(solution)/shard_map/weight_spread/pallas_call | solution.py:734
  64.1 1.7 convert_reduce_fusion.2
  65.8 4.5 fusion.45
  77.9 2.3 convolution_convert_fusion.9
  80.2 3.4 multiply_reduce_fusion.5
  86.0 151.1 %mixture_f.1 = (f32[128,1536]{1,0:T(8,128)}, bf16[16,128,1536]{2,1,0:T(8,128)(2,1)}, bf16[16,96,2560]{2,1,0:T(8,128)(2,1)}, bf16[16,96,1536]{2,1,0:T(8,128)(2,1)}, bf16[16,96,256]{2,1,0:T(8,128)(2,1)}) custom-call(bf16[16,8,128]{2,1,0:T(8,128)(2,1)} %pad.39.refs_0_, bf16[1536,128]{1,0:T(8,128)(2,1)} %slice.172.refs_1_, bf16[1536,1024]{1,0:T(8,128)(2,1)} %bitcast.312, ...), custom_call_target="tpu_custom_call" | custom-call | flops 9663676416 | bytes 12582912 | tf_op jit(solution)/shard_map/mixture_f/pallas_call | solution.py:1204
  237.2 1.6 fusion.39
  239.4 4.5 fusion.72
  246.4 1.6 bitcast_select_fusion
  248.0 2.3 convolution_convert_fusion.8
  250.3 3.4 multiply_reduce_fusion.4
  256.7 211.9 %mixture_fb.1 = (f32[128,1536]{1,0:T(8,128)}, f32[128,1536]{1,0:T(8,128)}, f32[16,8,128]{2,1,0:T(8,128)}, f32[1536,1024]{1,0:T(8,128)}, f32[512,1536]{1,0:T(8,128)}) custom-call(bf16[16,8,128]{2,1,0:T(8,128)(2,1)} %pad.40.refs_0_, bf16[1536,128]{1,0:T(8,128)(2,1)} %slice.182.refs_1_, bf16[1536,1024]{1,0:T(8,128)(2,1)} %bitcast.313, ...), custom_call_target="tpu_custom_call" | custom-call | flops 28991029248 | bytes 12582912 | tf_op jit(solution)/shard_map/mixture_fb/pallas_call | solution.py:1204
  472.3 1.9 multiply_reduce_fusion.2
  475.4 4.0 convolution_convert_fusion.5
  481.0 1.6 fusion.3
  485.0 2.4 fusion.14
  487.5 3.6 convolution_convert_fusion.3
  492.1 6.1 fusion.38
  498.1 5.5 convolution_convert_fusion.1
  506.4 162.9 %mixture_b.1 = (f32[128,1536]{1,0:T(8,128)}, f32[16,8,128]{2,1,0:T(8,128)}, f32[1536,1024]{1,0:T(8,128)}, f32[512,1536]{1,0:T(8,128)}, f32[96,2176]{1,0:T(8,128)}) custom-call(bf16[16,8,128]{2,1,0:T(8,128)(2,1)} %pad.39.refs_0_, bf16[1536,128]{1,0:T(8,128)(2,1)} %slice.172.refs_1_, bf16[1536,1024]{1,0:T(8,128)(2,1)} %bitcast.314, ...), custom_call_target="tpu_custom_call" | custom-call | flops 28991029248 | bytes 12582912 | tf_op jit(solution)/shard_map/mixture_b/pallas_call | solution.py:1204
  671.8 2.0 multiply_reduce_fusion
  674.1 4.0 convolution_convert_fusion.4
  679.7 1.6 fusion
  683.8 2.4 fusion.15
  686.4 3.6 convolution_convert_fusion.2
  691.1 6.1 fusion.24
  697.2 5.4 convolution_convert_fusion
  705.3 73.8 %closing.1 = (f32[96,2560]{1,0:T(8,128)}, f32[96,1536]{1,0:T(8,128)}, f32[96,256]{1,0:T(8,128)}, f32[1536,1024]{1,0:T(8,128)}, f32[512,1536]{1,0:T(8,128)}, /*index=5*/bf16[2,128,1536]{2,1,0:T(8,128)(2,1)}) custom-call(bf16[16,96,2560]{2,1,0:T(8,128)(2,1)} %bitcast.232, bf16[16,96,1536]{2,1,0:T(8,128)(2,1)} %bitcast.233, ...), custom_call_target="tpu_custom_call" | custom-call | bytes 100000000 | tf_op jit(solution)/shard_map/closing/pallas_call | solution.py:894
  780.1 1.6 slice_reduce_fusion
  782.3 2.1 copy.155
  786.2 6.8 copy.158
  793.0 1.7 copy.159
  (256 shorter events, 47.8 us)
Async XLA Ops:
  0.7 3.4 copy-start.69
  0.7 4.0 copy-start.32
  3.2 2.3 collective-permute-start
  3.3 82.7 %collective-permute-start.1 = (bf16[1536,1024]{1,0:T(8,128)(2,1)}, bf16[1536,1024]{1,0:T(8,128)(2,1)}, u32[]{:S(2)}, u32[]{:S(2)}) collective-permute-start(bf16[1536,1024]{1,0:T(8,128)(2,1)} %bitcast.311), channel_id=1, source_target_pairs={{0,16},{16,0},{1,17},{17,1},{2,18},{18,2},{3,19},{19,3},{4,20},{20... | collective-permute-start | bytes 9437192 | tf_op jit(solution)/shard_map/ppermute | solution.py:1216
  3.8 82.2 %collective-permute-start.2 = (bf16[512,1536]{1,0:T(8,128)(2,1)}, bf16[512,1536]{1,0:T(8,128)(2,1)}, u32[]{:S(2)}, u32[]{:S(2)}) collective-permute-start(bf16[512,1536]{1,0:T(8,128)(2,1)} %bitcast.315), channel_id=1, source_target_pairs={{0,16},{16,0},{1,17},{17,1},{2,18},{18,2},{3,19},{19,3},{4,20},{20... | collective-permute-start | bytes 4718600 | tf_op jit(solution)/shard_map/ppermute | solution.py:1216
  4.5 68.6 %copy-start.55 = (pred[128,128]{0,1:T(8,128)(4,1)}, pred[128,128]{0,1:T(8,128)(4,1)S(1)}, u32[]{:S(2)}) copy-start(pred[128,128]{0,1:T(8,128)(4,1)S(1)} %fusion.74) | copy-start | bytes 49156
  4.7 67.0 %copy-start.39 = (f32[128,32]{0,1:T(8,128)}, f32[128,32]{0,1:T(8,128)S(1)}, u32[]{:S(2)}) copy-start(f32[128,32]{0,1:T(8,128)S(1)} %get-tuple-element.131) | copy-start | bytes 49156
  4.7 61.0 %copy-start.57 = (f32[128]{0:T(128)}, f32[128]{0:T(128)S(1)}, u32[]{:S(2)}) copy-start(f32[128]{0:T(128)S(1)} %add_rsqrt_fusion.3) | copy-start | bytes 1540
  65.8 4.6 copy-start.41
  65.8 17.8 %copy-start.51 = (f32[1536]{0:T(1024)}, f32[1536]{0:T(1024)S(1)}, u32[]{:S(2)}) copy-start(f32[1536]{0:T(1024)S(1)} %get-tuple-element.98) | copy-start | bytes 18436
  80.2 3.4 copy-start.19
  238.8 11.5 %copy-start.2 = (bf16[128,1536]{1,0:T(8,128)(2,1)}, bf16[128,1536]{1,0:T(8,128)(2,1)S(1)}, u32[]{:S(2)}) copy-start(bf16[128,1536]{1,0:T(8,128)(2,1)S(1)} %get-tuple-element.103) | copy-start | bytes 1179652
  238.8 5.1 copy-start.59
  239.4 14.4 %copy-start.53 = (f32[1536]{0:T(1024)}, f32[1536]{0:T(1024)S(1)}, u32[]{:S(2)}) copy-start(f32[1536]{0:T(1024)S(1)} %get-tuple-element.96) | copy-start | bytes 18436
  246.3 4.0 copy-start.47
  246.4 3.9 copy-start.37
  250.3 3.4 copy-start.17
  470.9 3.3 copy-start.5
  470.9 3.3 copy-start.16
  470.9 3.3 copy-start.31
  470.9 3.3 copy-start.33
  470.9 3.3 copy-start.54
  470.9 3.3 copy-start.65
  475.4 4.3 copy-start.38
  506.4 165.4 %copy-start.52 = (f32[1536]{0:T(1024)S(1)}, f32[1536]{0:T(1024)}, u32[]{:S(2)}) copy-start(f32[1536]{0:T(1024)} %copy-done.51) | copy-start | bytes 18436
  669.3 4.4 copy-start.1
  669.3 4.4 copy-start.15
  669.3 4.4 copy-start.21
  669.4 4.4 copy-start.63
  674.1 4.3 copy-start.36
  779.2 5.3 copy-start.22
  786.2 6.8 copy-start.14
  (44 other events, 77.9 us)

commit v6 on v5

--- a/solution.py
+++ b/solution.py
@@ -743,11 +743,12 @@
 
 
 class WeightFold:
-    def __init__(self, axes, raws, total, got, load, out, sems, ranks):
+    def __init__(self, axes, data, total, got, made, tail, out, sems, ranks):
         send, recv, self.psend, self.precv, self.local = sems
-        self.raws, self.total, self.held, self.rows = raws, total, load, out.shape[0]
-        self.widths = [raw.shape[2] // 2 for raw in raws]
-        self.ranks = ranks
+        self.lefts, self.rights, self.small = data[:2], data[2:4], data[4]
+        self.total, self.made, self.tail, self.rows, self.ranks = total, made, tail, out.shape[0], ranks
+        self.widths = fold_widths(data)
+        self.columns = packed_columns(self.widths)
         streams = []
         for order, at, size in weight_parts(self.rows):
             rows, route = pl.ds(at, size), Route(axes, order)
@@ -755,38 +756,66 @@
         self.route = Route(axes, ORDERS[0])
         self.fold = Fold(streams, send, recv, ranks)
 
-    def pieces(self, c):
-        cols = packed_columns(self.widths)
-        return [(o, a, cols[a]) for o in self.route.all if o[0] == self.ranks[c] for a in range(len(self.raws))]
-
-    def give(self, offs, a, cols):
-        f = self.route.flat(offs)
-        src = self.raws[a].at[self.route.block(offs), :, weight_columns(self.widths[a])[1]]
-        return remote(src, self.total.at[f, :, cols], self.psend.at[a, f], self.precv.at[a, f], {"section": 1 - lax.axis_index("section")})
-
-    def load(self, offs, a, cols):
-        src = self.raws[a].at[self.route.block(offs), :, weight_columns(self.widths[a])[0]]
-        return pltpu.make_async_copy(src, self.held.at[offs[1] * 2 + offs[2], :, cols], self.local.at[a, self.route.flat(offs)])
+    def place(self, c, q):
+        k, route = self.ranks[c], self.route
+        j = lax.rem(q + route.digit(1), 2)
+        i = lax.rem(lax.div(q, 2) + route.digit(2), 2)
+        return route.plane(k) * 4 + q, (k * 2 + j) * 2 + i
+
+    def product(self, a, block, other):
+        rows = pl.ds(pl.multiple_of(block * self.rows, 32), self.rows)
+        return dot(self.lefts[a][rows, :], self.rights[a][:, weight_columns(self.widths[a])[other]])
+
+    def give(self, c, q):
+        block, f = self.place(c, q)
+        partner = {"section": 1 - lax.axis_index("section")}
+        main = pl.ds(0, sum(self.widths[:2]))
+        return (remote(self.made.at[q], self.total.at[f, :, main], self.psend.at[0, f], self.precv.at[0, f], partner),
+                remote(self.small.at[block, :, weight_columns(self.widths[2])[1]], self.total.at[f, :, self.columns[2]],
+                       self.psend.at[1, f], self.precv.at[1, f], partner))
+
+    def load(self, c, q):
+        block, f = self.place(c, q)
+        return pltpu.make_async_copy(self.small.at[block, :, weight_columns(self.widths[2])[0]], self.tail.at[q], self.local.at[f])
+
+    def produce(self, c):
+        def one(q, _):
+            block, _ = self.place(c, q)
+            for a in range(2):
+                self.made[q, :, self.columns[a]] = self.product(a, block, 1).astype(jnp.bfloat16)
+            for copy in self.give(c, q):
+                copy.start()
+            self.load(c, q).start()
+            return 0
+
+        lax.fori_loop(0, 4, one, 0)
 
     def begin(self):
-        for c in range(len(self.ranks)):
-            for piece in self.pieces(c):
-                self.give(*piece).start()
-                if c == 0:
-                    self.load(*piece).start()
+        self.produce(0)
 
     def step(self, t):
         if t < len(self.ranks):
-            for piece in self.pieces(t):
-                self.load(*piece).wait()
-                self.give(*piece).wait_recv()
-            for offs in self.route.all:
-                if offs[0] == self.ranks[t]:
-                    here = self.total.at[self.route.flat(offs)]
-                    add_rows([self.held.at[offs[1] * 2 + offs[2]], here], here, self.rows)
+            def own(q, _):
+                block, f = self.place(t, q)
+                for copy in self.give(t, q):
+                    copy.wait_recv()
+                for a in range(2):
+                    cols = self.columns[a]
+                    self.total[f, :, cols] = (self.total[f, :, cols].astype(jnp.float32) + self.product(a, block, 0)).astype(jnp.bfloat16)
+                cols = self.columns[2]
+                self.total[f, :, cols] = (self.total[f, :, cols].astype(jnp.float32) + self.tail[q].astype(jnp.float32)).astype(jnp.bfloat16)
+                return 0
+
+            def settled(q, _):
+                for copy in self.give(t, q):
+                    copy.wait_send()
+                self.load(t, q).wait()
+                return 0
+
+            lax.fori_loop(0, 4, settled, 0)
+            lax.fori_loop(0, 4, own, 0)
             if t + 1 < len(self.ranks):
-                for piece in self.pieces(t + 1):
-                    self.load(*piece).start()
+                self.produce(t + 1)
         self.fold.step(t)
 
     def steps(self):
@@ -794,37 +823,44 @@
 
     def end(self):
         self.fold.end()
-        for c in range(len(self.ranks)):
-            for piece in self.pieces(c):
-                self.give(*piece).wait_send()
-
-
-def fold_shape(arrays):
-    return jax.ShapeDtypeStruct((arrays[0].shape[1], sum(a.shape[2] // 2 for a in arrays)), jnp.float32)
-
-
-def fold_scratch(arrays, axes):
-    count, dma, block = arrays[0].shape[0], pltpu.SemaphoreType.DMA, fold_shape(arrays).shape
-    blocks = [pltpu.VMEM((n, *block), jnp.bfloat16) for n in (count, count + 4, axes[1][1] * axes[2][1])]
-    return blocks + [dma((len(ORDERS), count + 4))] * 2 + [dma((len(arrays), count))] * 3
-
-
-def closing_kernel(axes, count, *refs):
+
+
+def fold_widths(data):
+    return [a.shape[-1] // 2 for a in data[2:]]
+
+
+def fold_shape(data):
+    return jax.ShapeDtypeStruct((data[4].shape[1], sum(fold_widths(data))), jnp.float32)
+
+
+def fold_specs():
+    return [pl.BlockSpec(memory_space=pltpu.VMEM)] * 4 + [pl.BlockSpec(memory_space=pl.ANY)]
+
+
+def fold_scratch(data):
+    (rows, cols), count, dma = fold_shape(data).shape, data[4].shape[0], pltpu.SemaphoreType.DMA
+    small = fold_widths(data)[2]
+    blocks = [pltpu.VMEM(shape, jnp.bfloat16) for shape in ((count, rows, cols), (count + 4, rows, cols), (4, rows, cols - small), (4, rows, small))]
+    return blocks + [dma((len(ORDERS), count + 4))] * 2 + [dma((2, count))] * 2 + [dma((count,))]
+
+
+def closing_kernel(axes, *refs):
     refs = list(refs)
     take = lambda n: [refs.pop(0) for _ in range(n)]
-    raws = take(count)
+    data = take(5)
+    count = 3
     other = take(1)[0]
     first_up, first_down, last_up, last_down, grad_in, last_in = take(6)
     outs = take(count)
     up_out, down_out, edge_out = take(3)
-    blocks, sems = take(3), take(5)
+    blocks, sems = take(4), take(5)
     result, given, taken = take(3)
     own_up, own_down, got_up, got_down, edge_give, edge_got, x_send, x_recv, x_local, h_send, h_recv = take(11)
     sec = lax.axis_index("section")
     partner = {"section": 1 - sec}
     chunks = [axes[0][1] - 1 - c for c in range(axes[0][1])]
     meet(axes, False, True)
-    fold = WeightFold(axes, raws, *blocks, result, sems, chunks)
+    fold = WeightFold(axes, data, *blocks, result, sems, chunks)
     fold.begin()
     leading = sec == 0
 
@@ -884,24 +920,25 @@
         outs[a][:, weight_columns(fold.widths[a])[1]] = taken[:, packed[a]]
 
 
-def closing(raws, other, first, last, grad, final, count, cid):
-    axes, n = torus_axes(count), len(raws)
+def closing(data, other, first, last, grad, final, count, cid):
+    axes, n = torus_axes(count), 3
     vmem, anywhere = pl.BlockSpec(memory_space=pltpu.VMEM), pl.BlockSpec(memory_space=pl.ANY)
     dma, f32 = pltpu.SemaphoreType.DMA, jnp.float32
-    half = pltpu.VMEM(fold_shape(raws).shape, f32)
+    rows = fold_shape(data).shape[0]
+    half = pltpu.VMEM(fold_shape(data).shape, f32)
     experts = [pltpu.VMEM(w.shape, f32) for w in first]
     block = pltpu.VMEM(grad.shape, grad.dtype)
     return pl.pallas_call(
-        functools.partial(closing_kernel, axes, n),
-        out_shape=[jax.ShapeDtypeStruct(a.shape[1:], f32) for a in raws] + [jax.ShapeDtypeStruct(w.shape, f32) for w in first]
+        functools.partial(closing_kernel, axes),
+        out_shape=[jax.ShapeDtypeStruct((rows, 2 * w), f32) for w in fold_widths(data)] + [jax.ShapeDtypeStruct(w.shape, f32) for w in first]
         + [jax.ShapeDtypeStruct((2, *grad.shape), grad.dtype)],
-        in_specs=[anywhere] * n + [vmem] + [anywhere] * 4 + [vmem] * 2,
+        in_specs=fold_specs() + [vmem] + [anywhere] * 4 + [vmem] * 2,
         out_specs=[vmem] * n + [anywhere] * 2 + [vmem],
-        scratch_shapes=fold_scratch(raws, axes) + [half] * 3 + experts * 2 + [block, block, dma((3,)), dma((3,)), dma((2,)), dma((1,)), dma((1,))],
+        scratch_shapes=fold_scratch(data) + [half] * 3 + experts * 2 + [block, block, dma((3,)), dma((3,)), dma((2,)), dma((1,)), dma((1,))],
         compiler_params=pltpu.CompilerParams(collective_id=cid, has_side_effects=True, vmem_limit_bytes=VMEM_BYTES),
         cost_estimate=pl.CostEstimate(flops=0, bytes_accessed=100_000_000, transcendentals=0),
         name="closing",
-    )(*raws, other, *first, *last, grad, final)
+    )(*data, other, *first, *last, grad, final)
 
 
 def mixture_kernel(mode, axes, count, layer, extra, folded, *refs):
@@ -911,7 +948,7 @@
     mask_ref, router_ref, up_own, up_other, down_own, down_other, x_in = take(7)
     g_in = take(1)[0] if back else None
     next_in = take(1)[0] if extra else None
-    raws = take(folded)
+    data = take(folded)
     mixed_out = take(1)[0] if fore else None
     saved_out = take(1)[0] if mode == "f" else None
     if back:
@@ -926,8 +963,7 @@
         gathers.append((x_in, xg))
         folds.append((share_f, got_f, mixed_out))
     if back:
-        (gg, share_b, got_b, plain_at, ggu_at, actw_at, high_at, low_at, up_sum, down_sum, chance_row, chance_got, c_send, c_recv,
-         out_sem) = take(15)
+        (gg, share_b, got_b, plain_at, ggu_at, actw_at, high_at, low_at, chance_row, chance_got, c_send, c_recv, out_sem) = take(13)
         gathers.append((g_in, gg))
         folds.append((share_b, got_b, grad_out))
     me, sec = lax.axis_index("dp"), lax.axis_index("section")
@@ -952,7 +988,7 @@
     if extra:
         other = WeightSpread(axes, next_in, take(1)[0], next_out, take(5))
     if folded:
-        aside = WeightFold(axes, raws, *take(3), raw_out, take(5), ranks)
+        aside = WeightFold(axes, data, *take(4), raw_out, take(5), ranks)
         aside.begin()
 
     @pl.when(sec == layer)
@@ -1067,6 +1103,7 @@
             return 0
 
         lax.fori_loop(0, plane * ROWS // TILE, step, 0)
+
         for v in range(n0):
             @pl.when(c == v)
             def _(v=v):
@@ -1088,59 +1125,63 @@
             chance_copy(offs, me).start()
         chance_got[me] = chance_row[me]
 
-        def up_piece(n):
-            return pltpu.make_async_copy(up_sum.at[0], up_grad_out.at[pl.ds(n * PIECE, PIECE)], out_sem.at[0, 0])
-
-        def down_piece(n):
-            return pltpu.make_async_copy(down_sum.at[0], down_grad_out.at[pl.ds(n * PIECE, PIECE)], out_sem.at[1, 0])
-
-        ups, downs = MODEL_WIDTH // PIECE, FFE // PIECE
-
-        def gradient(n):
-            if n < ups:
-                if n:
-                    up_piece(n - 1).wait()
-                left = xg[:, :, n * PIECE : (n + 1) * PIECE].reshape(count * ROWS, PIECE)
-                up_sum[0] = contract(left, ggu_at[...], (0, 0))
-                up_piece(n).start()
-            else:
-                n -= ups
-                if n:
-                    down_piece(n - 1).wait()
-                down_sum[0] = contract(actw_at[:, n * PIECE : (n + 1) * PIECE], gg[...].reshape(count * ROWS, MODEL_WIDTH), (0, 0))
-                down_piece(n).start()
-
-        work = list(range(ups + downs))
-    else:
-        work = []
+        up_held = gates_at.at[pl.ds(0, PIECE)]
+        down_held = (gates_at.at[pl.ds(PIECE, PIECE)], plain_at.at[pl.ds(0, PIECE)])
+        down_parts = ((0, 2 * FFE), (2 * FFE, MODEL_WIDTH - 2 * FFE))
+
+        def put_up(n):
+            return pltpu.make_async_copy(up_held, up_grad_out.at[span(n, PIECE)], out_sem.at[0, 0])
+
+        def put_down(n, p):
+            cols = pl.ds(*down_parts[p])
+            return pltpu.make_async_copy(down_held[p], down_grad_out.at[span(n, PIECE), cols], out_sem.at[1, p])
+
+        def up_gradient(n, _):
+            @pl.when(n > 0)
+            def _():
+                put_up(n).wait()
+
+            left = xg[:, :, span(n, PIECE)].reshape(count * ROWS, PIECE)
+            up_held[...] = contract(left, ggu_at[...], (0, 0))
+            put_up(n).start()
+            return 0
+
+        def down_gradient(n, _):
+            @pl.when(n > 0)
+            def _():
+                put_down(n, 0).wait()
+                put_down(n, 1).wait()
+
+            for p, (at, width) in enumerate(down_parts):
+                right = gg[:, :, at : at + width].reshape(count * ROWS, width)
+                down_held[p][...] = contract(actw_at[:, span(n, PIECE)], right, (0, 0))
+                put_down(n, p).start()
+            return 0
+
     if saved_out is not None:
         save = pltpu.make_async_copy(xg, saved_out, local.at[2])
         save.start()
     last = fold.steps()
+    assert last == 6
     for t in range(n0, last):
-        share = -(-len(work) // (last - t))
-        for _ in range(share):
-            n = work.pop(0)
-            if "grad" not in SKIP:
-                gradient(n)
+        if back and t == n0:
+            lax.fori_loop(0, MODEL_WIDTH // PIECE, up_gradient, 0)
+        elif back:
+            lax.fori_loop(0, FFE // PIECE, down_gradient, 0)
         fold.step(t)
         if extra:
             other.step(t)
-        if folded:
-            aside.step(SPREAD_STEPS - 1 + t)
     if folded:
-        assert aside.steps() <= SPREAD_STEPS - 1 + last
+        assert aside.steps() == 6
         aside.end()
     if extra:
-        assert last >= SPREAD_STEPS
         other.end()
     spread.end()
     fold.end()
     if back:
-        for n in range(ups - 1, ups) if "grad" not in SKIP else ():
-            up_piece(n).wait()
-        for n in range(downs - 1, downs) if "grad" not in SKIP else ():
-            down_piece(n).wait()
+        put_up(0).wait()
+        put_down(0, 0).wait()
+        put_down(0, 1).wait()
         for offs in route.others:
             chance_copy(offs, route.block(offs)).wait()
         chance_out[...] = chance_got[...]
@@ -1158,7 +1199,7 @@
         args.append(g)
         in_specs.append(vmem)
     args += ([following] if widths else []) + list(summed)
-    in_specs += ([vmem] if widths else []) + [anywhere] * len(summed)
+    in_specs += ([vmem] if widths else []) + (fold_specs() if summed else [])
     whole = (count, ROWS, MODEL_WIDTH)
     out_shape, out_specs = [], []
     block = jax.ShapeDtypeStruct((ROWS, MODEL_WIDTH), jnp.float32)
@@ -1192,13 +1233,12 @@
     if back:
         scratch += [blocks, blocks, arrivals, pltpu.VMEM((TILE, FFE), jnp.float32),
                     low(count * ROWS, 2 * FFE), low(count * ROWS, FFE), low(TILE, FFE), low(TILE, FFE),
-                    pltpu.VMEM((1, PIECE, 2 * FFE), jnp.float32), pltpu.VMEM((1, PIECE, MODEL_WIDTH), jnp.float32),
                     pltpu.VMEM((count, 8, ROWS), jnp.float32), pltpu.VMEM((count, 8, ROWS), jnp.float32), dma((count,)), dma((count,)),
                     dma((2, 2))]
     if widths:
         scratch += weight_scratch(following, widths, count)
     if summed:
-        scratch += fold_scratch(summed, axes)
+        scratch += fold_scratch(summed)
     rows = count * ROWS
     flops = rows * 6 * MODEL_WIDTH * FFE * (fore + 2 * back + (mode == "b"))
     return pl.pallas_call(
@@ -1351,7 +1391,7 @@
     return mixed, grad_chance.T, grad_up, grad_down
 
 
-def front_backward(grad_out, grad_mixed, grad_chance, kept, place, weights):
+def front_backward(grad_out, grad_mixed, grad_chance, kept, place, weights, fused):
     joint, result_output, router, gain_attention, gain_mixture = weights
     allowed, cosine, sine = place
     inverse_one, scaled_one, normed, query, key, value, attention, context, inverse_two, scaled_two, normed_two = kept
@@ -1364,7 +1404,6 @@
     scaled_grad_two = grad_normed_two * gain_mixture
     grad_middle = grad_out + inverse_two * (scaled_grad_two - scaled_two * jnp.mean(scaled_grad_two * scaled_two, axis=-1, keepdims=True))
     branch = grad_middle.astype(jnp.bfloat16)
-    grad_output = dot_rows(context, branch)
     grad_context = dot_columns(branch, result_output).astype(jnp.bfloat16).reshape(rows, KEY_VALUE_HEADS, GROUP, HEAD_SIZE)
     grad_attention = jnp.einsum("qhgd,khd->hgqk", grad_context, value, preferred_element_type=jnp.float32)
     grad_value = jnp.einsum("hgqk,qhgd->khd", attention.astype(jnp.bfloat16), grad_context, preferred_element_type=jnp.float32)
@@ -1375,12 +1414,13 @@
     grad_key = rotary_embedding(grad_key * SCORE_SCALE, cosine, -sine)
     grad_projected = jnp.concatenate(
         [grad_query.reshape(rows, -1), grad_key.reshape(rows, -1), grad_value.reshape(rows, -1)], axis=-1).astype(jnp.bfloat16)
-    grad_joint = dot_rows(normed, grad_projected)
+    pairs = (normed, context, grad_projected, branch)
+    products = (pairs[0].T, pairs[1].T, *pairs[2:]) if fused else (dot_rows(normed, grad_projected), dot_rows(context, branch))
     grad_normed = dot_columns(grad_projected, joint)
     grad_gain_one = jnp.sum(grad_normed * scaled_one, axis=0)
     scaled_grad_one = grad_normed * gain_attention
     grad_hidden = grad_middle + inverse_one * (scaled_grad_one - scaled_one * jnp.mean(scaled_grad_one * scaled_one, axis=-1, keepdims=True))
-    return grad_hidden, (grad_joint, grad_output, grad_router, grad_gain_one, grad_gain_two)
+    return grad_hidden, (products, None, grad_router, grad_gain_one, grad_gain_two)
 
 
 def small_halves(rows, router, gains, codes):
@@ -1495,13 +1535,15 @@
                 shares[layer + 1] = more[0]
             grad_chance = rows[:, 0].T
         expert_grads[layer] = (grad_up, grad_down)
-        grad_hidden, parts = front_backward(grad.astype(jnp.float32), mixed, grad_chance, kept, place, weights[layer])
+        grad_hidden, parts = front_backward(grad.astype(jnp.float32), mixed, grad_chance, kept, place, weights[layer], fused)
         grad = grad_hidden.astype(jnp.bfloat16)
         tail = small_halves(MODEL_WIDTH, parts[2], jnp.stack([parts[3], parts[4]], axis=1), parts[2][:, :0])
-        packed = [parts[0], parts[1], jnp.concatenate(tail, axis=1)]
-        packs[layer] = [a.astype(jnp.bfloat16).reshape(count, shard, -1) for a in packed]
-        if not fused:
-            shares[layer] = reduce_all(packs[layer], count, 3, pair=True)
+        small = jnp.concatenate(tail, axis=1).astype(jnp.bfloat16).reshape(count, shard, -1)
+        if fused:
+            packs[layer] = [*parts[0], small]
+        else:
+            packed = [a.astype(jnp.bfloat16).reshape(count, shard, -1) for a in parts[0]] + [small]
+            shares[layer] = reduce_all(packed, count, 3, pair=True)
     if fused:
         *outs, grad_up, grad_down, boundary = closing(packs[0], shares[1], expert_grads[0], expert_grads[1], grad, last, count, 3)
         half = outs[2].shape[1] // 2

time: 808 us -> 804 us (level)
  matrix products: 77.1 us -> 57.7 us
  Pallas kernels: 657 us -> 666 us
    dot_general x6 -> x2, matrix products: 19.6 us -> 3.23 us  [dot_rows(): lax.dot_general(left, right, (((0,), (0,)), ((), ())), preferred_element_...]
    unnamed x154 -> x162, local copies, waits for them, and re-layouts: 22.2 us -> 22.5 us
where the time goes in v6:
time: 804 us; the launch traced here: 792 us
  Pallas kernels  666 us (83%)
  matrix products  57.7 us (7%)
  local copies, waits for them, and re-layouts  38.3 us (5%)
  other arithmetic  26.2 us (3%)
    pallas_call x3, Pallas kernels, mixture_call(): pl.pallas_call(functools.partial(mixture_kernel, mode, axes, count, layer...  533 us
    pallas_call x1, Pallas kernels, closing(): pl.pallas_call(functools.partial(closing_kernel, axes), out_shape=[jax.Sh...  76.4 us
    pallas_call x1, Pallas kernels, weight_spread(): pl.pallas_call(functools.partial(weight_spread_kernel, torus_axes(count),...  57.5 us
    dot_general x6, matrix products, dot_columns(): lax.dot_general(left, right, (((1,), (1,)), ((), ())), preferred_element_...  24.5 us
    unnamed x162, local copies, waits for them, and re-layouts  22.5 us
    dot_general x6, matrix products, dot(): return jnp.dot(left, right, preferred_element_type=jnp.float32)  18.1 us
  transfers between devices with their start and end apart: 3, of which 0 were waited for; matrix products, arithmetic and copies ran while one was open for 3% of the time, Pallas kernels for 7%

profile of v6, /device:TPU:28, one launch (start us, length us, event | category | flops | bytes accessed | tf_op | source)
XLA Modules:
  0.0 791.6 jit_solution(11269417642092085181)
XLA Ops:
  8.5 57.5 %weight_spread.1 = (bf16[16,96,2560]{2,1,0:T(8,128)(2,1)}, bf16[16,96,1536]{2,1,0:T(8,128)(2,1)}, bf16[16,96,256]{2,1,0:T(8,128)(2,1)}) custom-call(bf16[96,2176]{1,0:T(8,128)(2,1)} %get-tuple-element.109.refs_0_), custom_call_target="tpu_custom_call" | custom-call | tf_op jit(solution)/shard_map/weight_spread/pallas_call | solution.py:734
  66.0 2.4 convert_reduce_fusion.2
  68.4 4.5 fusion.45
  73.6 1.6 bitcast_select_fusion.1
  76.9 2.3 convolution_convert_fusion.5
  79.2 3.4 multiply_reduce_fusion.5
  83.7 1.4 fusion.86
  85.1 151.1 %mixture_f.1 = (f32[128,1536]{1,0:T(8,128)}, bf16[16,128,1536]{2,1,0:T(8,128)(2,1)}, bf16[16,96,2560]{2,1,0:T(8,128)(2,1)}, bf16[16,96,1536]{2,1,0:T(8,128)(2,1)}, bf16[16,96,256]{2,1,0:T(8,128)(2,1)}) custom-call(bf16[16,8,128]{2,1,0:T(8,128)(2,1)} %pad.39.refs_0_, bf16[1536,128]{1,0:T(8,128)(2,1)} %slice.172.refs_1_, bf16[1536,1024]{1,0:T(8,128)(2,1)} %bitcast.307, ...), custom_call_target="tpu_custom_call" | custom-call | flops 9663676416 | bytes 12582912 | tf_op jit(solution)/shard_map/mixture_f/pallas_call | solution.py:1244
  237.2 1.7 convert_reduce_fusion
  238.9 1.8 slice.182.refs_1_
  240.8 4.6 fusion.63
  248.8 3.4 multiply_reduce_fusion.4
  254.8 220.6 %mixture_fb.1 = (f32[128,1536]{1,0:T(8,128)}, f32[128,1536]{1,0:T(8,128)}, f32[16,8,128]{2,1,0:T(8,128)}, f32[1536,1024]{1,0:T(8,128)}, f32[512,1536]{1,0:T(8,128)}) custom-call(bf16[16,8,128]{2,1,0:T(8,128)(2,1)} %pad.40.refs_0_, bf16[1536,128]{1,0:T(8,128)(2,1)} %slice.182.refs_1_, bf16[1536,1024]{1,0:T(8,128)(2,1)} %bitcast.308, ...), custom_call_target="tpu_custom_call" | custom-call | flops 28991029248 | bytes 12582912 | tf_op jit(solution)/shard_map/mixture_fb/pallas_call | solution.py:1244
  477.5 1.3 convolution_convert_fusion.3
  478.8 2.0 multiply_reduce_fusion.2
  482.6 4.0 convolution_convert_fusion.1
  486.8 2.4 fusion.14
  490.7 1.4 fusion.3
  494.6 5.8 fusion.82
  503.9 1.8 fusion.37.refs_7_
  506.7 160.7 %mixture_b.1 = (f32[128,1536]{1,0:T(8,128)}, f32[16,8,128]{2,1,0:T(8,128)}, f32[1536,1024]{1,0:T(8,128)}, f32[512,1536]{1,0:T(8,128)}, f32[96,2176]{1,0:T(8,128)}) custom-call(bf16[16,8,128]{2,1,0:T(8,128)(2,1)} %pad.39.refs_0_, bf16[1536,128]{1,0:T(8,128)(2,1)} %slice.172.refs_1_, bf16[1536,1024]{1,0:T(8,128)(2,1)} %bitcast.309, ...), custom_call_target="tpu_custom_call" | custom-call | flops 28991029248 | bytes 12582912 | tf_op jit(solution)/shard_map/mixture_b/pallas_call | solution.py:1244
  669.7 1.9 convolution_convert_fusion.2
  671.6 2.6 multiply_reduce_fusion
  675.2 4.0 convolution_convert_fusion
  679.4 2.4 fusion.15
  683.3 1.4 fusion
  688.6 6.2 fusion.24
  699.4 76.4 %closing.1 = (f32[96,2560]{1,0:T(8,128)}, f32[96,1536]{1,0:T(8,128)}, f32[96,256]{1,0:T(8,128)}, f32[1536,1024]{1,0:T(8,128)}, f32[512,1536]{1,0:T(8,128)}, /*index=5*/bf16[2,128,1536]{2,1,0:T(8,128)(2,1)}) custom-call(bf16[1536,128]{1,0:T(8,128)(2,1)} %copy.154.refs_0_, bf16[1536,128]{1,0:T(8,128)(2,1)} %bitcast.270, ...), custom_call_target="tpu_custom_call" | custom-call | bytes 100000000 | tf_op jit(solution)/shard_map/closing/pallas_call | solution.py:931
  775.8 1.6 slice_reduce_fusion
  778.9 2.1 copy.181
  782.8 6.8 copy.184
  789.6 1.7 copy.185
  (270 shorter events, 46.4 us)
Async XLA Ops:
  0.6 4.6 copy-start.72
  0.6 5.1 copy-start.15
  0.7 6.0 copy-start.22
  4.6 2.9 collective-permute-start
  4.6 80.5 %collective-permute-start.2 = (bf16[512,1536]{1,0:T(8,128)(2,1)}, bf16[512,1536]{1,0:T(8,128)(2,1)}, u32[]{:S(2)}, u32[]{:S(2)}) collective-permute-start(bf16[512,1536]{1,0:T(8,128)(2,1)} %bitcast.310), channel_id=1, source_target_pairs={{0,16},{16,0},{1,17},{17,1},{2,18},{18,2},{3,19},{19,3},{4,20},{20... | collective-permute-start | bytes 4718600 | tf_op jit(solution)/shard_map/ppermute | solution.py:1256
  5.1 80.0 %collective-permute-start.1 = (bf16[1536,1024]{1,0:T(8,128)(2,1)}, bf16[1536,1024]{1,0:T(8,128)(2,1)}, u32[]{:S(2)}, u32[]{:S(2)}) collective-permute-start(bf16[1536,1024]{1,0:T(8,128)(2,1)} %bitcast.306), channel_id=1, source_target_pairs={{0,16},{16,0},{1,17},{17,1},{2,18},{18,2},{3,19},{19,3},{4,20},{20... | collective-permute-start | bytes 9437192 | tf_op jit(solution)/shard_map/ppermute | solution.py:1256
  5.6 68.0 %copy-start.62 = (pred[128,128]{0,1:T(8,128)(4,1)}, pred[128,128]{0,1:T(8,128)(4,1)S(1)}, u32[]{:S(2)}) copy-start(pred[128,128]{0,1:T(8,128)(4,1)S(1)} %fusion.65) | copy-start | bytes 49156
  6.6 66.8 %copy-start.43 = (f32[128,32]{0,1:T(8,128)}, f32[128,32]{0,1:T(8,128)S(1)}, u32[]{:S(2)}) copy-start(f32[128,32]{0,1:T(8,128)S(1)} %get-tuple-element.137) | copy-start | bytes 49156
  6.7 61.7 %copy-start.70 = (f32[128]{0:T(128)}, f32[128]{0:T(128)S(1)}, u32[]{:S(2)}) copy-start(f32[128]{0:T(128)S(1)} %add_rsqrt_fusion.3) | copy-start | bytes 1540
  68.4 4.5 copy-start.55
  79.2 3.4 copy-start.20
  79.2 4.3 copy-start.58
  236.3 4.4 copy-start.1
  236.3 4.4 copy-start.24
  238.9 262.8 %copy-start.46 = (f32[1536]{0:T(1024)}, f32[1536]{0:T(1024)S(1)}, u32[]{:S(2)}) copy-start(f32[1536]{0:T(1024)S(1)} %get-tuple-element.97) | copy-start | bytes 18436
  240.8 8.0 %copy-start.3 = (bf16[128,1536]{1,0:T(8,128)(2,1)}, bf16[128,1536]{1,0:T(8,128)(2,1)S(1)}, u32[]{:S(2)}) copy-start(bf16[128,1536]{1,0:T(8,128)(2,1)S(1)} %get-tuple-element.107) | copy-start | bytes 1179652
  240.8 4.7 copy-start.64
  248.8 3.4 copy-start.45
  248.8 5.2 copy-start.8
  477.4 3.3 copy-start.23
  506.7 161.6 %copy-start.60 = (f32[128,16]{0,1:T(8,128)S(1)}, f32[128,16]{0,1:T(8,128)}, u32[]{:S(2)}) copy-start(f32[128,16]{0,1:T(8,128)} %get-tuple-element.149) | copy-start | bytes 24580
  506.7 164.9 %copy-start.59 = (f32[1536]{0:T(1024)S(1)}, f32[1536]{0:T(1024)}, u32[]{:S(2)}) copy-start(f32[1536]{0:T(1024)} %get-tuple-element.98) | copy-start | bytes 18436
  669.7 4.5 copy-start.2
  669.7 4.5 copy-start.13
  669.7 4.5 copy-start.18
  669.7 4.5 copy-start.67
  688.6 6.2 copy-start.39
  688.6 6.2 copy-start.40
  688.6 7.1 copy-start.61
  688.6 7.1 copy-start.57
  775.8 5.2 copy-start.21
  782.8 6.8 copy-start.12
  (47 other events, 74.8 us)

commit v7 on v6

--- a/solution.py
+++ b/solution.py
@@ -384,7 +384,6 @@
 TILE = 512
 STRIP = 16
 SPAN = 512
-SKIP = set()
 PIECE = 256
 MESH = pl.DeviceIdType.MESH
 ORDERS = ((0, 1, 2), (0, 2, 1), (1, 0, 2), (2, 0, 1))
@@ -488,8 +487,6 @@
                 copy.start()
 
     def step(self, t):
-        if "comm" in SKIP or "ag" in SKIP:
-            return
         work = [(offs, s) for s in self.ids for offs in self.streams[s][0].all if offs[0] + offs[1] + offs[2] == t]
         if t == 0:
             first = [(s, item) for offs, s in work for item in self.onward(s, offs)]
@@ -501,8 +498,6 @@
             self.launch([(s, item) for item in sorted(self.onward(s, offs), key=lambda e: (e[1], e[0]))])
 
     def end(self):
-        if "comm" in SKIP or "ag" in SKIP:
-            return
         for s in self.ids:
             for offs in self.streams[s][0].all:
                 for _, inner, copy in self.onward(s, offs):
@@ -623,8 +618,6 @@
             self.copy(s, offs).start()
 
     def step(self, t):
-        if "comm" in SKIP or "rs" in SKIP:
-            return
         for when, _, _, s, offs, action in self.plan:
             if when == t:
                 action(s, offs)
@@ -633,8 +626,6 @@
         return 1 + max(e[0] for e in self.plan)
 
     def end(self):
-        if "comm" in SKIP or "rs" in SKIP:
-            return
         for s in self.ids:
             for offs in self.streams[s][0].others:
                 self.copy(s, offs).wait_send()
@@ -1098,8 +1089,7 @@
             source = jnp.where(c == v, sources[v], source)
 
         def step(q, _):
-            if "tile" not in SKIP:
-                tile(source * plane + q * (TILE // ROWS))
+            tile(source * plane + q * (TILE // ROWS))
             return 0
 
         lax.fori_loop(0, plane * ROWS // TILE, step, 0)
@@ -1165,8 +1155,9 @@
     assert last == 6
     for t in range(n0, last):
         if back and t == n0:
-            lax.fori_loop(0, MODEL_WIDTH // PIECE, up_gradient, 0)
+            lax.fori_loop(0, 4, up_gradient, 0)
         elif back:
+            lax.fori_loop(4, MODEL_WIDTH // PIECE, up_gradient, 0)
             lax.fori_loop(0, FFE // PIECE, down_gradient, 0)
         fold.step(t)
         if extra:

time: 804 us -> 812 us (level)
  no operation moved by 1% of the time
where the time goes in v7:
time: 812 us; the launch traced here: 799 us
  Pallas kernels  674 us (83%)
  matrix products  57.7 us (7%)
  local copies, waits for them, and re-layouts  38.3 us (5%)
  other arithmetic  26.2 us (3%)
    pallas_call x3, Pallas kernels, mixture_call(): pl.pallas_call(functools.partial(mixture_kernel, mode, axes, count, layer...  534 us
    pallas_call x1, Pallas kernels, closing(): pl.pallas_call(functools.partial(closing_kernel, axes), out_shape=[jax.Sh...  82.4 us
    pallas_call x1, Pallas kernels, weight_spread(): pl.pallas_call(functools.partial(weight_spread_kernel, torus_axes(count),...  57.5 us
    dot_general x6, matrix products, dot_columns(): lax.dot_general(left, right, (((1,), (1,)), ((), ())), preferred_element_...  24.5 us
    unnamed x162, local copies, waits for them, and re-layouts  22.5 us
    dot_general x6, matrix products, dot(): return jnp.dot(left, right, preferred_element_type=jnp.float32)  18.1 us
  transfers between devices with their start and end apart: 3, of which 0 were waited for; matrix products, arithmetic and copies ran while one was open for 3% of the time, Pallas kernels for 7%

profile of v7, /device:TPU:28, one launch (start us, length us, event | category | flops | bytes accessed | tf_op | source)
XLA Modules:
  0.0 799.0 jit_solution(1055182384022919383)
XLA Ops:
  8.5 57.5 %weight_spread.1 = (bf16[16,96,2560]{2,1,0:T(8,128)(2,1)}, bf16[16,96,1536]{2,1,0:T(8,128)(2,1)}, bf16[16,96,256]{2,1,0:T(8,128)(2,1)}) custom-call(bf16[96,2176]{1,0:T(8,128)(2,1)} %get-tuple-element.109.refs_0_), custom_call_target="tpu_custom_call" | custom-call | tf_op jit(solution)/shard_map/weight_spread/pallas_call | solution.py:725
  66.0 2.4 convert_reduce_fusion.2
  68.4 4.5 fusion.45
  73.6 1.6 bitcast_select_fusion.1
  76.9 2.3 convolution_convert_fusion.5
  79.2 3.4 multiply_reduce_fusion.5
  83.7 1.4 fusion.86
  85.1 151.1 %mixture_f.1 = (f32[128,1536]{1,0:T(8,128)}, bf16[16,128,1536]{2,1,0:T(8,128)(2,1)}, bf16[16,96,2560]{2,1,0:T(8,128)(2,1)}, bf16[16,96,1536]{2,1,0:T(8,128)(2,1)}, bf16[16,96,256]{2,1,0:T(8,128)(2,1)}) custom-call(bf16[16,8,128]{2,1,0:T(8,128)(2,1)} %pad.39.refs_0_, bf16[1536,128]{1,0:T(8,128)(2,1)} %slice.172.refs_1_, bf16[1536,1024]{1,0:T(8,128)(2,1)} %bitcast.307, ...), custom_call_target="tpu_custom_call" | custom-call | flops 9663676416 | bytes 12582912 | tf_op jit(solution)/shard_map/mixture_f/pallas_call | solution.py:1235
  237.2 1.7 convert_reduce_fusion
  238.9 1.8 slice.182.refs_1_
  240.8 4.6 fusion.63
  248.8 3.4 multiply_reduce_fusion.4
  254.8 220.6 %mixture_fb.1 = (f32[128,1536]{1,0:T(8,128)}, f32[128,1536]{1,0:T(8,128)}, f32[16,8,128]{2,1,0:T(8,128)}, f32[1536,1024]{1,0:T(8,128)}, f32[512,1536]{1,0:T(8,128)}) custom-call(bf16[16,8,128]{2,1,0:T(8,128)(2,1)} %pad.40.refs_0_, bf16[1536,128]{1,0:T(8,128)(2,1)} %slice.182.refs_1_, bf16[1536,1024]{1,0:T(8,128)(2,1)} %bitcast.308, ...), custom_call_target="tpu_custom_call" | custom-call | flops 28991029248 | bytes 12582912 | tf_op jit(solution)/shard_map/mixture_fb/pallas_call | solution.py:1235
  477.5 1.3 convolution_convert_fusion.3
  478.8 2.0 multiply_reduce_fusion.2
  482.6 4.0 convolution_convert_fusion.1
  486.8 2.4 fusion.14
  490.7 1.4 fusion.3
  494.6 5.8 fusion.82
  503.9 1.8 fusion.37.refs_7_
  506.7 162.1 %mixture_b.1 = (f32[128,1536]{1,0:T(8,128)}, f32[16,8,128]{2,1,0:T(8,128)}, f32[1536,1024]{1,0:T(8,128)}, f32[512,1536]{1,0:T(8,128)}, f32[96,2176]{1,0:T(8,128)}) custom-call(bf16[16,8,128]{2,1,0:T(8,128)(2,1)} %pad.39.refs_0_, bf16[1536,128]{1,0:T(8,128)(2,1)} %slice.172.refs_1_, bf16[1536,1024]{1,0:T(8,128)(2,1)} %bitcast.309, ...), custom_call_target="tpu_custom_call" | custom-call | flops 28991029248 | bytes 12582912 | tf_op jit(solution)/shard_map/mixture_b/pallas_call | solution.py:1235
  671.1 1.9 convolution_convert_fusion.2
  673.0 2.6 multiply_reduce_fusion
  676.6 4.0 convolution_convert_fusion
  680.9 2.4 fusion.15
  684.7 1.4 fusion
  690.0 6.2 fusion.24
  700.8 82.4 %closing.1 = (f32[96,2560]{1,0:T(8,128)}, f32[96,1536]{1,0:T(8,128)}, f32[96,256]{1,0:T(8,128)}, f32[1536,1024]{1,0:T(8,128)}, f32[512,1536]{1,0:T(8,128)}, /*index=5*/bf16[2,128,1536]{2,1,0:T(8,128)(2,1)}) custom-call(bf16[1536,128]{1,0:T(8,128)(2,1)} %copy.154.refs_0_, bf16[1536,128]{1,0:T(8,128)(2,1)} %bitcast.270, ...), custom_call_target="tpu_custom_call" | custom-call | bytes 100000000 | tf_op jit(solution)/shard_map/closing/pallas_call | solution.py:922
  783.2 1.6 slice_reduce_fusion
  786.3 2.1 copy.181
  790.2 6.8 copy.184
  797.0 1.7 copy.185
  (270 shorter events, 46.4 us)
Async XLA Ops:
  0.6 4.6 copy-start.72
  0.6 5.1 copy-start.15
  0.7 6.0 copy-start.22
  4.6 2.9 collective-permute-start
  4.6 80.5 %collective-permute-start.2 = (bf16[512,1536]{1,0:T(8,128)(2,1)}, bf16[512,1536]{1,0:T(8,128)(2,1)}, u32[]{:S(2)}, u32[]{:S(2)}) collective-permute-start(bf16[512,1536]{1,0:T(8,128)(2,1)} %bitcast.310), channel_id=1, source_target_pairs={{0,16},{16,0},{1,17},{17,1},{2,18},{18,2},{3,19},{19,3},{4,20},{20... | collective-permute-start | bytes 4718600 | tf_op jit(solution)/shard_map/ppermute | solution.py:1247
  5.1 80.0 %collective-permute-start.1 = (bf16[1536,1024]{1,0:T(8,128)(2,1)}, bf16[1536,1024]{1,0:T(8,128)(2,1)}, u32[]{:S(2)}, u32[]{:S(2)}) collective-permute-start(bf16[1536,1024]{1,0:T(8,128)(2,1)} %bitcast.306), channel_id=1, source_target_pairs={{0,16},{16,0},{1,17},{17,1},{2,18},{18,2},{3,19},{19,3},{4,20},{20... | collective-permute-start | bytes 9437192 | tf_op jit(solution)/shard_map/ppermute | solution.py:1247
  5.6 68.0 %copy-start.62 = (pred[128,128]{0,1:T(8,128)(4,1)}, pred[128,128]{0,1:T(8,128)(4,1)S(1)}, u32[]{:S(2)}) copy-start(pred[128,128]{0,1:T(8,128)(4,1)S(1)} %fusion.65) | copy-start | bytes 49156
  6.6 66.8 %copy-start.43 = (f32[128,32]{0,1:T(8,128)}, f32[128,32]{0,1:T(8,128)S(1)}, u32[]{:S(2)}) copy-start(f32[128,32]{0,1:T(8,128)S(1)} %get-tuple-element.137) | copy-start | bytes 49156
  6.7 61.7 %copy-start.70 = (f32[128]{0:T(128)}, f32[128]{0:T(128)S(1)}, u32[]{:S(2)}) copy-start(f32[128]{0:T(128)S(1)} %add_rsqrt_fusion.3) | copy-start | bytes 1540
  68.4 4.5 copy-start.55
  79.2 3.4 copy-start.20
  79.2 4.3 copy-start.58
  236.3 4.4 copy-start.1
  236.3 4.4 copy-start.24
  238.9 262.8 %copy-start.46 = (f32[1536]{0:T(1024)}, f32[1536]{0:T(1024)S(1)}, u32[]{:S(2)}) copy-start(f32[1536]{0:T(1024)S(1)} %get-tuple-element.97) | copy-start | bytes 18436
  240.8 8.0 copy-start.3
  240.8 4.7 copy-start.64
  248.8 3.4 copy-start.45
  248.8 5.2 copy-start.8
  477.4 3.3 copy-start.23
  506.7 163.0 %copy-start.60 = (f32[128,16]{0,1:T(8,128)S(1)}, f32[128,16]{0,1:T(8,128)}, u32[]{:S(2)}) copy-start(f32[128,16]{0,1:T(8,128)} %get-tuple-element.149) | copy-start | bytes 24580
  506.7 166.3 %copy-start.59 = (f32[1536]{0:T(1024)S(1)}, f32[1536]{0:T(1024)}, u32[]{:S(2)}) copy-start(f32[1536]{0:T(1024)} %get-tuple-element.98) | copy-start | bytes 18436
  671.1 4.5 copy-start.2
  671.1 4.5 copy-start.13
  671.1 4.5 copy-start.18
  671.1 4.5 copy-start.67
  690.0 6.2 copy-start.39
  690.0 6.2 copy-start.40
  690.0 7.1 copy-start.61
  690.0 7.1 copy-start.57
  783.2 5.2 copy-start.21
  790.2 6.8 copy-start.12
  (47 other events, 74.8 us)
